TPU v7x, 128 devices: a whole 4x4x4 slice. The times are simulated.
128 devices in a mesh: row: 2 (over z_lo), col: 64 (over y, x, z_hi, core).
Axes of the slice: x: 4, y: 4, z: 4 (z_hi: 2, z_lo: 2; z = z_hi * 2 + z_lo), core: 2. Of those that a mesh axis runs over, the one named last changes fastest.
Arguments:
- tokens: bfloat16 [512, 4608], P('col', 'row'), may hold values from -6 to 6
- pre_gain: float32 [2, 4608], P(None, 'row'), may hold values from -0.6 to 0.6
- post_gain: float32 [2, 4608], P(None, 'row'), may hold values from -0.6 to 0.6
- gate_weight: bfloat16 [2, 4608, 36864], P(None, ('row', 'col')), may hold values from -0.09375 to 0.09375
- up_weight: bfloat16 [2, 4608, 36864], P(None, ('row', 'col')), may hold values from -0.09375 to 0.09375
- down_weight: bfloat16 [2, 36864, 4608], P(None, ('row', 'col')), may hold values from -0.13541667 to 0.13541667
Outputs:
- stream: bfloat16 [512, 4608], P('col', 'row')
All inputs are finite; a program needn't handle non-finite values.
Results may differ from a plain program's by a relative error of at most 0.019.
Values may be sent and summed in bfloat16 or wider, within the bound.
No kernel may reach another device: no remote copies, remote signals or barrier semaphores. Data moves between devices by JAX's collectives and lax.ppermute only.
A program may use at most 128 MiB of HBM per device.

v0:
```python
import jax
import jax.numpy as jnp
from jax import lax
from jax.sharding import Mesh
from jax.sharding import PartitionSpec as P

COL = ("col_0", "col_1", "col_2", "col_3")
ROW_COL = ("row", "col_0", "col_1", "col_2", "col_3")


norm_eps = 1e-06


def sent_to_all(value, axis):
    copies = jnp.broadcast_to(value, (lax.axis_size(axis), *value.shape))
    return lax.all_to_all(copies, axis, split_axis=0, concat_axis=0, tiled=True)


def over_copies(value, axis):
    everything = sent_to_all(value, axis)
    return jnp.sum(everything, axis=0)


def laid_out(blocks, dim):
    lengths = list(blocks.shape[1:])
    lengths[dim] *= blocks.shape[0]
    return jnp.moveaxis(blocks, 0, dim).reshape(lengths)


def whole_of(value, axes, dim):
    far, near = axes
    first = sent_to_all(value, far)
    blocks = jnp.swapaxes(sent_to_all(first, near), 0, 1)
    return laid_out(blocks.reshape(-1, *value.shape), dim)


def over_copies_2(value, axis):
    everything = sent_to_all(value, axis)
    return jnp.sum(everything.astype(jnp.float32), axis=0)


def split_up(value, dim, peers):
    before, after = (value.shape[:dim], value.shape[dim + 1 :])
    return jnp.moveaxis(value.reshape(*before, peers, -1, *after), dim, 0)


def summed_on_arrival(value, axis, dim):
    peers = lax.axis_size(axis)
    blocks = lax.all_to_all(split_up(value, dim, peers), axis, 0, 0, tiled=True)
    return jnp.sum(blocks.astype(jnp.float32), axis=0)


def sum_by_axis(value, axes, dim):
    far, near = axes
    blocks = split_up(value, dim, lax.axis_size(far))
    nearer = summed_on_arrival(blocks, near, dim + 1)
    arrived = lax.all_to_all(
        nearer.astype(jnp.bfloat16), far, split_axis=0, concat_axis=0, tiled=True
    )
    return arrived.astype(jnp.float32).sum(axis=0)


def activate(summed, columns):
    gate = summed[:, :columns]
    up_proj = summed[:, columns:]
    return (jax.nn.gelu(gate, approximate=True) * up_proj).astype(jnp.bfloat16)


def on_device(tokens, pre_gain, post_gain, gate_weight, up_weight, down_weight):
    layer_count = gate_weight.shape[0]
    row_count = lax.axis_size("row")
    col_count = lax.axis_size(COL)
    model_width = tokens.shape[1] * row_count
    stored_rows = gate_weight.shape[1]
    hidden_total = gate_weight.shape[2]
    block_width = hidden_total // (row_count * col_count)
    tile_rows = stored_rows * col_count
    tile_columns = hidden_total // col_count
    gate_split = gate_weight.reshape(layer_count, stored_rows, row_count, col_count, block_width)
    up_split = up_weight.reshape(layer_count, stored_rows, row_count, col_count, block_width)
    gate_tiles, up_tiles = (
        lax.all_to_all(gate_split, COL, split_axis=3, concat_axis=1, tiled=True),
        lax.all_to_all(up_split, COL, split_axis=3, concat_axis=1, tiled=True),
    )
    gate_tiles = gate_tiles.reshape(layer_count, tile_rows, tile_columns)
    up_tiles = up_tiles.reshape(layer_count, tile_rows, tile_columns)
    down_tiles = lax.all_to_all(down_weight, "row", split_axis=2, concat_axis=1, tiled=True)
    current = tokens
    for layer_index in range(layer_count):
        gate_up = jnp.concatenate((gate_tiles[layer_index], up_tiles[layer_index]), axis=1)
        down_tile = down_tiles[layer_index]
        columns = gate_up.shape[1] // 2
        values = current.astype(jnp.float32)
        squares = over_copies(jnp.sum(values * values, axis=1), "row")
        scale_pre = lax.rsqrt(squares / model_width + norm_eps)[:, None]
        normed = (values * scale_pre * (1.0 + pre_gain[layer_index])[None, :]).astype(jnp.bfloat16)
        partial_sums = jnp.dot(
            whole_of(normed, (("col_0", "col_1", "col_2"), "col_3"), 0),
            gate_up,
            preferred_element_type=jnp.float32,
        )
        summed = over_copies_2(partial_sums.astype(jnp.bfloat16), "row").astype(jnp.float32)
        hidden = activate(summed, columns)
        branch = sum_by_axis(
            jnp.dot(hidden, down_tile, preferred_element_type=jnp.float32).astype(jnp.bfloat16),
            (("col_0", "col_1", "col_2"), "col_3"),
            0,
        )
        branch_squares = over_copies(jnp.sum(branch * branch, axis=1), "row")
        scale_post = lax.rsqrt(branch_squares / model_width + norm_eps)[:, None]
        post = branch * scale_post * (1.0 + post_gain[layer_index])[None, :]
        current = (values + post).astype(jnp.bfloat16)
    return current


def solution(mesh):
    split = Mesh(
        mesh.devices.reshape(mesh.shape["row"], 4, 4, 2, 2),
        ("row", "col_0", "col_1", "col_2", "col_3"),
    )
    in_specs = (
        P(COL, "row"),
        P(None, "row"),
        P(None, "row"),
        P(None, ROW_COL, None),
        P(None, ROW_COL, None),
        P(None, ROW_COL, None),
    )
    out_specs = P(COL, "row")
    return jax.shard_map(
        on_device, mesh=split, in_specs=in_specs, out_specs=out_specs, check_vma=False
    )
```

profile of v0, /device:TPU:0, one launch (start us, length us, event | category | flops | bytes accessed | tf_op | source)
XLA Modules:
  0.0 577.0 jit_solution(1357578688195838266)
XLA Ops:
  0.0 0.9 fusion.42
  1.5 3.3 all-to-all-start
  4.8 1.4 add_reduce_fusion.1
  6.2 2.3 all-to-all-done
  8.5 0.8 fusion.44
  9.3 1.1 broadcast_in_dim.39
  10.5 10.6 %all-to-all-start.1 = ((bf16[32,8,2304]{2,1,0:T(8,128)(2,1)}), bf16[32,8,2304]{2,1,0:T(8,128)(2,1)S(1)}, u32[]{:S(2)}, u32[]{:S(2)}) async-start(bf16[32,8,2304]{2,1,0:T(8,128)(2,1)} %broadcast_in_dim.39), calls=%async_computation.1 | async-start | bytes 2359296 | tf_op jit(solution)/shard_map/all_to_all | solution.py:16
  21.1 14.4 %reshape.58 = bf16[2,36,2,64,288]{4,3,2,0,1:T(8,128)(2,1)} reshape(bf16[2,36,36864]{2,0,1:T(2,128)(2,1)} %param.9) | data formatting | bytes 10616832 | tf_op jit(solution)/shard_map/reshape | solution.py:79
  35.5 11.5 %copy.43 = bf16[2,36,2,64,288]{4,2,1,0,3:T(2,128)(2,1)} copy(bf16[2,36,2,64,288]{4,3,2,0,1:T(8,128)(2,1)} %reshape.58) | data formatting | bytes 10616832 | tf_op jit(solution)/shard_map/reshape | solution.py:79
  47.1 5.6 all_to_all.119
  52.7 10.6 %all-to-all-start.3 = ((bf16[2,36,2,64,288]{4,2,1,0,3:T(2,128)(2,1)}), bf16[2,36,2,64,288]{4,2,1,0,3:T(2,128)(2,1)}, u32[]{:S(2)}, u32[]{:S(2)}) async-start(bf16[2,36,2,64,288]{4,2,1,0,3:T(2,128)(2,1)} %copy.43), calls=%async_computation.3 | async-start | bytes 14155776 | tf_op jit(solution)/shard_map/all_to_all | solution.py:82
  63.4 14.4 %reshape.59 = bf16[2,36,2,64,288]{4,3,2,0,1:T(8,128)(2,1)} reshape(bf16[2,36,36864]{2,0,1:T(2,128)(2,1)} %param.10) | data formatting | bytes 10616832 | tf_op jit(solution)/shard_map/reshape | solution.py:80
  77.8 11.5 %copy.44 = bf16[2,36,2,64,288]{4,2,1,0,3:T(2,128)(2,1)} copy(bf16[2,36,2,64,288]{4,3,2,0,1:T(8,128)(2,1)} %reshape.59) | data formatting | bytes 10616832 | tf_op jit(solution)/shard_map/reshape | solution.py:80
  89.3 62.8 %all-to-all-done.3 = bf16[2,36,2,64,288]{4,2,1,0,3:T(2,128)(2,1)} async-done(((bf16[2,36,2,64,288]{4,2,1,0,3:T(2,128)(2,1)}), bf16[2,36,2,64,288]{4,2,1,0,3:T(2,128)(2,1)}, u32[]{:S(2)}, u32[]{:S(2)}) %all-to-all-start.3) | async-done | bytes 5308448 | tf_op jit(solution)/shard_map/all_to_all | solution.py:82
  152.1 16.1 %all-to-all-start.4 = ((bf16[2,36,2,64,288]{4,2,1,0,3:T(2,128)(2,1)}), bf16[2,36,2,64,288]{4,2,1,0,3:T(2,128)(2,1)}, u32[]{:S(2)}, u32[]{:S(2)}) async-start(bf16[2,36,2,64,288]{4,2,1,0,3:T(2,128)(2,1)} %copy.44), calls=%async_computation.4 | async-start | bytes 14155776 | tf_op jit(solution)/shard_map/all_to_all | solution.py:83
  168.1 18.0 %copy.45 = bf16[2,288,4608]{1,0,2:T(2,128)(2,1)} copy(bf16[2,288,4608]{2,1,0:T(8,128)(2,1)} %param.11) | data formatting | bytes 10616832 | tf_op args[5]
  186.1 1.6 copy.42
  187.7 69.1 %all-to-all-done.4 = bf16[2,36,2,64,288]{4,2,1,0,3:T(2,128)(2,1)} async-done(((bf16[2,36,2,64,288]{4,2,1,0,3:T(2,128)(2,1)}), bf16[2,36,2,64,288]{4,2,1,0,3:T(2,128)(2,1)}, u32[]{:S(2)}, u32[]{:S(2)}) %all-to-all-start.4) | async-done | bytes 5308448 | tf_op jit(solution)/shard_map/all_to_all | solution.py:83
  256.8 7.0 %all-to-all-start.6 = ((bf16[2,288,4608]{1,0,2:T(2,128)(2,1)}), bf16[2,288,4608]{1,0,2:T(2,128)(2,1)}, u32[]{:S(2)}, u32[]{:S(2)}) async-start(bf16[2,288,4608]{1,0,2:T(2,128)(2,1)} %copy.45), calls=%async_computation.6 | async-start | bytes 14155776 | tf_op jit(solution)/shard_map/all_to_all | solution.py:87
  263.9 9.8 %fusion.61 = (bf16[1,64,36,2,1,288]{5,3,2,0,1,4:T(2,128)(2,1)S(1)}, bf16[1,64,36,2,1,288]{5,3,2,0,1,4:T(2,128)(2,1)}) fusion(bf16[2,64,36,2,1,288]{5,3,2,0,1,4:T(2,128)(2,1)} %bitcast.4), kind=kLoop, calls=%fused_computation.80 | loop fusion | bytes 10616832 | tf_op jit(solution)/shard_map/slice | solution.py:90
  273.7 8.1 %squeeze.22 = bf16[2304,576]{1,0:T(8,128)(2,1)} reshape(bf16[1,64,36,2,1,288]{5,3,2,0,1,4:T(2,128)(2,1)} %get-tuple-element.12) | data formatting | bytes 5308416 | tf_op jit(solution)/shard_map/squeeze | solution.py:90
  281.8 10.8 %fusion.62 = (bf16[1,64,36,2,1,288]{5,3,2,0,1,4:T(2,128)(2,1)}, bf16[1,64,36,2,1,288]{5,3,2,0,1,4:T(2,128)(2,1)}) fusion(bf16[2,64,36,2,1,288]{5,3,2,0,1,4:T(2,128)(2,1)} %bitcast.6), kind=kLoop, calls=%fused_computation.81 | loop fusion | bytes 10616832 | tf_op jit(solution)/shard_map/slice | solution.py:90
  292.6 8.0 %squeeze.23 = bf16[2304,576]{1,0:T(8,128)(2,1)} reshape(bf16[1,64,36,2,1,288]{5,3,2,0,1,4:T(2,128)(2,1)} %get-tuple-element.14) | data formatting | bytes 5308416 | tf_op jit(solution)/shard_map/squeeze | solution.py:90
  300.6 7.7 %fusion.11 = bf16[512,1152]{1,0:T(8,128)(2,1)} fusion(bf16[512,2304]{1,0:T(8,128)(2,1)} %bitcast.49, bf16[2304,576]{1,0:T(8,128)(2,1)} %squeeze.23, bf16[2304,576]{1,0:T(8,128)(2,1)} %squeeze.22), kind=kOutput, calls=%fused_computation.13 | convolution fusion | flops 2729115648 | bytes 8847360 | tf_op jit(solution)/shard_map/dot_general | solution.py:97
  308.2 34.0 %all-to-all-done.6 = bf16[2,288,4608]{1,0,2:T(2,128)(2,1)} async-done(((bf16[2,288,4608]{1,0,2:T(2,128)(2,1)}), bf16[2,288,4608]{1,0,2:T(2,128)(2,1)}, u32[]{:S(2)}, u32[]{:S(2)}) %all-to-all-start.6) | async-done | bytes 5308448 | tf_op jit(solution)/shard_map/all_to_all | solution.py:87
  342.2 2.8 broadcast_in_dim.41
  345.0 4.9 all-to-all-start.5
  350.0 33.0 %copy.55 = bf16[2,288,2,2304]{3,2,1,0:T(2,128)(2,1)} copy(bf16[2,288,2,2304]{1,0,3,2:T(2,128)(2,1)} %bitcast.7) | data formatting | bytes 10616832 | tf_op jit(solution)/shard_map/all_to_all | solution.py:87
  383.0 7.0 %fusion.63 = (bf16[1,2,288,2304]{3,1,2,0:T(2,128)(2,1)}, bf16[1,2,288,2304]{3,1,2,0:T(2,128)(2,1)S(1)}) fusion(bf16[2,2,288,2304]{3,1,2,0:T(2,128)(2,1)} %bitcast.44), kind=kLoop, calls=%fused_computation.82 | loop fusion | bytes 10616832 | tf_op jit(solution)/shard_map/slice | solution.py:91
  390.1 1.8 copy.47
  391.9 2.5 convert_reduce_fusion.1
  394.4 2.3 convolution_convert_fusion.1
  396.9 6.5 %all_to_all.120 = bf16[2,32,8,2304]{3,2,1,0:T(8,128)(2,1)} all-to-all(bf16[2,32,8,2304]{3,2,1,0:T(8,128)(2,1)S(1)} %bitcast.45), channel_id=1, replica_groups=mesh['row'=2,'col_0'=4,'col_1'=4,'col_2'=2,'col_3'=2] {'col_3'}, dimensions={0} | all-to-all | bytes 4718592 | tf_op jit(solution)/shard_map/all_to_all | solution.py:49
  403.4 3.4 reduce_sum.135
  406.8 15.8 %all-to-all-start.8 = ((bf16[32,8,2304]{2,1,0:T(8,128)(2,1)}), bf16[32,8,2304]{2,1,0:T(8,128)(2,1)}, u32[]{:S(2)}, u32[]{:S(2)}) async-start(bf16[32,8,2304]{2,1,0:T(8,128)(2,1)} %reduce_sum.135), calls=%async_computation.8 | async-start | bytes 2359296 | tf_op jit(solution)/shard_map/all_to_all | solution.py:57
  422.7 1.5 add_reduce_fusion
  424.1 19.6 %all-to-all-done.8 = bf16[32,8,2304]{2,1,0:T(8,128)(2,1)} async-done(((bf16[32,8,2304]{2,1,0:T(8,128)(2,1)}), bf16[32,8,2304]{2,1,0:T(8,128)(2,1)}, u32[]{:S(2)}, u32[]{:S(2)}) %all-to-all-start.8) | async-done | bytes 1179680 | tf_op jit(solution)/shard_map/all_to_all | solution.py:57
  443.7 1.4 convert_reduce_fusion.3
  445.1 0.6 copy-done.4
  445.9 6.2 %all_to_all.121 = f32[2,1,8]{2,1,0:T(1,128)S(1)} all-to-all(f32[2,1,8]{2,1,0:T(1,128)S(1)} %broadcast_in_dim.42), channel_id=1, replica_groups=mesh['row'=2,'col_0'=4,'col_1'=4,'col_2'=2,'col_3'=2] {'row'}, dimensions={0} | all-to-all | bytes 128 | tf_op jit(solution)/shard_map/all_to_all | solution.py:16
  452.6 0.7 add_rsqrt_fusion.2
  453.3 1.7 fusion.46
  455.0 6.1 %all_to_all.122 = f32[2,1,8]{2,1,0:T(1,128)S(1)} all-to-all(f32[2,1,8]{2,1,0:T(1,128)S(1)} %broadcast_in_dim.43), channel_id=1, replica_groups=mesh['row'=2,'col_0'=4,'col_1'=4,'col_2'=2,'col_3'=2] {'row'}, dimensions={0} | all-to-all | bytes 128 | tf_op jit(solution)/shard_map/all_to_all | solution.py:16
  461.7 0.7 add_rsqrt_fusion.1
  462.4 0.9 fusion.48
  463.3 1.1 broadcast_in_dim.44
  464.3 4.7 all-to-all-start.11
  469.0 4.0 squeeze.25
  473.0 6.9 %squeeze.26 = bf16[2304,576]{1,0:T(8,128)(2,1)S(1)} reshape(bf16[1,64,36,2,1,288]{5,3,2,0,1,4:T(2,128)(2,1)} %get-tuple-element.13) | data formatting | bytes 5308416 | tf_op jit(solution)/shard_map/squeeze | solution.py:90
  480.0 6.5 %all-to-all-done.11 = bf16[32,8,2304]{2,1,0:T(8,128)(2,1)} async-done(((bf16[32,8,2304]{2,1,0:T(8,128)(2,1)}), bf16[32,8,2304]{2,1,0:T(8,128)(2,1)}, u32[]{:S(2)}, u32[]{:S(2)}) %all-to-all-start.11) | async-done | bytes 1179680 | tf_op jit(solution)/shard_map/all_to_all | solution.py:16
  486.5 1.4 broadcast_in_dim.45
  487.9 5.6 all_to_all.123
  493.7 1.7 copy-done.1
  495.4 3.2 fusion.8
  498.6 1.6 broadcast_in_dim.46
  500.3 5.4 all-to-all-start.13
  505.7 1.8 copy.52
  507.5 26.5 %all-to-all-done.13 = bf16[2,512,1152]{2,1,0:T(8,128)(2,1)} async-done(((bf16[2,512,1152]{2,1,0:T(8,128)(2,1)}), bf16[2,512,1152]{2,1,0:T(8,128)(2,1)}, u32[]{:S(2)}, u32[]{:S(2)}) %all-to-all-start.13) | async-done | bytes 2359328 | tf_op jit(solution)/shard_map/all_to_all | solution.py:16
  534.0 2.4 convert_reduce_fusion
  536.4 2.3 convolution_convert_fusion
  538.9 5.6 all_to_all.124
  545.1 24.5 %all_to_all.125 = bf16[32,8,2304]{2,1,0:T(8,128)(2,1)S(1)} all-to-all(bf16[32,8,2304]{2,1,0:T(8,128)(2,1)S(1)} %reduce_sum.142), channel_id=1, replica_groups=mesh['row'=2,'col_0'=4,'col_1'=4,'col_2'=2,'col_3'=2] {'col_0','col_1','..., dimensions={0} | all-to-all | bytes 2359296 | tf_op jit(solution)/shard_map/all_to_all | solution.py:57
  569.9 6.1 %all_to_all.126 = f32[2,1,8]{2,1,0:T(1,128)S(1)} all-to-all(f32[2,1,8]{2,1,0:T(1,128)S(1)} %broadcast_in_dim.47), channel_id=1, replica_groups=mesh['row'=2,'col_0'=4,'col_1'=4,'col_2'=2,'col_3'=2] {'row'}, dimensions={0} | all-to-all | bytes 128 | tf_op jit(solution)/shard_map/all_to_all | solution.py:16
  576.0 0.7 fusion.49
  (30 shorter events, 3.5 us)
Async XLA Ops:
  1.5 7.0 %all-to-all-start = ((f32[2,1,8]{2,1,0:T(1,128)}), f32[2,1,8]{2,1,0:T(1,128)S(1)}, u32[]{:S(2)}, u32[]{:S(2)}) async-start(f32[2,1,8]{2,1,0:T(1,128)} %broadcast_in_dim.38), calls=%async_computation | async-start | bytes 2048 | tf_op jit(solution)/shard_map/all_to_all | solution.py:16
  10.5 36.5 %all-to-all-start.1 = ((bf16[32,8,2304]{2,1,0:T(8,128)(2,1)}), bf16[32,8,2304]{2,1,0:T(8,128)(2,1)S(1)}, u32[]{:S(2)}, u32[]{:S(2)}) async-start(bf16[32,8,2304]{2,1,0:T(8,128)(2,1)} %broadcast_in_dim.39), calls=%async_computation.1 | async-start | bytes 2359296 | tf_op jit(solution)/shard_map/all_to_all | solution.py:16
  52.7 99.3 %all-to-all-start.3 = ((bf16[2,36,2,64,288]{4,2,1,0,3:T(2,128)(2,1)}), bf16[2,36,2,64,288]{4,2,1,0,3:T(2,128)(2,1)}, u32[]{:S(2)}, u32[]{:S(2)}) async-start(bf16[2,36,2,64,288]{4,2,1,0,3:T(2,128)(2,1)} %copy.43), calls=%async_computation.3 | async-start | bytes 14155776 | tf_op jit(solution)/shard_map/all_to_all | solution.py:82
  152.1 104.7 %all-to-all-start.4 = ((bf16[2,36,2,64,288]{4,2,1,0,3:T(2,128)(2,1)}), bf16[2,36,2,64,288]{4,2,1,0,3:T(2,128)(2,1)}, u32[]{:S(2)}, u32[]{:S(2)}) async-start(bf16[2,36,2,64,288]{4,2,1,0,3:T(2,128)(2,1)} %copy.44), calls=%async_computation.4 | async-start | bytes 14155776 | tf_op jit(solution)/shard_map/all_to_all | solution.py:83
  256.8 85.4 %all-to-all-start.6 = ((bf16[2,288,4608]{1,0,2:T(2,128)(2,1)}), bf16[2,288,4608]{1,0,2:T(2,128)(2,1)}, u32[]{:S(2)}, u32[]{:S(2)}) async-start(bf16[2,288,4608]{1,0,2:T(2,128)(2,1)} %copy.45), calls=%async_computation.6 | async-start | bytes 14155776 | tf_op jit(solution)/shard_map/all_to_all | solution.py:87
  345.0 46.8 %all-to-all-start.5 = ((bf16[2,512,1152]{2,1,0:T(8,128)(2,1)}), bf16[2,512,1152]{2,1,0:T(8,128)(2,1)}, u32[]{:S(2)}, u32[]{:S(2)}) async-start(bf16[2,512,1152]{2,1,0:T(8,128)(2,1)} %broadcast_in_dim.41), calls=%async_computation.5 | async-start | bytes 4718592 | tf_op jit(solution)/shard_map/all_to_all | solution.py:16
  391.9 2.5 copy-start.2
  406.8 36.9 %all-to-all-start.8 = ((bf16[32,8,2304]{2,1,0:T(8,128)(2,1)}), bf16[32,8,2304]{2,1,0:T(8,128)(2,1)}, u32[]{:S(2)}, u32[]{:S(2)}) async-start(bf16[32,8,2304]{2,1,0:T(8,128)(2,1)} %reduce_sum.135), calls=%async_computation.8 | async-start | bytes 2359296 | tf_op jit(solution)/shard_map/all_to_all | solution.py:57
  445.1 0.6 copy-start.4
  464.3 22.1 %all-to-all-start.11 = ((bf16[32,8,2304]{2,1,0:T(8,128)(2,1)}), bf16[32,8,2304]{2,1,0:T(8,128)(2,1)}, u32[]{:S(2)}, u32[]{:S(2)}) async-start(bf16[32,8,2304]{2,1,0:T(8,128)(2,1)} %broadcast_in_dim.44), calls=%async_computation.11 | async-start | bytes 2359296 | tf_op jit(solution)/shard_map/all_to_all | solution.py:16
  493.5 1.8 copy-start.1
  500.3 5.5 copy-start
  500.3 33.7 %all-to-all-start.13 = ((bf16[2,512,1152]{2,1,0:T(8,128)(2,1)}), bf16[2,512,1152]{2,1,0:T(8,128)(2,1)}, u32[]{:S(2)}, u32[]{:S(2)}) async-start(bf16[2,512,1152]{2,1,0:T(8,128)(2,1)} %broadcast_in_dim.46), calls=%async_computation.13 | async-start | bytes 4718592 | tf_op jit(solution)/shard_map/all_to_all | solution.py:16
  507.5 28.9 %copy-start.3 = (bf16[1,2,288,2304]{3,2,1,0:T(8,128)(2,1)S(1)}, bf16[1,2,288,2304]{3,2,1,0:T(8,128)(2,1)}, u32[]{:S(2)}) copy-start(bf16[1,2,288,2304]{3,2,1,0:T(8,128)(2,1)} %copy.52) | copy-start | bytes 7962628
  545.1 30.9 %copy-start.5 = (bf16[8,2304]{1,0:T(8,128)(2,1)S(1)}, bf16[8,2304]{1,0:T(8,128)(2,1)}, u32[]{:S(2)}) copy-start(bf16[8,2304]{1,0:T(8,128)(2,1)} %get-tuple-element.10) | copy-start | bytes 110596
where the time goes:
time: 587 us; the launch traced here: 577 us
  waiting for transfers between devices  221 us (38%)
  local copies, waits for them, and re-layouts  174 us (30%)
  starting transfers between devices  78.5 us (13%)
  blocking collectives  66.3 us (11%)
  other arithmetic  21.2 us (4%)
  matrix products  15.6 us (3%)
    all_to_all x1, waiting for transfers between devices, on_device(): lax.all_to_all(up_split, COL, split_axis=3, concat_axis=1, tiled=True)  69.1 us
    all_to_all x1, waiting for transfers between devices, on_device(): lax.all_to_all(gate_split, COL, split_axis=3, concat_axis=1, tiled=True)  62.8 us
    all_to_all x5, waiting for transfers between devices, sent_to_all(): return lax.all_to_all(copies, axis, split_axis=0, concat_axis=0, tiled=True)  35.2 us
    all_to_all x1, waiting for transfers between devices, on_device(): lax.all_to_all(down_weight, 'row', split_axis=2, concat_axis=1, tiled=True)  34 us
    all_to_all x1, local copies, waits for them, and re-layouts, on_device(): lax.all_to_all(down_weight, 'row', split_axis=2, concat_axis=1, tiled=True)  33 us
    all_to_all x5, blocking collectives, sent_to_all(): return lax.all_to_all(copies, axis, split_axis=0, concat_axis=0, tiled=True)  29.7 us
    all_to_all x5, starting transfers between devices, sent_to_all(): return lax.all_to_all(copies, axis, split_axis=0, concat_axis=0, tiled=True)  29 us
    reshape x2, local copies, waits for them, and re-layouts, on_device(): up_weight.reshape(layer_count, stored_rows, row_count, col_count, block_w...  25.9 us
  transfers between devices with their start and end apart: 9, of which 7 were waited for; matrix products, arithmetic and copies ran while one was open for 30% of the time, Pallas kernels for 0%

commit v1 on v0

v1 whole, which is shorter than its diff:
```python
import jax
import jax.numpy as jnp
from jax import lax
from jax.experimental import pallas as pl
from jax.experimental.pallas import tpu as pltpu
from jax.sharding import Mesh
from jax.sharding import PartitionSpec as P

COL = ("col_0", "col_1", "col_2", "core")
ROW_COL = ("row", *COL)
CHIP = ("row", "col_0", "col_1", "col_2")

norm_eps = 1e-06


def pack_kernel(gate_ref, up_ref, out_ref):
    layers, rows, width = gate_ref.shape
    whole = rows // 8 * 8
    rest = rows - whole
    half = width // 2
    aligned = half // 128 * 128
    odd = half - aligned
    for side in range(2):
        first = 0 if side == 0 else width - aligned
        extra = aligned if side == 0 else half
        for layer in range(layers):
            places = (
                (slice(0, whole), slice(layer * whole, (layer + 1) * whole)),
                (
                    slice(whole, rows),
                    slice(layers * whole + layer * rest, layers * whole + (layer + 1) * rest),
                ),
            )
            for taken, put in places:
                out_ref[side, put, 0:aligned] = gate_ref[layer, taken, first : first + aligned]
                out_ref[side, put, aligned : 2 * aligned] = up_ref[
                    layer, taken, first : first + aligned
                ]
                out_ref[side, put, 2 * aligned : 2 * aligned + odd] = gate_ref[
                    layer, taken, extra : extra + odd
                ]
                out_ref[side, put, 2 * aligned + odd : width] = up_ref[
                    layer, taken, extra : extra + odd
                ]


def packed(gate_weight, up_weight, chips):
    layers, rows, hidden = gate_weight.shape
    width = hidden // chips * 2
    taken = pl.BlockSpec((layers, rows, width), lambda i: (0, 0, i))
    return pl.pallas_call(
        pack_kernel,
        grid=(chips // 2,),
        in_specs=[taken, taken],
        out_specs=pl.BlockSpec((2, layers * rows, width), lambda i: (i, 0, 0)),
        out_shape=jax.ShapeDtypeStruct((chips, layers * rows, width), gate_weight.dtype),
        name="pack",
    )(gate_weight, up_weight)


def gate_up_kernel(main_ref, rest_ref, weight_ref, weight_rest_ref, out_ref, total_ref):
    step = pl.program_id(0)
    width = weight_ref.shape[2]
    part = jnp.dot(
        main_ref[...], weight_ref[...].reshape(-1, width), preferred_element_type=jnp.float32
    )
    part += jnp.dot(
        rest_ref[...], weight_rest_ref[...].reshape(-1, width), preferred_element_type=jnp.float32
    )

    @pl.when(step == 0)
    def _():
        total_ref[...] = part

    @pl.when(step > 0)
    def _():
        total_ref[...] += part

    @pl.when(step == pl.num_programs(0) - 1)
    def _():
        out_ref[...] = total_ref[...].astype(out_ref.dtype)


def gate_up(normed, tiles, layer, layers):
    tokens = normed.shape[0]
    chips, rows, width = tiles.shape
    whole = rows // layers // 8 * 8
    rest = rows - layers * whole
    group = 128 // rest
    steps = chips // group
    return pl.pallas_call(
        gate_up_kernel,
        grid=(steps,),
        in_specs=[
            pl.BlockSpec((tokens, group * whole), lambda i: (0, i)),
            pl.BlockSpec((tokens, group * rest), lambda i: (0, chips * whole // 128 + i)),
            pl.BlockSpec((group, whole, width), lambda i: (i, layer, 0)),
            pl.BlockSpec((group, rest, width), lambda i: (i, layers * whole // rest, 0)),
        ],
        out_specs=pl.BlockSpec((tokens, width), lambda i: (0, 0)),
        out_shape=jax.ShapeDtypeStruct((tokens, width), jnp.bfloat16),
        scratch_shapes=[pltpu.VMEM((tokens, width), jnp.float32)],
        name="gate_up",
    )(normed, normed, tiles, tiles)


def copies_of(value, axes):
    return jnp.broadcast_to(value, (lax.axis_size(axes), *value.shape))


def exchanged(blocks, axes):
    return lax.all_to_all(blocks, axes, split_axis=0, concat_axis=0, tiled=True)


def slabs(normed, layer, layers, chips, cores):
    count, model_width = normed.shape
    rows = model_width // (chips * cores)
    whole = rows // 8 * 8
    rest = rows - whole
    cut = normed.reshape(count, chips, cores, rows).transpose(2, 0, 1, 3)
    main = cut[..., :whole].reshape(cores, count, chips * whole)
    tail = jnp.pad(
        cut[..., whole:], ((0, 0), (0, 0), (0, 0), (layer * rest, (layers - 1 - layer) * rest))
    ).reshape(cores, count, chips * rest * layers)
    return jnp.concatenate((main, tail), axis=2)


def on_device(tokens, pre_gain, post_gain, gate_weight, up_weight, down_weight):
    layers = gate_weight.shape[0]
    chips = lax.axis_size(CHIP)
    cores = lax.axis_size("core")
    model_width = tokens.shape[1] * lax.axis_size("row")
    core = lax.axis_index("core")
    side = lax.axis_index("col_2")

    current = lax.all_to_all(tokens, "row", split_axis=0, concat_axis=1, tiled=True)
    gains = exchanged(copies_of(jnp.concatenate((pre_gain, post_gain), axis=0), "row"), "row")
    gains = 1.0 + jnp.concatenate((gains[0], gains[1]), axis=1)
    count = current.shape[0]

    tiles = exchanged(packed(gate_weight, up_weight, chips), CHIP)
    other_down = lax.ppermute(down_weight, "core", [(0, 1), (1, 0)])

    for layer in range(layers):
        values = current.astype(jnp.float32)
        scale_pre = lax.rsqrt(jnp.mean(values * values, axis=1, keepdims=True) + norm_eps)
        normed = (values * scale_pre * gains[layer][None, :]).astype(jnp.bfloat16)
        cut = exchanged(slabs(normed, layer, layers, chips, cores), "core")
        cut = cut.reshape(cores * count, -1)
        everything = exchanged(copies_of(cut, CHIP), CHIP).reshape(-1, cut.shape[1])
        partial = gate_up(everything, tiles, layer, layers)
        width = partial.shape[1]
        partial = partial.reshape(chips, cores, count, width).transpose(1, 0, 2, 3)
        both = exchanged(partial.reshape(cores, chips * count, width), "core")
        summed = both[0].astype(jnp.float32) + both[1].astype(jnp.float32)
        half = width // 2
        aligned = half // 128 * 128
        gate = jnp.concatenate(
            (summed[:, :aligned], summed[:, 2 * aligned : half + aligned]), axis=1
        )
        up_proj = jnp.concatenate(
            (summed[:, aligned : 2 * aligned], summed[:, half + aligned :]), axis=1
        )
        hidden = (jax.nn.gelu(gate, approximate=True) * up_proj).astype(jnp.bfloat16)
        turned = jnp.concatenate((hidden[:, aligned:], hidden[:, :aligned]), axis=1)
        hidden = jnp.where(side == 0, hidden, turned)
        stored = down_weight.shape[1]
        low, high = hidden[:, :stored], hidden[:, stored:]
        own = jnp.where(core == 0, low, high)
        other = jnp.where(core == 0, high, low)
        branch = jnp.dot(own, down_weight[layer], preferred_element_type=jnp.float32)
        branch += jnp.dot(other, other_down[layer], preferred_element_type=jnp.float32)
        arrived = exchanged(branch.astype(jnp.bfloat16).reshape(chips, count, -1), CHIP)
        branch = jnp.sum(arrived.astype(jnp.float32), axis=0)
        scale_post = lax.rsqrt(jnp.mean(branch * branch, axis=1, keepdims=True) + norm_eps)
        post = branch * scale_post * gains[layers + layer][None, :]
        current = (values + post).astype(jnp.bfloat16)
    return lax.all_to_all(current, "row", split_axis=1, concat_axis=0, tiled=True)


def solution(mesh):
    split = Mesh(
        mesh.devices.reshape(mesh.shape["row"], 4, 4, 2, 2),
        ROW_COL,
    )
    in_specs = (
        P(COL, "row"),
        P(None, "row"),
        P(None, "row"),
        P(None, ROW_COL, None),
        P(None, ROW_COL, None),
        P(None, ROW_COL, None),
    )
    out_specs = P(COL, "row")
    return jax.shard_map(
        on_device, mesh=split, in_specs=in_specs, out_specs=out_specs, check_vma=False
    )
```

time: 587 us -> 438 us (0.75); the launches traced: 577 us -> 436 us
  local copies, waits for them, and re-layouts: 174 us -> 37.5 us
  Pallas kernels: 0 us -> 38.1 us
  starting transfers between devices: 78.5 us -> 50.6 us
  other arithmetic: 21.2 us -> 5.09 us
  waiting for transfers between devices: 221 us -> 229 us
  matrix products: 15.6 us -> 9.23 us
    reshape x4 -> x14, local copies, waits for them, and re-layouts: 51.7 us -> 12.1 us  [the longest x4 6.79 us: on_device(): partial = partial.reshape(chips, cores, count, width).transpose(1, 0, 2, 3)]
    pallas_call x0 -> x3, Pallas kernels: none -> 38.1 us  [the longest x1 21.5 us: packed(): pl.pallas_call(pack_kernel, grid=(chips // 2,), in_specs=[taken, taken],...]
    all_to_all x3 -> x2, local copies, waits for them, and re-layouts: 34.8 us -> 2.03 us  [the longest x1 1.4 us: on_device(): lax.all_to_all(tokens, 'row', split_axis=0, concat_axis=1, tiled=True)]
    slice x5 -> x13, local copies, waits for them, and re-layouts: 31.2 us -> 1.14 us  [the longest x2 0.42 us: slabs(): cut[..., whole:]]
    all_to_all x9 -> x6, starting transfers between devices: 78.5 us -> 50.4 us  [the longest x5 47.1 us: exchanged(): return lax.all_to_all(blocks, axes, split_axis=0, concat_axis=0, tiled=True)]
    squeeze x4 -> x1, local copies, waits for them, and re-layouts: 27.1 us -> 0.01 us  [on_device(): gains = 1.0 + jnp.concatenate((gains[0], gains[1]), axis=1)]
    reduce_sum x14 -> x6, other arithmetic: 14.6 us -> 2.59 us  [the longest x2 1.9 us: on_device(): branch = jnp.sum(arrived.astype(jnp.float32), axis=0)]
    all_to_all x9 -> x6, waiting for transfers between devices: 221 us -> 229 us  [the longest x5 226 us: exchanged(): return lax.all_to_all(blocks, axes, split_axis=0, concat_axis=0, tiled=True)]
  transfers between devices with their start and end apart: 9 -> 7, of which waited for: 7 -> 5; matrix products, arithmetic and copies ran while one was open for 30% -> 5% of each run, Pallas kernels for 0% -> 7%
where the time goes in v1:
time: 438 us; the launch traced here: 436 us
  waiting for transfers between devices  229 us (52%)
  blocking collectives  66.1 us (15%)
  starting transfers between devices  50.6 us (12%)
  Pallas kernels  38.1 us (9%)
  local copies, waits for them, and re-layouts  37.5 us (9%)
  matrix products  9.23 us (2%)
  other arithmetic  5.09 us (1%)
    all_to_all x5, waiting for transfers between devices, exchanged(): return lax.all_to_all(blocks, axes, split_axis=0, concat_axis=0, tiled=True)  226 us
    all_to_all x5, blocking collectives, exchanged(): return lax.all_to_all(blocks, axes, split_axis=0, concat_axis=0, tiled=True)  59.8 us
    all_to_all x5, starting transfers between devices, exchanged(): return lax.all_to_all(blocks, axes, split_axis=0, concat_axis=0, tiled=True)  47.1 us
    pallas_call x1, Pallas kernels, packed(): pl.pallas_call(pack_kernel, grid=(chips // 2,), in_specs=[taken, taken],...  21.5 us
    unnamed x14, local copies, waits for them, and re-layouts  18.2 us
    pallas_call x2, Pallas kernels, gate_up(): pl.pallas_call(gate_up_kernel, grid=(steps,), in_specs=[pl.BlockSpec((tok...  16.6 us
  transfers between devices with their start and end apart: 7, of which 5 were waited for; matrix products, arithmetic and copies ran while one was open for 5% of the time, Pallas kernels for 7%

profile of v1, /device:TPU:0, one launch (start us, length us, event | category | flops | bytes accessed | tf_op | source)
XLA Modules:
  0.0 436.3 jit_solution(1926198746723958620)
XLA Ops:
  0.0 1.4 all_to_all.52
  1.4 3.3 all-to-all-start
  4.7 0.8 pad_maximum_fusion.2
  5.5 3.2 all-to-all-done
  8.7 0.6 broadcast_in_dim.6
  9.3 3.3 all-to-all-start.1
  12.6 0.2 multiply_reduce_fusion.2
  12.8 0.4 reshape.170
  13.3 3.5 all-to-all-done.1
  16.8 0.2 slice_reduce_fusion
  17.1 0.2 fusion.43
  17.3 0.2 slice.140
  17.6 0.2 reshape.157
  17.8 0.2 reshape.156
  18.0 3.8 all_to_all.79
  21.8 1.7 broadcast_in_dim.14
  23.5 11.3 %all-to-all-start.3 = ((bf16[64,8,2560]{2,1,0:T(8,128)(2,1)}), bf16[64,8,2560]{2,1,0:T(8,128)(2,1)S(1)}, u32[]{:S(2)}, u32[]{:S(2)}) async-start(bf16[64,8,2560]{2,1,0:T(8,128)(2,1)} %broadcast_in_dim.14), calls=%async_computation.3 | async-start | bytes 5242880 | tf_op jit(solution)/shard_map/all_to_all | solution.py:112
  34.8 7.9 %copy.47.gate_ref = bf16[2,36,36864]{2,1,0:T(8,128)(2,1)} copy(bf16[2,36,36864]{2,0,1:T(2,128)(2,1)} %param.9) | data formatting | bytes 10616832 | tf_op args[3]
  42.7 8.0 %copy.48.up_ref = bf16[2,36,36864]{2,1,0:T(8,128)(2,1)} copy(bf16[2,36,36864]{2,0,1:T(2,128)(2,1)} %param.10) | data formatting | bytes 10616832 | tf_op args[4]
  50.7 21.5 %pack.1 = bf16[64,72,1152]{2,1,0:T(8,128)(2,1)} custom-call(bf16[2,36,36864]{2,1,0:T(8,128)(2,1)} %copy.47.gate_ref, bf16[2,36,36864]{2,1,0:T(8,128)(2,1)} %copy.48.up_ref), custom_call_target="tpu_custom_call" | custom-call | tf_op jit(solution)/shard_map/pack/pallas_call | solution.py:51
  72.2 1.5 copy-done
  73.7 10.4 %all-to-all-start.4 = ((bf16[64,72,1152]{2,1,0:T(8,128)(2,1)}), bf16[64,72,1152]{2,1,0:T(8,128)(2,1)}, u32[]{:S(2)}, u32[]{:S(2)}) async-start(bf16[64,72,1152]{2,1,0:T(8,128)(2,1)} %pack.1), calls=%async_computation.4 | async-start | bytes 21233664 | tf_op jit(solution)/shard_map/all_to_all | solution.py:112
  84.1 0.3 collective-permute-start
  84.4 159.4 %all-to-all-done.4.weight_ref.weight_rest_ref = bf16[64,72,1152]{2,1,0:T(8,128)(2,1)} async-done(((bf16[64,72,1152]{2,1,0:T(8,128)(2,1)}), bf16[64,72,1152]{2,1,0:T(8,128)(2,1)}, u32[]{:S(2)}, u32[]{:S(2)}) %all-to-all-start.4) | async-done | bytes 10616864 | tf_op jit(solution)/shard_map/all_to_all | solution.py:112
  243.7 8.3 %gate_up.2 = bf16[512,1152]{1,0:T(8,128)(2,1)} custom-call(bf16[512,2560]{1,0:T(8,128)(2,1)} %bitcast.52, bf16[512,2560]{1,0:T(8,128)(2,1)} %bitcast.53, bf16[64,72,1152]{2,1,0:T(8,128)(2,1)} %all-to-all-done.4.weight_ref.weight_rest_ref, bf16[64,72,1152]{2,1,0:T(8,128)(2,1)} %all-to-all-done.4.weight_ref.weight_rest_ref), custom_call_target="tpu_custom_call" | custom-call | tf_op jit(solution)/shard_map/gate_up/pallas_call | solution.py:91
  252.0 2.5 reshape.160
  254.5 0.9 copy.49
  255.6 4.9 %all_to_all.80 = bf16[2,256,1152]{2,1,0:T(8,128)(2,1)S(1)} all-to-all(bf16[2,256,1152]{2,1,0:T(8,128)(2,1)S(1)} %copy.50), channel_id=1, replica_groups=mesh['row'=2,'col_0'=4,'col_1'=4,'col_2'=2,'core'=2] {'core'}, dimensions={0} | all-to-all | bytes 2359296 | tf_op jit(solution)/shard_map/all_to_all | solution.py:112
  260.9 0.2 fusion.16
  261.2 0.2 maximum_select_fusion
  261.4 0.4 slice-done.1
  261.8 1.4 fusion.4
  263.2 3.2 fusion
  266.4 2.2 reshape.162
  268.6 17.1 %all-to-all-start.6 = ((bf16[64,4,4608]{2,1,0:T(4,128)(2,1)}), bf16[64,4,4608]{2,1,0:T(4,128)(2,1)S(1)}, u32[]{:S(2)}, u32[]{:S(2)}) async-start(bf16[64,4,4608]{2,1,0:T(4,128)(2,1)} %reshape.162), calls=%async_computation.6 | async-start | bytes 4718592 | tf_op jit(solution)/shard_map/all_to_all | solution.py:112
  285.7 0.1 mul.157
  286.0 31.4 %all-to-all-done.6 = bf16[64,4,4608]{2,1,0:T(4,128)(2,1)S(1)} async-done(((bf16[64,4,4608]{2,1,0:T(4,128)(2,1)}), bf16[64,4,4608]{2,1,0:T(4,128)(2,1)S(1)}, u32[]{:S(2)}, u32[]{:S(2)}) %all-to-all-start.6) | async-done | bytes 2359328 | tf_op jit(solution)/shard_map/all_to_all | solution.py:112
  317.4 1.0 convert_reduce_fusion.1
  318.4 0.4 reduce_sum.64
  318.8 0.2 multiply_reduce_fusion.1
  319.0 0.2 fusion.44
  319.2 0.3 fusion.42
  319.5 0.2 slice.155
  319.8 0.2 reshape.164
  320.0 0.2 reshape.163
  320.3 3.8 all_to_all.81
  324.0 0.2 broadcast_in_dim.15
  324.2 42.4 %all_to_all.82 = bf16[64,8,2560]{2,1,0:T(8,128)(2,1)} all-to-all(bf16[64,8,2560]{2,1,0:T(8,128)(2,1)S(1)} %broadcast_in_dim.15), channel_id=1, replica_groups=mesh['row'=2,'col_0'=4,'col_1'=4,'col_2'=2,'core'=2] {'row','col_0','col..., dimensions={0} | all-to-all | bytes 5242880 | tf_op jit(solution)/shard_map/all_to_all | solution.py:112
  366.6 8.3 %gate_up.3 = bf16[512,1152]{1,0:T(8,128)(2,1)} custom-call(bf16[512,2560]{1,0:T(8,128)(2,1)} %bitcast.54, bf16[512,2560]{1,0:T(8,128)(2,1)} %bitcast.55, bf16[64,72,1152]{2,1,0:T(8,128)(2,1)} %all-to-all-done.4.weight_ref.weight_rest_ref, bf16[64,72,1152]{2,1,0:T(8,128)(2,1)} %all-to-all-done.4.weight_ref.weight_rest_ref), custom_call_target="tpu_custom_call" | custom-call | tf_op jit(solution)/shard_map/gate_up/pallas_call | solution.py:91
  374.9 2.5 reshape.167
  377.3 0.9 copy.53
  378.4 4.9 %all_to_all.83 = bf16[2,256,1152]{2,1,0:T(8,128)(2,1)S(1)} all-to-all(bf16[2,256,1152]{2,1,0:T(8,128)(2,1)S(1)} %copy.54), channel_id=1, replica_groups=mesh['row'=2,'col_0'=4,'col_1'=4,'col_2'=2,'core'=2] {'core'}, dimensions={0} | all-to-all | bytes 2359296 | tf_op jit(solution)/shard_map/all_to_all | solution.py:112
  383.7 0.2 fusion.25
  384.0 0.2 maximum_select_fusion.1
  384.2 0.4 slice-done.3
  384.6 1.4 fusion.2
  386.1 3.2 fusion.1
  389.2 2.1 reshape.169
  391.4 4.9 %all-to-all-start.10 = ((bf16[64,4,4608]{2,1,0:T(4,128)(2,1)}), bf16[64,4,4608]{2,1,0:T(4,128)(2,1)S(1)}, u32[]{:S(2)}, u32[]{:S(2)}) async-start(bf16[64,4,4608]{2,1,0:T(4,128)(2,1)} %reshape.169), calls=%async_computation.10 | async-start | bytes 4718592 | tf_op jit(solution)/shard_map/all_to_all | solution.py:112
  396.4 31.7 %all-to-all-done.10 = bf16[64,4,4608]{2,1,0:T(4,128)(2,1)S(1)} async-done(((bf16[64,4,4608]{2,1,0:T(4,128)(2,1)}), bf16[64,4,4608]{2,1,0:T(4,128)(2,1)S(1)}, u32[]{:S(2)}, u32[]{:S(2)}) %all-to-all-start.10) | async-done | bytes 2359328 | tf_op jit(solution)/shard_map/all_to_all | solution.py:112
  428.1 1.0 convert_reduce_fusion
  429.0 0.2 multiply_reduce_fusion
  429.3 6.3 %all_to_all.84 = bf16[4,2,2304]{2,0,1:T(4,128)(2,1)S(1)} all-to-all(bf16[4,2,2304]{2,0,1:T(4,128)(2,1)S(1)} %fusion.45), channel_id=1, replica_groups=mesh['row'=2,'col_0'=4,'col_1'=4,'col_2'=2,'core'=2] {'row'}, dimensions={1} | all-to-all | bytes 73728 | tf_op jit(solution)/shard_map/all_to_all | solution.py:178
  435.6 0.6 all_to_all.66
  (46 shorter events, 1.8 us)
Async XLA Ops:
  1.4 7.3 %all-to-all-start = ((bf16[2,4,2304]{2,1,0:T(4,128)(2,1)}), bf16[2,4,2304]{2,1,0:T(4,128)(2,1)S(1)}, u32[]{:S(2)}, u32[]{:S(2)}) async-start(bf16[2,4,2304]{2,1,0:T(4,128)(2,1)} %all_to_all.52), calls=%async_computation | async-start | bytes 73728 | tf_op jit(solution)/shard_map/all_to_all | solution.py:136
  9.3 7.5 %all-to-all-start.1 = ((f32[2,4,2304]{2,1,0:T(4,128)}), f32[2,4,2304]{2,1,0:T(4,128)S(1)}, u32[]{:S(2)}, u32[]{:S(2)}) async-start(f32[2,4,2304]{2,1,0:T(4,128)} %broadcast_in_dim.6), calls=%async_computation.1 | async-start | bytes 147456 | tf_op jit(solution)/shard_map/all_to_all | solution.py:112
  23.5 48.7 %all-to-all-start.3 = ((bf16[64,8,2560]{2,1,0:T(8,128)(2,1)}), bf16[64,8,2560]{2,1,0:T(8,128)(2,1)S(1)}, u32[]{:S(2)}, u32[]{:S(2)}) async-start(bf16[64,8,2560]{2,1,0:T(8,128)(2,1)} %broadcast_in_dim.14), calls=%async_computation.3 | async-start | bytes 5242880 | tf_op jit(solution)/shard_map/all_to_all | solution.py:112
  72.2 1.5 copy-start
  73.7 170.1 %all-to-all-start.4 = ((bf16[64,72,1152]{2,1,0:T(8,128)(2,1)}), bf16[64,72,1152]{2,1,0:T(8,128)(2,1)}, u32[]{:S(2)}, u32[]{:S(2)}) async-start(bf16[64,72,1152]{2,1,0:T(8,128)(2,1)} %pack.1), calls=%async_computation.4 | async-start | bytes 21233664 | tf_op jit(solution)/shard_map/all_to_all | solution.py:112
  84.1 179.1 %collective-permute-start = (bf16[2,288,4608]{2,1,0:T(8,128)(2,1)}, bf16[2,288,4608]{2,1,0:T(8,128)(2,1)}, u32[]{:S(2)}, u32[]{:S(2)}) collective-permute-start(bf16[2,288,4608]{2,1,0:T(8,128)(2,1)} %param.11), channel_id=1, source_target_pairs={{0,1},{1,0},{2,3},{3,2},{4,5},{5,4},{6,7},{7,6},{8,9},{9,8},{10,11... | collective-permute-start | bytes 15925256 | tf_op jit(solution)/shard_map/ppermute | solution.py:142
  255.4 5.9 %slice-start = ((s8[5308416]{0:T(1024)(128)(4,1)}), s8[4194304]{0:T(1024)(128)(4,1)S(1)}, s32[]{:S(2)}) async-start(s8[5308416]{0:T(1024)(128)(4,1)} %bitcast.56), calls=%async_computation.12 | async-start | bytes 8388608
  260.5 1.2 slice-start.1
  268.6 48.8 %all-to-all-start.6 = ((bf16[64,4,4608]{2,1,0:T(4,128)(2,1)}), bf16[64,4,4608]{2,1,0:T(4,128)(2,1)S(1)}, u32[]{:S(2)}, u32[]{:S(2)}) async-start(bf16[64,4,4608]{2,1,0:T(4,128)(2,1)} %reshape.162), calls=%async_computation.6 | async-start | bytes 4718592 | tf_op jit(solution)/shard_map/all_to_all | solution.py:112
  378.3 5.9 %slice-start.2 = ((s8[5308416]{0:T(1024)(128)(4,1)}), s8[4194304]{0:T(1024)(128)(4,1)S(1)}, s32[]{:S(2)}) async-start(s8[5308416]{0:T(1024)(128)(4,1)} %bitcast.58), calls=%async_computation.14 | async-start | bytes 8388608
  383.4 1.2 slice-start.3
  391.4 36.7 %all-to-all-start.10 = ((bf16[64,4,4608]{2,1,0:T(4,128)(2,1)}), bf16[64,4,4608]{2,1,0:T(4,128)(2,1)S(1)}, u32[]{:S(2)}, u32[]{:S(2)}) async-start(bf16[64,4,4608]{2,1,0:T(4,128)(2,1)} %reshape.169), calls=%async_computation.10 | async-start | bytes 4718592 | tf_op jit(solution)/shard_map/all_to_all | solution.py:112

commit v2 on v1

v2 whole, which is shorter than its diff:
```python
import functools

import jax
import jax.numpy as jnp
from jax import lax
from jax.experimental import pallas as pl
from jax.experimental.pallas import tpu as pltpu
from jax.sharding import Mesh
from jax.sharding import PartitionSpec as P

COL = ("col_0", "col_1", "col_2", "core")
ROW_COL = ("row", *COL)
CHIP = ("row", "col_0", "col_1", "col_2")

SWAP = [(0, 1), (1, 0)]

norm_eps = 1e-06


def pack_kernel(gate_ref, up_ref, first_ref, later_ref):
    rows, layers, lanes = gate_ref.shape
    pairs = first_ref.shape[0] // 2
    width = lanes // pairs
    whole = rows // 8 * 8
    rest = rows - whole
    half = width // 2
    aligned = half // 128 * 128
    odd = half - aligned
    for pair in range(pairs):
        for index, ref in enumerate((gate_ref, up_ref)):
            block = jnp.swapaxes(ref[:, :, pair * width : (pair + 1) * width], 0, 1)
            for side in range(2):
                first = 0 if side == 0 else width - aligned
                extra = aligned if side == 0 else half
                main = slice(index * aligned, (index + 1) * aligned)
                tail = slice(2 * aligned + index * odd, 2 * aligned + (index + 1) * odd)
                place = 2 * pair + side
                for layer in range(layers):
                    out_ref = first_ref if layer == 0 else later_ref
                    start = 0 if layer == 0 else (layer - 1) * whole
                    put = slice(start, start + whole)
                    out_ref[place, put, main] = block[layer, :whole, first : first + aligned]
                    out_ref[place, put, tail] = block[layer, :whole, extra : extra + odd]
                    put = slice(whole + layer * rest, whole + (layer + 1) * rest)
                    first_ref[place, put, main] = block[layer, whole:, first : first + aligned]
                    first_ref[place, put, tail] = block[layer, whole:, extra : extra + odd]


def packed(gate_weight, up_weight, chips):
    layers, rows, hidden = gate_weight.shape
    width = hidden // chips * 2
    whole = rows // 8 * 8
    pairs = 4
    taken = pl.BlockSpec((rows, layers, pairs * width), lambda i: (0, 0, i))
    lengths = (whole + layers * (rows - whole), (layers - 1) * whole)
    return pl.pallas_call(
        pack_kernel,
        grid=(chips // 2 // pairs,),
        in_specs=[taken, taken],
        out_specs=[pl.BlockSpec((2 * pairs, n, width), lambda i: (i, 0, 0)) for n in lengths],
        out_shape=[jax.ShapeDtypeStruct((chips, n, width), gate_weight.dtype) for n in lengths],
        compiler_params=pltpu.CompilerParams(vmem_limit_bytes=48 * 2**20),
        name="pack",
    )(jnp.swapaxes(gate_weight, 0, 1), jnp.swapaxes(up_weight, 0, 1))


def gate_up_kernel(
    layer, core_ref, normed_ref, weight_ref, rest_ref, own_ref, other_ref, spread_ref
):
    tokens = normed_ref.shape[0]
    chips, whole, width = weight_ref.shape
    rest = rest_ref.shape[1]
    own = own_ref.shape[0]
    cores = tokens // own
    count = own // chips
    narrow = normed_ref.shape[1] - chips * whole

    @pl.when(pl.program_id(0) == 0)
    def _():
        part = narrow // chips
        taken = lax.broadcasted_iota(jnp.int32, (narrow, chips * rest), 0)
        put = lax.broadcasted_iota(jnp.int32, (narrow, chips * rest), 1)
        place = taken // part * rest + layer * part + taken % part
        spread_ref[...] = jnp.dot(
            normed_ref[:, chips * whole :],
            (place == put).astype(jnp.float32).astype(jnp.bfloat16),
            preferred_element_type=jnp.float32,
        ).astype(jnp.bfloat16)

    part = jnp.dot(
        normed_ref[:, : chips * whole],
        weight_ref[...].reshape(chips * whole, width),
        preferred_element_type=jnp.float32,
    )
    part += jnp.dot(
        spread_ref[...],
        rest_ref[...].reshape(chips * rest, width),
        preferred_element_type=jnp.float32,
    )
    put = lax.broadcasted_iota(jnp.int32, (tokens, tokens), 0)
    taken = lax.broadcasted_iota(jnp.int32, (tokens, tokens), 1)
    owner = (put // own + core_ref[0]) % cores
    place = put % own // count * (cores * count) + owner * count + put % count
    ordered = jnp.dot(
        (place == taken).astype(jnp.float32).astype(jnp.bfloat16),
        part.astype(jnp.bfloat16),
        preferred_element_type=jnp.float32,
    ).astype(own_ref.dtype)
    own_ref[...] = ordered[:own]
    other_ref[...] = ordered[own:]


def gate_up(normed, weights, rests, layer, core, cores):
    tokens, depth = normed.shape
    chips, _, width = weights.shape
    layers = 2
    rows = depth // chips
    whole = rows // 8 * 8
    rest = layers * (rows - whole)
    step = 384
    own = tokens // cores
    return pl.pallas_call(
        functools.partial(gate_up_kernel, layer),
        grid=(width // step,),
        in_specs=[
            pl.BlockSpec(memory_space=pltpu.SMEM),
            pl.BlockSpec((tokens, depth), lambda i: (0, 0)),
            pl.BlockSpec((chips, whole, step), lambda i: (0, 0, i)),
            pl.BlockSpec((chips, rest, step), lambda i: (0, whole // rest, i)),
        ],
        out_specs=[pl.BlockSpec((own, step), lambda i: (0, i))] * 2,
        out_shape=[jax.ShapeDtypeStruct((own, width), jnp.bfloat16)] * 2,
        scratch_shapes=[pltpu.VMEM((tokens, chips * rest), jnp.bfloat16)],
        compiler_params=pltpu.CompilerParams(vmem_limit_bytes=40 * 2**20),
        name="gate_up",
    )(core.reshape(1), normed, weights, rests)


def copies_of(value, axes):
    return jnp.broadcast_to(value, (lax.axis_size(axes), *value.shape))


def exchanged(blocks, axes):
    return lax.all_to_all(blocks, axes, split_axis=0, concat_axis=0, tiled=True)


def slabs(normed, chips, cores):
    count, model_width = normed.shape
    rows = model_width // (chips * cores)
    whole = rows // 8 * 8
    cut = normed.reshape(count, chips, cores, rows).transpose(2, 0, 1, 3)
    main = cut[..., :whole].reshape(cores, count, chips * whole)
    tail = cut[..., whole:].reshape(cores, count, chips * (rows - whole))
    return jnp.concatenate((main, tail), axis=2)


def on_device(tokens, pre_gain, post_gain, gate_weight, up_weight, down_weight):
    layers = gate_weight.shape[0]
    chips = lax.axis_size(CHIP)
    cores = lax.axis_size("core")
    core = lax.axis_index("core")
    side = lax.axis_index("col_2")

    count = tokens.shape[0] // lax.axis_size("row")
    gains = copies_of(jnp.concatenate((pre_gain, post_gain), axis=0), "row")
    mixed = tokens.reshape(-1, count, tokens.shape[1]).astype(jnp.float32)
    mixed = exchanged(jnp.concatenate((mixed, gains), axis=1), "row")
    mixed = jnp.concatenate((mixed[0], mixed[1]), axis=1)
    current = mixed[:count].astype(jnp.bfloat16)
    gains = 1.0 + mixed[count:]

    other_down = lax.ppermute(down_weight, "core", SWAP)
    first, later = packed(gate_weight, up_weight, chips)
    first, other_down = lax.optimization_barrier((first, other_down))
    first = exchanged(first, CHIP)
    later = exchanged(later, CHIP)

    for layer in range(layers):
        values = current.astype(jnp.float32)
        scale_pre = lax.rsqrt(jnp.mean(values * values, axis=1, keepdims=True) + norm_eps)
        normed = (values * scale_pre * gains[layer][None, :]).astype(jnp.bfloat16)
        cut = exchanged(slabs(normed, chips, cores), "core")
        cut = cut.reshape(cores * count, -1)
        everything = exchanged(copies_of(cut, CHIP), CHIP).reshape(-1, cut.shape[1])
        weights = first if layer == 0 else later
        mine, theirs = gate_up(everything, weights, first, layer, core, cores)
        width = mine.shape[1]
        arrived = lax.ppermute(theirs, "core", SWAP)
        summed = mine.astype(jnp.float32) + arrived.astype(jnp.float32)
        half = width // 2
        aligned = half // 128 * 128
        gate = jnp.concatenate(
            (summed[:, :aligned], summed[:, 2 * aligned : half + aligned]), axis=1
        )
        up_proj = jnp.concatenate(
            (summed[:, aligned : 2 * aligned], summed[:, half + aligned :]), axis=1
        )
        hidden = (jax.nn.gelu(gate, approximate=True) * up_proj).astype(jnp.bfloat16)
        turned = jnp.concatenate((hidden[:, aligned:], hidden[:, :aligned]), axis=1)
        hidden = jnp.where(side == 0, hidden, turned)
        stored = down_weight.shape[1]
        low, high = hidden[:, :stored], hidden[:, stored:]
        own = jnp.where(core == 0, low, high)
        other = jnp.where(core == 0, high, low)
        branch = jnp.dot(own, down_weight[layer], preferred_element_type=jnp.float32)
        branch += jnp.dot(other, other_down[layer], preferred_element_type=jnp.float32)
        sent = branch.astype(jnp.bfloat16)
        if layer == 0:
            sent, later = lax.optimization_barrier((sent, later))
        arrived = exchanged(sent.reshape(chips, count, -1), CHIP)
        branch = jnp.sum(arrived.astype(jnp.float32), axis=0)
        scale_post = lax.rsqrt(jnp.mean(branch * branch, axis=1, keepdims=True) + norm_eps)
        post = branch * scale_post * gains[layers + layer][None, :]
        current = (values + post).astype(jnp.bfloat16)
    return lax.all_to_all(current, "row", split_axis=1, concat_axis=0, tiled=True)


def solution(mesh):
    split = Mesh(
        mesh.devices.reshape(mesh.shape["row"], 4, 4, 2, 2),
        ROW_COL,
    )
    in_specs = (
        P(COL, "row"),
        P(None, "row"),
        P(None, "row"),
        P(None, ROW_COL, None),
        P(None, ROW_COL, None),
        P(None, ROW_COL, None),
    )
    out_specs = P(COL, "row")

    return jax.shard_map(
        on_device, mesh=split, in_specs=in_specs, out_specs=out_specs, check_vma=False
    )
```

time: 438 us -> 355 us (0.81)
  waiting for transfers between devices: 229 us -> 60.3 us
  blocking collectives: 66.1 us -> 217 us
  starting transfers between devices: 50.6 us -> 17 us
  local copies, waits for them, and re-layouts: 37.5 us -> 18.1 us
  Pallas kernels: 38.1 us -> 24.4 us
    all_to_all x5 -> x2, waiting for transfers between devices: 226 us -> 56.3 us  [exchanged(): return lax.all_to_all(blocks, axes, split_axis=0, concat_axis=0, tiled=True)]
    all_to_all x5 -> x7, blocking collectives: 59.8 us -> 211 us  [exchanged(): return lax.all_to_all(blocks, axes, split_axis=0, concat_axis=0, tiled=True)]
    all_to_all x5 -> x2, starting transfers between devices: 47.1 us -> 16.8 us  [exchanged(): return lax.all_to_all(blocks, axes, split_axis=0, concat_axis=0, tiled=True)]
    pallas_call x3, Pallas kernels: 38.1 us -> 24.4 us  [the longest x2 14.4 us: gate_up(): pl.pallas_call(functools.partial(gate_up_kernel, layer), grid=(width // s...]
    unnamed x14 -> x20, local copies, waits for them, and re-layouts: 18.2 us -> 7.48 us
    reshape x10 -> x6, local copies, waits for them, and re-layouts: 11.7 us -> 5.36 us  [the longest x2 4.28 us: on_device(): arrived = exchanged(sent.reshape(chips, count, -1), CHIP)]
  transfers between devices with their start and end apart: 7 -> 5, of which waited for: 5 -> 4; matrix products, arithmetic and copies ran while one was open for 5% -> 3% of each run, Pallas kernels for 7% -> 5%
where the time goes in v2:
time: 355 us; the launch traced here: 353 us
  blocking collectives  217 us (61%)
  waiting for transfers between devices  60.3 us (17%)
  Pallas kernels  24.4 us (7%)
  local copies, waits for them, and re-layouts  18.1 us (5%)
  starting transfers between devices  17 us (5%)
  matrix products  11 us (3%)
  other arithmetic  4.79 us (1%)
    all_to_all x7, blocking collectives, exchanged(): return lax.all_to_all(blocks, axes, split_axis=0, concat_axis=0, tiled=True)  211 us
    all_to_all x2, waiting for transfers between devices, exchanged(): return lax.all_to_all(blocks, axes, split_axis=0, concat_axis=0, tiled=True)  56.3 us
    all_to_all x2, starting transfers between devices, exchanged(): return lax.all_to_all(blocks, axes, split_axis=0, concat_axis=0, tiled=True)  16.8 us
    pallas_call x2, Pallas kernels, gate_up(): pl.pallas_call(functools.partial(gate_up_kernel, layer), grid=(width // s...  14.4 us
    pallas_call x1, Pallas kernels, packed(): pl.pallas_call(pack_kernel, grid=(chips // 2 // pairs,), in_specs=[taken,...  9.99 us
    unnamed x20, local copies, waits for them, and re-layouts  7.48 us
  transfers between devices with their start and end apart: 5, of which 4 were waited for; matrix products, arithmetic and copies ran while one was open for 3% of the time, Pallas kernels for 5%

profile of v2, /device:TPU:0, one launch (start us, length us, event | category | flops | bytes accessed | tf_op | source)
XLA Modules:
  0.0 353.2 jit_solution(2507766868614583828)
XLA Ops:
  0.0 0.0 collective-permute-start
  0.0 0.8 reshape.91
  0.8 0.8 pad_maximum_fusion.2
  1.6 7.7 %all_to_all.64 = f32[2,8,2304]{2,1,0:T(8,128)S(1)} all-to-all(f32[2,8,2304]{2,1,0:T(8,128)S(1)} %pad_maximum_fusion), channel_id=1, replica_groups=mesh['row'=2,'col_0'=4,'col_1'=4,'col_2'=2,'core'=2] {'row'}, dimensions={0} | all-to-all | bytes 294912 | tf_op jit(solution)/shard_map/all_to_all | solution.py:144
  9.3 0.2 fusion.46
  9.5 0.8 slice_reduce_fusion
  10.3 0.1 fusion.48
  10.4 0.4 reshape.79
  10.7 0.2 slice.135
  11.0 0.2 reshape.81
  11.2 0.2 reshape.80
  11.4 3.8 %all_to_all.65 = bf16[2,4,2304]{2,1,0:T(4,128)(2,1)S(1)} all-to-all(bf16[2,4,2304]{2,1,0:T(4,128)(2,1)S(1)} %pad_maximum_fusion.3), channel_id=1, replica_groups=mesh['row'=2,'col_0'=4,'col_1'=4,'col_2'=2,'core'=2] {'core'}, dimensions={0} | all-to-all | bytes 73728 | tf_op jit(solution)/shard_map/all_to_all | solution.py:144
  15.2 1.6 broadcast_in_dim.14
  16.7 11.0 %all-to-all-start.2 = ((bf16[64,8,2304]{2,1,0:T(8,128)(2,1)}), bf16[64,8,2304]{2,1,0:T(8,128)(2,1)S(1)}, u32[]{:S(2)}, u32[]{:S(2)}) async-start(bf16[64,8,2304]{2,1,0:T(8,128)(2,1)} %broadcast_in_dim.14), calls=%async_computation.2 | async-start | bytes 4718592 | tf_op jit(solution)/shard_map/all_to_all | solution.py:144
  27.7 10.0 %pack.1 = (bf16[64,40,1152]{2,1,0:T(8,128)(2,1)}, bf16[64,32,1152]{2,1,0:T(8,128)(2,1)S(1)}) custom-call(bf16[36,2,36864]{2,1,0:T(2,128)(2,1)} %bitcast.37, bf16[36,2,36864]{2,1,0:T(2,128)(2,1)} %bitcast.38), custom_call_target="tpu_custom_call" | custom-call | tf_op jit(solution)/shard_map/pack/pallas_call | solution.py:56
  37.7 2.1 copy-done.2
  39.8 0.0 collective-permute-done
  39.8 19.6 %all-to-all-done.2 = bf16[64,8,2304]{2,1,0:T(8,128)(2,1)S(1)} async-done(((bf16[64,8,2304]{2,1,0:T(8,128)(2,1)}), bf16[64,8,2304]{2,1,0:T(8,128)(2,1)S(1)}, u32[]{:S(2)}, u32[]{:S(2)}) %all-to-all-start.2) | async-done | bytes 2359328 | tf_op jit(solution)/shard_map/all_to_all | solution.py:144
  59.4 75.6 %all_to_all.66.weight_ref.rest_ref = bf16[64,40,1152]{2,1,0:T(8,128)(2,1)} all-to-all(bf16[64,40,1152]{2,1,0:T(8,128)(2,1)} %get-tuple-element.16), channel_id=1, replica_groups=mesh['row'=2,'col_0'=4,'col_1'=4,'col_2'=2,'core'=2] {'row','col_0','col..., dimensions={0} | all-to-all | bytes 11796480 | tf_op jit(solution)/shard_map/all_to_all | solution.py:144
  135.0 5.8 %all-to-all-start.4 = ((bf16[64,32,1152]{2,1,0:T(8,128)(2,1)}), bf16[64,32,1152]{2,1,0:T(8,128)(2,1)}, u32[]{:S(2)}, u32[]{:S(2)}) async-start(bf16[64,32,1152]{2,1,0:T(8,128)(2,1)} %copy-done.2), calls=%async_computation.4 | async-start | bytes 9437184 | tf_op jit(solution)/shard_map/all_to_all | solution.py:144
  140.8 2.7 copy-done
  143.5 6.7 %gate_up.2 = (bf16[256,1152]{1,0:T(8,128)(2,1)S(1)}, bf16[256,1152]{1,0:T(8,128)(2,1)S(1)}) custom-call(s32[1]{0:T(128)} %bitcast.2.core_ref, bf16[512,2304]{1,0:T(8,128)(2,1)S(1)} %bitcast.36, bf16[64,40,1152]{2,1,0:T(8,128)(2,1)S(1)} %copy-done, bf16[64,40,1152]{2,1,0:T(8,128)(2,1)S(1)} %copy-done), custom_call_target="tpu_custom_call" | custom-call | tf_op jit(solution)/shard_map/gate_up/pallas_call | solution.py:122
  150.2 0.1 collective-permute-start.1
  150.3 2.0 collective-permute-done.1
  152.3 0.1 convert_add_fusion.1
  152.4 0.1 fusion.62
  152.5 0.1 fusion.61
  152.7 0.2 fusion.20
  153.0 0.2 maximum_select_fusion
  153.1 3.2 fusion.6
  156.3 3.2 fusion
  159.5 36.7 %all-to-all-done.4.weight_ref = bf16[64,32,1152]{2,1,0:T(8,128)(2,1)} async-done(((bf16[64,32,1152]{2,1,0:T(8,128)(2,1)}), bf16[64,32,1152]{2,1,0:T(8,128)(2,1)}, u32[]{:S(2)}, u32[]{:S(2)}) %all-to-all-start.4) | async-done | bytes 4718624 | tf_op jit(solution)/shard_map/all_to_all | solution.py:144
  196.2 2.1 reshape.84
  198.3 43.6 %all_to_all.67 = bf16[64,4,4608]{2,1,0:T(4,128)(2,1)S(1)} all-to-all(bf16[64,4,4608]{2,1,0:T(4,128)(2,1)} %reshape.84), channel_id=1, replica_groups=mesh['row'=2,'col_0'=4,'col_1'=4,'col_2'=2,'core'=2] {'row','col_0','col..., dimensions={0} | all-to-all | bytes 4718592 | tf_op jit(solution)/shard_map/all_to_all | solution.py:144
  242.0 1.0 convert_reduce_fusion.1
  242.9 0.2 multiply_reduce_fusion.1
  243.1 0.2 fusion.50
  243.3 0.1 fusion.52
  243.4 0.4 reshape.85
  243.8 0.0 slice-start
  243.8 0.2 slice.147
  244.1 0.2 reshape.87
  244.3 0.2 reshape.86
  244.5 3.8 %all_to_all.68 = bf16[2,4,2304]{2,1,0:T(4,128)(2,1)S(1)} all-to-all(bf16[2,4,2304]{2,1,0:T(4,128)(2,1)S(1)} %pad_maximum_fusion.4), channel_id=1, replica_groups=mesh['row'=2,'col_0'=4,'col_1'=4,'col_2'=2,'core'=2] {'core'}, dimensions={0} | all-to-all | bytes 73728 | tf_op jit(solution)/shard_map/all_to_all | solution.py:144
  248.2 0.2 broadcast_in_dim.15
  248.4 38.0 %all_to_all.69 = bf16[64,8,2304]{2,1,0:T(8,128)(2,1)S(1)} all-to-all(bf16[64,8,2304]{2,1,0:T(8,128)(2,1)S(1)} %broadcast_in_dim.15), channel_id=1, replica_groups=mesh['row'=2,'col_0'=4,'col_1'=4,'col_2'=2,'core'=2] {'row','col_0','col..., dimensions={0} | all-to-all | bytes 4718592 | tf_op jit(solution)/shard_map/all_to_all | solution.py:144
  286.4 2.7 copy-done.1
  289.1 7.7 %gate_up.3 = (bf16[256,1152]{1,0:T(8,128)(2,1)S(1)}, bf16[256,1152]{1,0:T(8,128)(2,1)S(1)}) custom-call(s32[1]{0:T(128)} %bitcast.2.core_ref, bf16[512,2304]{1,0:T(8,128)(2,1)S(1)} %bitcast.35, bf16[64,32,1152]{2,1,0:T(8,128)(2,1)} %all-to-all-done.4.weight_ref, bf16[64,40,1152]{2,1,0:T(8,128)(2,1)S(1)} %copy-done.1), custom_call_target="tpu_custom_call" | custom-call | tf_op jit(solution)/shard_map/gate_up/pallas_call | solution.py:122
  296.8 0.1 collective-permute-start.2
  296.9 2.0 collective-permute-done.2
  298.9 0.1 convert_add_fusion
  299.0 0.1 fusion.59
  299.2 0.1 fusion.60
  299.3 0.2 fusion.29
  299.6 0.2 maximum_select_fusion.1
  299.8 1.4 fusion.3
  301.2 3.2 fusion.1
  304.4 2.1 reshape.90
  306.5 38.5 %all_to_all.70 = bf16[64,4,4608]{2,1,0:T(4,128)(2,1)S(1)} all-to-all(bf16[64,4,4608]{2,1,0:T(4,128)(2,1)} %reshape.90), channel_id=1, replica_groups=mesh['row'=2,'col_0'=4,'col_1'=4,'col_2'=2,'core'=2] {'row','col_0','col..., dimensions={0} | all-to-all | bytes 4718592 | tf_op jit(solution)/shard_map/all_to_all | solution.py:144
  345.0 1.0 convert_reduce_fusion
  345.9 0.2 multiply_reduce_fusion
  346.1 0.1 fusion.53
  346.2 6.3 %all_to_all.71 = bf16[4,2,2304]{2,0,1:T(4,128)(2,1)S(1)} all-to-all(bf16[4,2,2304]{2,0,1:T(4,128)(2,1)S(1)} %bitcast.46), channel_id=1, replica_groups=mesh['row'=2,'col_0'=4,'col_1'=4,'col_2'=2,'core'=2] {'row'}, dimensions={1} | all-to-all | bytes 73728 | tf_op jit(solution)/shard_map/all_to_all | solution.py:215
  352.5 0.6 all_to_all.53
  (36 shorter events, 0.3 us)
Async XLA Ops:
  0.0 39.8 %collective-permute-start = (bf16[2,288,4608]{2,1,0:T(8,128)(2,1)}, bf16[2,288,4608]{2,1,0:T(8,128)(2,1)}, u32[]{:S(2)}, u32[]{:S(2)}) collective-permute-start(bf16[2,288,4608]{2,1,0:T(8,128)(2,1)} %param.11), channel_id=1, source_target_pairs={{0,1},{1,0},{2,3},{3,2},{4,5},{5,4},{6,7},{7,6},{8,9},{9,8},{10,11... | collective-permute-start | bytes 15925256 | tf_op jit(solution)/shard_map/ppermute | solution.py:172
  9.5 0.8 copy-start.3
  16.7 42.7 %all-to-all-start.2 = ((bf16[64,8,2304]{2,1,0:T(8,128)(2,1)}), bf16[64,8,2304]{2,1,0:T(8,128)(2,1)S(1)}, u32[]{:S(2)}, u32[]{:S(2)}) async-start(bf16[64,8,2304]{2,1,0:T(8,128)(2,1)} %broadcast_in_dim.14), calls=%async_computation.2 | async-start | bytes 4718592 | tf_op jit(solution)/shard_map/all_to_all | solution.py:144
  37.7 2.1 copy-start.2
  135.0 61.2 %all-to-all-start.4 = ((bf16[64,32,1152]{2,1,0:T(8,128)(2,1)}), bf16[64,32,1152]{2,1,0:T(8,128)(2,1)}, u32[]{:S(2)}, u32[]{:S(2)}) async-start(bf16[64,32,1152]{2,1,0:T(8,128)(2,1)} %copy-done.2), calls=%async_computation.4 | async-start | bytes 9437184 | tf_op jit(solution)/shard_map/all_to_all | solution.py:144
  140.8 2.7 copy-start
  150.2 2.1 collective-permute-start.1
  198.3 44.8 %copy-start.4 = (bf16[4,4608]{1,0:T(4,128)(2,1)S(1)}, bf16[4,4608]{1,0:T(4,128)(2,1)}, u32[]{:S(2)}) copy-start(bf16[4,4608]{1,0:T(4,128)(2,1)} %copy-done.3) | copy-start | bytes 110596
  198.3 44.8 %copy-start.7 = (f32[4608]{0:T(1024)S(1)}, f32[4608]{0:T(1024)}, u32[]{:S(2)}) copy-start(f32[4608]{0:T(1024)} %get-tuple-element.27) | copy-start | bytes 55300
  198.3 45.0 %copy-start.5 = (f32[4608]{0:T(1024)S(1)}, f32[4608]{0:T(1024)}, u32[]{:S(2)}) copy-start(f32[4608]{0:T(1024)} %get-tuple-element.26) | copy-start | bytes 55300
  243.8 55.9 %slice-start = ((s8[5308416]{0:T(1024)(128)(4,1)}), s8[1114112]{0:T(1024)(128)(4,1)S(1)}, s32[]{:S(2)}) async-start(s8[5308416]{0:T(1024)(128)(4,1)} %bitcast.39), calls=%async_computation.10 | async-start | bytes 2228224
  286.4 2.7 copy-start.1
  289.1 10.7 %slice-start.1 = ((s8[5308416]{0:T(1024)(128)(4,1)}), s8[4194304]{0:T(1024)(128)(4,1)S(1)}, s32[]{:S(2)}) async-start(s8[5308416]{0:T(1024)(128)(4,1)} %bitcast.39), calls=%async_computation.11 | async-start | bytes 8388608
  296.8 2.1 collective-permute-start.2
  306.5 39.6 %copy-start.6 = (f32[4608]{0:T(1024)S(1)}, f32[4608]{0:T(1024)}, u32[]{:S(2)}) copy-start(f32[4608]{0:T(1024)} %get-tuple-element.25) | copy-start | bytes 55300

commit v3 on v2

--- a/solution.py
+++ b/solution.py
@@ -59,13 +59,21 @@
         in_specs=[taken, taken],
         out_specs=[pl.BlockSpec((2 * pairs, n, width), lambda i: (i, 0, 0)) for n in lengths],
         out_shape=[jax.ShapeDtypeStruct((chips, n, width), gate_weight.dtype) for n in lengths],
-        compiler_params=pltpu.CompilerParams(vmem_limit_bytes=48 * 2**20),
+        compiler_params=pltpu.CompilerParams(vmem_limit_bytes=59 * 2**20),
         name="pack",
     )(jnp.swapaxes(gate_weight, 0, 1), jnp.swapaxes(up_weight, 0, 1))
 
 
+def bits(length):
+    return length.bit_length() - 1
+
+
+def one_hot(place, taken):
+    return (place == taken).astype(jnp.float32).astype(jnp.bfloat16)
+
+
 def gate_up_kernel(
-    layer, core_ref, normed_ref, weight_ref, rest_ref, own_ref, other_ref, spread_ref
+    layer, core_ref, normed_ref, weight_ref, rest_ref, own_ref, other_ref, spread_ref, order_ref
 ):
     tokens = normed_ref.shape[0]
     chips, whole, width = weight_ref.shape
@@ -80,12 +88,18 @@
         part = narrow // chips
         taken = lax.broadcasted_iota(jnp.int32, (narrow, chips * rest), 0)
         put = lax.broadcasted_iota(jnp.int32, (narrow, chips * rest), 1)
-        place = taken // part * rest + layer * part + taken % part
+        place = ((taken >> bits(part)) << bits(rest)) + layer * part + (taken & (part - 1))
         spread_ref[...] = jnp.dot(
             normed_ref[:, chips * whole :],
-            (place == put).astype(jnp.float32).astype(jnp.bfloat16),
+            one_hot(place, put),
             preferred_element_type=jnp.float32,
         ).astype(jnp.bfloat16)
+        put = lax.broadcasted_iota(jnp.int32, (tokens, tokens), 0)
+        taken = lax.broadcasted_iota(jnp.int32, (tokens, tokens), 1)
+        owner = ((put >> bits(own)) + core_ref[0]) & (cores - 1)
+        chip = (put & (own - 1)) >> bits(count)
+        place = chip * (cores * count) + owner * count + (put & (count - 1))
+        order_ref[...] = one_hot(place, taken)
 
     part = jnp.dot(
         normed_ref[:, : chips * whole],
@@ -97,14 +111,8 @@
         rest_ref[...].reshape(chips * rest, width),
         preferred_element_type=jnp.float32,
     )
-    put = lax.broadcasted_iota(jnp.int32, (tokens, tokens), 0)
-    taken = lax.broadcasted_iota(jnp.int32, (tokens, tokens), 1)
-    owner = (put // own + core_ref[0]) % cores
-    place = put % own // count * (cores * count) + owner * count + put % count
     ordered = jnp.dot(
-        (place == taken).astype(jnp.float32).astype(jnp.bfloat16),
-        part.astype(jnp.bfloat16),
-        preferred_element_type=jnp.float32,
+        order_ref[...], part.astype(jnp.bfloat16), preferred_element_type=jnp.float32
     ).astype(own_ref.dtype)
     own_ref[...] = ordered[:own]
     other_ref[...] = ordered[own:]
@@ -130,12 +138,96 @@
         ],
         out_specs=[pl.BlockSpec((own, step), lambda i: (0, i))] * 2,
         out_shape=[jax.ShapeDtypeStruct((own, width), jnp.bfloat16)] * 2,
-        scratch_shapes=[pltpu.VMEM((tokens, chips * rest), jnp.bfloat16)],
-        compiler_params=pltpu.CompilerParams(vmem_limit_bytes=40 * 2**20),
+        scratch_shapes=[
+            pltpu.VMEM((tokens, chips * rest), jnp.bfloat16),
+            pltpu.VMEM((tokens, tokens), jnp.bfloat16),
+        ],
+        compiler_params=pltpu.CompilerParams(vmem_limit_bytes=56 * 2**20),
         name="gate_up",
     )(core.reshape(1), normed, weights, rests)
 
 
+def down_kernel(place_ref, mine_ref, got_ref, *refs):
+    own_low_ref, own_high_ref, other_low_ref, other_high_ref, out_ref = refs[:5]
+    hidden_ref, own_ref, other_ref, order_ref = refs[5:]
+    rows, width = mine_ref.shape
+    half = width // 2
+    aligned = half // 128 * 128
+    stored = own_ref.shape[1]
+    chips, put_rows, step = out_ref.shape
+    count = put_rows // 2
+
+    @pl.when(pl.program_id(0) == 0)
+    def _():
+        summed = mine_ref[...].astype(jnp.float32) + got_ref[...].astype(jnp.float32)
+        main = jax.nn.gelu(summed[:, :aligned], approximate=True)
+        main = (main * summed[:, aligned : 2 * aligned]).astype(jnp.bfloat16)
+        tail = jax.nn.gelu(summed[:, 2 * aligned : half + aligned], approximate=True)
+        tail = (tail * summed[:, half + aligned :]).astype(jnp.bfloat16)
+
+        @pl.when(place_ref[1] == 0)
+        def _():
+            hidden_ref[:, :aligned] = main
+            hidden_ref[:, aligned:] = tail
+
+        @pl.when(place_ref[1] != 0)
+        def _():
+            hidden_ref[:, : half - aligned] = tail
+            hidden_ref[:, half - aligned :] = main
+
+        @pl.when(place_ref[0] == 0)
+        def _():
+            own_ref[...] = hidden_ref[:, :stored]
+            other_ref[...] = hidden_ref[:, stored:]
+
+        @pl.when(place_ref[0] != 0)
+        def _():
+            own_ref[...] = hidden_ref[:, stored:]
+            other_ref[...] = hidden_ref[:, :stored]
+
+        put = lax.broadcasted_iota(jnp.int32, (2 * rows, 2 * rows), 0)
+        taken = lax.broadcasted_iota(jnp.int32, (2 * rows, 2 * rows), 1)
+        side = (put >> bits(count)) & 1
+        place = side * rows + ((put >> bits(put_rows)) << bits(count)) + (put & (count - 1))
+        order_ref[...] = one_hot(place, taken)
+
+    sides = []
+    for mine, theirs in ((own_low_ref, other_low_ref), (own_high_ref, other_high_ref)):
+        part = jnp.dot(own_ref[...], mine[0], preferred_element_type=jnp.float32)
+        part += jnp.dot(other_ref[...], theirs[0], preferred_element_type=jnp.float32)
+        sides.append(part.astype(jnp.bfloat16))
+    ordered = jnp.dot(
+        order_ref[...], jnp.concatenate(sides, axis=0), preferred_element_type=jnp.float32
+    )
+    out_ref[...] = ordered.reshape(chips, put_rows, step).astype(out_ref.dtype)
+
+
+def down(mine, got, own_down, other_down, layer, place, chips):
+    rows, width = mine.shape
+    _, stored, model_width = own_down.shape
+    step = 384
+    steps = model_width // 2 // step
+    whole = pl.BlockSpec((rows, width), lambda i: (0, 0))
+    low = pl.BlockSpec((1, stored, step), lambda i: (layer, 0, i))
+    high = pl.BlockSpec((1, stored, step), lambda i: (layer, 0, steps + i))
+    put_rows = 2 * rows // chips
+    return pl.pallas_call(
+        down_kernel,
+        grid=(steps,),
+        in_specs=[pl.BlockSpec(memory_space=pltpu.SMEM), whole, whole, low, high, low, high],
+        out_specs=pl.BlockSpec((chips, put_rows, step), lambda i: (0, 0, i)),
+        out_shape=jax.ShapeDtypeStruct((chips, put_rows, model_width // 2), jnp.bfloat16),
+        scratch_shapes=[
+            pltpu.VMEM((rows, width // 2), jnp.bfloat16),
+            pltpu.VMEM((rows, stored), jnp.bfloat16),
+            pltpu.VMEM((rows, stored), jnp.bfloat16),
+            pltpu.VMEM((2 * rows, 2 * rows), jnp.bfloat16),
+        ],
+        compiler_params=pltpu.CompilerParams(vmem_limit_bytes=48 * 2**20),
+        name="down",
+    )(place, mine, got, own_down, own_down, other_down, other_down)
+
+
 def copies_of(value, axes):
     return jnp.broadcast_to(value, (lax.axis_size(axes), *value.shape))
 
@@ -145,13 +237,18 @@
 
 
 def slabs(normed, chips, cores):
-    count, model_width = normed.shape
-    rows = model_width // (chips * cores)
+    halves, count, model_half = normed.shape
+    rows = model_half * halves // (chips * cores)
     whole = rows // 8 * 8
-    cut = normed.reshape(count, chips, cores, rows).transpose(2, 0, 1, 3)
+    cut = normed.reshape(halves, count, chips // halves, cores, rows).transpose(3, 1, 0, 2, 4)
     main = cut[..., :whole].reshape(cores, count, chips * whole)
     tail = cut[..., whole:].reshape(cores, count, chips * (rows - whole))
     return jnp.concatenate((main, tail), axis=2)
+
+
+def scale_of(values):
+    squares = jnp.sum(values * values, axis=(0, 2), keepdims=True)
+    return lax.rsqrt(squares / (values.shape[0] * values.shape[2]) + norm_eps)
 
 
 def on_device(tokens, pre_gain, post_gain, gate_weight, up_weight, down_weight):
@@ -159,15 +256,15 @@
     chips = lax.axis_size(CHIP)
     cores = lax.axis_size("core")
     core = lax.axis_index("core")
-    side = lax.axis_index("col_2")
-
-    count = tokens.shape[0] // lax.axis_size("row")
+    place = jnp.stack((core, lax.axis_index("col_2")))
+
+    halves = lax.axis_size("row")
+    count = tokens.shape[0] // halves
     gains = copies_of(jnp.concatenate((pre_gain, post_gain), axis=0), "row")
-    mixed = tokens.reshape(-1, count, tokens.shape[1]).astype(jnp.float32)
+    mixed = tokens.reshape(halves, count, tokens.shape[1]).astype(jnp.float32)
     mixed = exchanged(jnp.concatenate((mixed, gains), axis=1), "row")
-    mixed = jnp.concatenate((mixed[0], mixed[1]), axis=1)
-    current = mixed[:count].astype(jnp.bfloat16)
-    gains = 1.0 + mixed[count:]
+    current = mixed[:, :count].astype(jnp.bfloat16)
+    gains = 1.0 + mixed[:, count:]
 
     other_down = lax.ppermute(down_weight, "core", SWAP)
     first, later = packed(gate_weight, up_weight, chips)
@@ -177,42 +274,21 @@
 
     for layer in range(layers):
         values = current.astype(jnp.float32)
-        scale_pre = lax.rsqrt(jnp.mean(values * values, axis=1, keepdims=True) + norm_eps)
-        normed = (values * scale_pre * gains[layer][None, :]).astype(jnp.bfloat16)
+        normed = (values * scale_of(values) * gains[:, layer][:, None]).astype(jnp.bfloat16)
         cut = exchanged(slabs(normed, chips, cores), "core")
         cut = cut.reshape(cores * count, -1)
         everything = exchanged(copies_of(cut, CHIP), CHIP).reshape(-1, cut.shape[1])
         weights = first if layer == 0 else later
         mine, theirs = gate_up(everything, weights, first, layer, core, cores)
-        width = mine.shape[1]
-        arrived = lax.ppermute(theirs, "core", SWAP)
-        summed = mine.astype(jnp.float32) + arrived.astype(jnp.float32)
-        half = width // 2
-        aligned = half // 128 * 128
-        gate = jnp.concatenate(
-            (summed[:, :aligned], summed[:, 2 * aligned : half + aligned]), axis=1
-        )
-        up_proj = jnp.concatenate(
-            (summed[:, aligned : 2 * aligned], summed[:, half + aligned :]), axis=1
-        )
-        hidden = (jax.nn.gelu(gate, approximate=True) * up_proj).astype(jnp.bfloat16)
-        turned = jnp.concatenate((hidden[:, aligned:], hidden[:, :aligned]), axis=1)
-        hidden = jnp.where(side == 0, hidden, turned)
-        stored = down_weight.shape[1]
-        low, high = hidden[:, :stored], hidden[:, stored:]
-        own = jnp.where(core == 0, low, high)
-        other = jnp.where(core == 0, high, low)
-        branch = jnp.dot(own, down_weight[layer], preferred_element_type=jnp.float32)
-        branch += jnp.dot(other, other_down[layer], preferred_element_type=jnp.float32)
-        sent = branch.astype(jnp.bfloat16)
+        got = lax.ppermute(theirs, "core", SWAP)
+        sent = down(mine, got, down_weight, other_down, layer, place, chips)
         if layer == 0:
             sent, later = lax.optimization_barrier((sent, later))
-        arrived = exchanged(sent.reshape(chips, count, -1), CHIP)
-        branch = jnp.sum(arrived.astype(jnp.float32), axis=0)
-        scale_post = lax.rsqrt(jnp.mean(branch * branch, axis=1, keepdims=True) + norm_eps)
-        post = branch * scale_post * gains[layers + layer][None, :]
+        arrived = exchanged(sent, CHIP)
+        branch = jnp.sum(arrived.astype(jnp.float32), axis=0).reshape(values.shape)
+        post = branch * scale_of(branch) * gains[:, layers + layer][:, None]
         current = (values + post).astype(jnp.bfloat16)
-    return lax.all_to_all(current, "row", split_axis=1, concat_axis=0, tiled=True)
+    return exchanged(current, "row").reshape(tokens.shape)
 
 
 def solution(mesh):

time: 355 us -> 351 us (0.989)
  blocking collectives: 217 us -> 137 us
  waiting for transfers between devices: 60.3 us -> 121 us
  Pallas kernels: 24.4 us -> 48.9 us
  starting transfers between devices: 17 us -> 32.6 us
  matrix products: 11 us -> 0 us
  local copies, waits for them, and re-layouts: 18.1 us -> 7.56 us
    all_to_all x7 -> x6, blocking collectives: 211 us -> 137 us  [exchanged(): return lax.all_to_all(blocks, axes, split_axis=0, concat_axis=0, tiled=True)]
    all_to_all x2 -> x4, waiting for transfers between devices: 56.3 us -> 117 us  [exchanged(): return lax.all_to_all(blocks, axes, split_axis=0, concat_axis=0, tiled=True)]
    pallas_call x0 -> x2, Pallas kernels: none -> 19 us  [down(): pl.pallas_call(down_kernel, grid=(steps,), in_specs=[pl.BlockSpec(memory_...]
    all_to_all x2 -> x4, starting transfers between devices: 16.8 us -> 32.6 us  [exchanged(): return lax.all_to_all(blocks, axes, split_axis=0, concat_axis=0, tiled=True)]
    dot_general x4 -> x0, matrix products: 11 us -> none  [the longest x2 6.37 us: on_device(): jnp.dot(other, other_down[layer], preferred_element_type=jnp.float32)]
    all_to_all x1 -> x0, blocking collectives: 6.32 us -> none  [on_device(): lax.all_to_all(current, 'row', split_axis=1, concat_axis=0, tiled=True)]
    unnamed x20 -> x9, local copies, waits for them, and re-layouts: 7.48 us -> 2.18 us
    pallas_call x2, Pallas kernels: 14.4 us -> 18.3 us  [gate_up(): pl.pallas_call(functools.partial(gate_up_kernel, layer), grid=(width // s...]
  transfers between devices with their start and end apart: 5 -> 7, of which waited for: 4 -> 6; matrix products, arithmetic and copies ran while one was open for 3% -> 1% of each run, Pallas kernels for 5% -> 9%
where the time goes in v3:
time: 351 us; the launch traced here: 350 us
  blocking collectives  137 us (39%)
  waiting for transfers between devices  121 us (34%)
  Pallas kernels  48.9 us (14%)
  starting transfers between devices  32.6 us (9%)
  local copies, waits for them, and re-layouts  7.56 us (2%)
    all_to_all x6, blocking collectives, exchanged(): return lax.all_to_all(blocks, axes, split_axis=0, concat_axis=0, tiled=True)  137 us
    all_to_all x4, waiting for transfers between devices, exchanged(): return lax.all_to_all(blocks, axes, split_axis=0, concat_axis=0, tiled=True)  117 us
    all_to_all x4, starting transfers between devices, exchanged(): return lax.all_to_all(blocks, axes, split_axis=0, concat_axis=0, tiled=True)  32.6 us
    pallas_call x2, Pallas kernels, down(): pl.pallas_call(down_kernel, grid=(steps,), in_specs=[pl.BlockSpec(memory_...  19 us
    pallas_call x2, Pallas kernels, gate_up(): pl.pallas_call(functools.partial(gate_up_kernel, layer), grid=(width // s...  18.3 us
    pallas_call x1, Pallas kernels, packed(): pl.pallas_call(pack_kernel, grid=(chips // 2 // pairs,), in_specs=[taken,...  11.7 us
  transfers between devices with their start and end apart: 7, of which 6 were waited for; matrix products, arithmetic and copies ran while one was open for 1% of the time, Pallas kernels for 9%

profile of v3, /device:TPU:0, one launch (start us, length us, event | category | flops | bytes accessed | tf_op | source)
XLA Modules:
  0.0 349.6 jit_solution(11697369889493856690)
XLA Ops:
  0.0 0.0 collective-permute-start
  0.0 0.8 reshape.91
  0.8 0.8 pad_maximum_fusion.1
  1.6 7.7 %all_to_all.50 = f32[2,8,2304]{2,1,0:T(8,128)S(1)} all-to-all(f32[2,8,2304]{2,1,0:T(8,128)S(1)} %pad_maximum_fusion), channel_id=1, replica_groups=mesh['row'=2,'col_0'=4,'col_1'=4,'col_2'=2,'core'=2] {'row'}, dimensions={0} | all-to-all | bytes 294912 | tf_op jit(solution)/shard_map/all_to_all | solution.py:236
  9.3 0.2 fusion
  9.5 0.1 fusion.9
  9.6 0.1 fusion.2
  9.7 0.4 reshape.78
  10.0 0.2 slice.45
  10.3 0.2 reshape.80
  10.5 0.2 reshape.79
  10.7 3.8 %all_to_all.51 = bf16[2,4,2304]{2,1,0:T(4,128)(2,1)S(1)} all-to-all(bf16[2,4,2304]{2,1,0:T(4,128)(2,1)S(1)} %pad_maximum_fusion.2), channel_id=1, replica_groups=mesh['row'=2,'col_0'=4,'col_1'=4,'col_2'=2,'core'=2] {'core'}, dimensions={0} | all-to-all | bytes 73728 | tf_op jit(solution)/shard_map/all_to_all | solution.py:236
  14.5 1.6 broadcast_in_dim.14
  16.0 11.0 %all-to-all-start.2 = ((bf16[64,8,2304]{2,1,0:T(8,128)(2,1)}), bf16[64,8,2304]{2,1,0:T(8,128)(2,1)S(1)}, u32[]{:S(2)}, u32[]{:S(2)}) async-start(bf16[64,8,2304]{2,1,0:T(8,128)(2,1)} %broadcast_in_dim.14), calls=%async_computation.2 | async-start | bytes 4718592 | tf_op jit(solution)/shard_map/all_to_all | solution.py:236
  27.0 11.7 %pack.1 = (bf16[64,40,1152]{2,1,0:T(8,128)(2,1)}, bf16[64,32,1152]{2,1,0:T(8,128)(2,1)}) custom-call(bf16[36,2,36864]{2,1,0:T(2,128)(2,1)} %bitcast.30, bf16[36,2,36864]{2,1,0:T(2,128)(2,1)} %bitcast.31), custom_call_target="tpu_custom_call" | custom-call | tf_op jit(solution)/shard_map/pack/pallas_call | solution.py:56
  38.7 0.0 collective-permute-done.refs_2_.refs_3_
  38.7 20.1 %all-to-all-done.2 = bf16[64,8,2304]{2,1,0:T(8,128)(2,1)S(1)} async-done(((bf16[64,8,2304]{2,1,0:T(8,128)(2,1)}), bf16[64,8,2304]{2,1,0:T(8,128)(2,1)S(1)}, u32[]{:S(2)}, u32[]{:S(2)}) %all-to-all-start.2) | async-done | bytes 2359328 | tf_op jit(solution)/shard_map/all_to_all | solution.py:236
  58.7 0.0 copy-start.2
  58.7 75.6 %all_to_all.52.weight_ref.rest_ref = bf16[64,40,1152]{2,1,0:T(8,128)(2,1)} all-to-all(bf16[64,40,1152]{2,1,0:T(8,128)(2,1)} %get-tuple-element.16), channel_id=1, replica_groups=mesh['row'=2,'col_0'=4,'col_1'=4,'col_2'=2,'core'=2] {'row','col_0','col..., dimensions={0} | all-to-all | bytes 11796480 | tf_op jit(solution)/shard_map/all_to_all | solution.py:236
  134.3 0.0 copy-done.2
  134.3 5.8 %all-to-all-start.4 = ((bf16[64,32,1152]{2,1,0:T(8,128)(2,1)}), bf16[64,32,1152]{2,1,0:T(8,128)(2,1)}, u32[]{:S(2)}, u32[]{:S(2)}) async-start(bf16[64,32,1152]{2,1,0:T(8,128)(2,1)} %get-tuple-element.20), calls=%async_computation.4 | async-start | bytes 9437184 | tf_op jit(solution)/shard_map/all_to_all | solution.py:236
  140.1 9.1 %gate_up.2 = (bf16[256,1152]{1,0:T(8,128)(2,1)}, bf16[256,1152]{1,0:T(8,128)(2,1)}) custom-call(s32[1]{0:T(128)} %bitcast.core_ref, bf16[512,2304]{1,0:T(8,128)(2,1)} %bitcast.29, bf16[64,40,1152]{2,1,0:T(8,128)(2,1)} %all_to_all.52.weight_ref.rest_ref, bf16[64,40,1152]{2,1,0:T(8,128)(2,1)} %all_to_all.52.weight_ref.rest_ref), custom_call_target="tpu_custom_call" | custom-call | tf_op jit(solution)/shard_map/gate_up/pallas_call | solution.py:130
  149.3 0.0 collective-permute-start.1
  149.3 0.1 pad_add_fusion.place_ref
  149.4 2.1 collective-permute-done.1.got_ref
  151.5 0.0 copy-start
  151.5 1.1 copy-done
  152.6 9.5 %down.2 = bf16[64,8,2304]{2,1,0:T(8,128)(2,1)} custom-call(s32[2]{0:T(128)S(1)} %pad_add_fusion.place_ref, bf16[256,1152]{1,0:T(8,128)(2,1)S(1)} %copy-done, bf16[256,1152]{1,0:T(8,128)(2,1)S(1)} %collective-permute-done.1.got_ref, bf16[2,288,4608]{2,1,0:T(8,128)(2,1)} %refs_1_.3, bf16[2,288,4608]{2,1,0:T(8,128)(2,1)} %refs_1_.3, ...), custom_call_target="tpu_custom_call" | custom-call | tf_op jit(solution)/shard_map/down/pallas_call | solution.py:214
  162.1 33.5 %all-to-all-done.4.weight_ref = bf16[64,32,1152]{2,1,0:T(8,128)(2,1)} async-done(((bf16[64,32,1152]{2,1,0:T(8,128)(2,1)}), bf16[64,32,1152]{2,1,0:T(8,128)(2,1)}, u32[]{:S(2)}, u32[]{:S(2)}) %all-to-all-start.4) | async-done | bytes 4718624 | tf_op jit(solution)/shard_map/all_to_all | solution.py:236
  195.5 10.7 %all-to-all-start.5 = ((bf16[64,8,2304]{2,1,0:T(8,128)(2,1)}), bf16[64,8,2304]{2,1,0:T(8,128)(2,1)S(1)}, u32[]{:S(2)}, u32[]{:S(2)}) async-start(bf16[64,8,2304]{2,1,0:T(8,128)(2,1)} %down.2), calls=%async_computation.5 | async-start | bytes 4718592 | tf_op jit(solution)/shard_map/all_to_all | solution.py:236
  206.3 31.4 %all-to-all-done.5 = bf16[64,8,2304]{2,1,0:T(8,128)(2,1)S(1)} async-done(((bf16[64,8,2304]{2,1,0:T(8,128)(2,1)}), bf16[64,8,2304]{2,1,0:T(8,128)(2,1)S(1)}, u32[]{:S(2)}, u32[]{:S(2)}) %all-to-all-start.5) | async-done | bytes 2359328 | tf_op jit(solution)/shard_map/all_to_all | solution.py:236
  237.6 0.3 convert_reduce_fusion.1
  238.0 0.1 multiply_reduce_fusion.1
  238.1 0.1 reduce_sum.71
  238.3 0.2 fusion.4
  238.5 0.1 fusion.6
  238.6 0.4 reshape.84
  239.0 0.2 slice.49
  239.2 0.2 reshape.86
  239.4 0.2 reshape.85
  239.6 3.8 %all_to_all.53 = bf16[2,4,2304]{2,1,0:T(4,128)(2,1)S(1)} all-to-all(bf16[2,4,2304]{2,1,0:T(4,128)(2,1)S(1)} %pad_maximum_fusion.3), channel_id=1, replica_groups=mesh['row'=2,'col_0'=4,'col_1'=4,'col_2'=2,'core'=2] {'core'}, dimensions={0} | all-to-all | bytes 73728 | tf_op jit(solution)/shard_map/all_to_all | solution.py:236
  243.4 0.2 broadcast_in_dim.15
  243.6 39.6 %all_to_all.54 = bf16[64,8,2304]{2,1,0:T(8,128)(2,1)} all-to-all(bf16[64,8,2304]{2,1,0:T(8,128)(2,1)S(1)} %broadcast_in_dim.15), channel_id=1, replica_groups=mesh['row'=2,'col_0'=4,'col_1'=4,'col_2'=2,'core'=2] {'row','col_0','col..., dimensions={0} | all-to-all | bytes 4718592 | tf_op jit(solution)/shard_map/all_to_all | solution.py:236
  283.2 9.1 %gate_up.3 = (bf16[256,1152]{1,0:T(8,128)(2,1)}, bf16[256,1152]{1,0:T(8,128)(2,1)}) custom-call(s32[1]{0:T(128)} %bitcast.core_ref, bf16[512,2304]{1,0:T(8,128)(2,1)} %bitcast.28, bf16[64,32,1152]{2,1,0:T(8,128)(2,1)} %all-to-all-done.4.weight_ref, bf16[64,40,1152]{2,1,0:T(8,128)(2,1)} %all_to_all.52.weight_ref.rest_ref), custom_call_target="tpu_custom_call" | custom-call | tf_op jit(solution)/shard_map/gate_up/pallas_call | solution.py:130
  292.3 0.0 collective-permute-start.2
  292.3 2.2 collective-permute-done.2.got_ref
  294.5 0.0 copy-start.1
  294.5 1.1 copy-done.1
  295.6 9.5 %down.3 = bf16[64,8,2304]{2,1,0:T(8,128)(2,1)} custom-call(s32[2]{0:T(128)S(1)} %pad_add_fusion.place_ref, bf16[256,1152]{1,0:T(8,128)(2,1)S(1)} %copy-done.1, bf16[256,1152]{1,0:T(8,128)(2,1)S(1)} %collective-permute-done.2.got_ref, bf16[2,288,4608]{2,1,0:T(8,128)(2,1)} %refs_1_.3, bf16[2,288,4608]{2,1,0:T(8,128)(2,1)} %refs_1_.3, ...), custom_call_target="tpu_custom_call" | custom-call | tf_op jit(solution)/shard_map/down/pallas_call | solution.py:214
  305.1 5.1 %all-to-all-start.8 = ((bf16[64,8,2304]{2,1,0:T(8,128)(2,1)}), bf16[64,8,2304]{2,1,0:T(8,128)(2,1)S(1)}, u32[]{:S(2)}, u32[]{:S(2)}) async-start(bf16[64,8,2304]{2,1,0:T(8,128)(2,1)} %down.3), calls=%async_computation.8 | async-start | bytes 4718592 | tf_op jit(solution)/shard_map/all_to_all | solution.py:236
  310.2 31.7 %all-to-all-done.8 = bf16[64,8,2304]{2,1,0:T(8,128)(2,1)S(1)} async-done(((bf16[64,8,2304]{2,1,0:T(8,128)(2,1)}), bf16[64,8,2304]{2,1,0:T(8,128)(2,1)S(1)}, u32[]{:S(2)}, u32[]{:S(2)}) %all-to-all-start.8) | async-done | bytes 2359328 | tf_op jit(solution)/shard_map/all_to_all | solution.py:236
  341.9 0.3 convert_reduce_fusion
  342.3 0.1 multiply_reduce_fusion
  342.4 0.1 reduce_sum.76
  342.5 0.1 fusion.7
  342.6 6.3 %all_to_all.55 = bf16[2,4,2304]{2,1,0:T(4,128)(2,1)S(1)} all-to-all(bf16[2,4,2304]{2,1,0:T(4,128)(2,1)S(1)} %fusion.7), channel_id=1, replica_groups=mesh['row'=2,'col_0'=4,'col_1'=4,'col_2'=2,'core'=2] {'row'}, dimensions={0} | all-to-all | bytes 73728 | tf_op jit(solution)/shard_map/all_to_all | solution.py:236
  349.0 0.6 reshape.90
  (21 shorter events, 0.4 us)
Async XLA Ops:
  0.0 38.7 %collective-permute-start = (bf16[2,288,4608]{2,1,0:T(8,128)(2,1)}, bf16[2,288,4608]{2,1,0:T(8,128)(2,1)}, u32[]{:S(2)}, u32[]{:S(2)}) collective-permute-start(bf16[2,288,4608]{2,1,0:T(8,128)(2,1)} %refs_1_.3), channel_id=1, source_target_pairs={{0,1},{1,0},{2,3},{3,2},{4,5},{5,4},{6,7},{7,6},{8,9},{9,8},{10,11... | collective-permute-start | bytes 15925256 | tf_op jit(solution)/shard_map/ppermute | solution.py:269
  16.0 42.7 %all-to-all-start.2 = ((bf16[64,8,2304]{2,1,0:T(8,128)(2,1)}), bf16[64,8,2304]{2,1,0:T(8,128)(2,1)S(1)}, u32[]{:S(2)}, u32[]{:S(2)}) async-start(bf16[64,8,2304]{2,1,0:T(8,128)(2,1)} %broadcast_in_dim.14), calls=%async_computation.2 | async-start | bytes 4718592 | tf_op jit(solution)/shard_map/all_to_all | solution.py:236
  58.7 75.6 %copy-start.2 = (bf16[64,8,2304]{2,1,0:T(8,128)(2,1)}, bf16[64,8,2304]{2,1,0:T(8,128)(2,1)S(1)}, u32[]{:S(2)}) copy-start(bf16[64,8,2304]{2,1,0:T(8,128)(2,1)S(1)} %all-to-all-done.2) | copy-start | bytes 7077892
  134.3 61.2 %all-to-all-start.4 = ((bf16[64,32,1152]{2,1,0:T(8,128)(2,1)}), bf16[64,32,1152]{2,1,0:T(8,128)(2,1)}, u32[]{:S(2)}, u32[]{:S(2)}) async-start(bf16[64,32,1152]{2,1,0:T(8,128)(2,1)} %get-tuple-element.20), calls=%async_computation.4 | async-start | bytes 9437184 | tf_op jit(solution)/shard_map/all_to_all | solution.py:236
  149.3 2.2 collective-permute-start.1
  151.5 1.1 copy-start
  195.5 42.1 %all-to-all-start.5 = ((bf16[64,8,2304]{2,1,0:T(8,128)(2,1)}), bf16[64,8,2304]{2,1,0:T(8,128)(2,1)S(1)}, u32[]{:S(2)}, u32[]{:S(2)}) async-start(bf16[64,8,2304]{2,1,0:T(8,128)(2,1)} %down.2), calls=%async_computation.5 | async-start | bytes 4718592 | tf_op jit(solution)/shard_map/all_to_all | solution.py:236
  292.3 2.2 collective-permute-start.2
  294.5 1.1 copy-start.1
  305.1 36.8 %all-to-all-start.8 = ((bf16[64,8,2304]{2,1,0:T(8,128)(2,1)}), bf16[64,8,2304]{2,1,0:T(8,128)(2,1)S(1)}, u32[]{:S(2)}, u32[]{:S(2)}) async-start(bf16[64,8,2304]{2,1,0:T(8,128)(2,1)} %down.3), calls=%async_computation.8 | async-start | bytes 4718592 | tf_op jit(solution)/shard_map/all_to_all | solution.py:236

commit v4 on v3

--- a/solution.py
+++ b/solution.py
@@ -12,6 +12,7 @@
 ROW_COL = ("row", *COL)
 CHIP = ("row", "col_0", "col_1", "col_2")
 
+ORDER = ("col_2", "row", "col_0", "col_1")
 SWAP = [(0, 1), (1, 0)]
 
 norm_eps = 1e-06
@@ -72,18 +73,22 @@
     return (place == taken).astype(jnp.float32).astype(jnp.bfloat16)
 
 
-def gate_up_kernel(
-    layer, core_ref, normed_ref, weight_ref, rest_ref, own_ref, other_ref, spread_ref, order_ref
-):
-    tokens = normed_ref.shape[0]
-    chips, whole, width = weight_ref.shape
+def turned(low, high):
+    low_first = lax.broadcasted_iota(jnp.int32, low.shape, 1) < low.shape[1] // 2
+    low_turned = pltpu.roll(low, low.shape[1] // 2, 1)
+    high_turned = pltpu.roll(high, low.shape[1] // 2, 1)
+    return jnp.where(low_first, low, high_turned), jnp.where(low_first, low_turned, high)
+
+
+def gate_up_kernel(layer, core_ref, normed_ref, *refs):
+    weight_ref, rest_ref, weight_end_ref, rest_end_ref = refs[:4]
+    own_ref, other_ref, spread_ref = refs[4:]
+    chips, whole, _ = weight_ref.shape
     rest = rest_ref.shape[1]
-    own = own_ref.shape[0]
-    cores = tokens // own
-    count = own // chips
     narrow = normed_ref.shape[1] - chips * whole
-
-    @pl.when(pl.program_id(0) == 0)
+    step = pl.program_id(0)
+
+    @pl.when(step == 0)
     def _():
         part = narrow // chips
         taken = lax.broadcasted_iota(jnp.int32, (narrow, chips * rest), 0)
@@ -94,28 +99,41 @@
             one_hot(place, put),
             preferred_element_type=jnp.float32,
         ).astype(jnp.bfloat16)
-        put = lax.broadcasted_iota(jnp.int32, (tokens, tokens), 0)
-        taken = lax.broadcasted_iota(jnp.int32, (tokens, tokens), 1)
-        owner = ((put >> bits(own)) + core_ref[0]) & (cores - 1)
-        chip = (put & (own - 1)) >> bits(count)
-        place = chip * (cores * count) + owner * count + (put & (count - 1))
-        order_ref[...] = one_hot(place, taken)
-
-    part = jnp.dot(
-        normed_ref[:, : chips * whole],
-        weight_ref[...].reshape(chips * whole, width),
-        preferred_element_type=jnp.float32,
-    )
-    part += jnp.dot(
-        spread_ref[...],
-        rest_ref[...].reshape(chips * rest, width),
-        preferred_element_type=jnp.float32,
-    )
-    ordered = jnp.dot(
-        order_ref[...], part.astype(jnp.bfloat16), preferred_element_type=jnp.float32
-    ).astype(own_ref.dtype)
-    own_ref[...] = ordered[:own]
-    other_ref[...] = ordered[own:]
+
+    def product(main_ref, tail_ref, lanes):
+        width = main_ref.shape[2]
+        part = jnp.dot(
+            normed_ref[:, : chips * whole],
+            main_ref[...].reshape(chips * whole, width),
+            preferred_element_type=jnp.float32,
+        )
+        part += jnp.dot(
+            spread_ref[...],
+            tail_ref[...].reshape(chips * rest, width),
+            preferred_element_type=jnp.float32,
+        )
+        part = part.reshape(chips, -1, width)
+        first, second = turned(part[: chips // 2], part[chips // 2 :])
+        first = first.reshape(-1, width).astype(own_ref.dtype)
+        second = second.reshape(-1, width).astype(own_ref.dtype)
+
+        @pl.when(core_ref[0] == 0)
+        def _():
+            own_ref[:, lanes] = first
+            other_ref[:, lanes] = second
+
+        @pl.when(core_ref[0] != 0)
+        def _():
+            own_ref[:, lanes] = second
+            other_ref[:, lanes] = first
+
+    width = weight_ref.shape[2]
+    product(weight_ref, rest_ref, pl.ds(pl.multiple_of(step * width, width), width))
+
+    @pl.when(step == pl.num_programs(0) - 1)
+    def _():
+        end = weight_end_ref.shape[2]
+        product(weight_end_ref, rest_end_ref, slice(own_ref.shape[1] - end, own_ref.shape[1]))
 
 
 def gate_up(normed, weights, rests, layer, core, cores):
@@ -125,8 +143,10 @@
     rows = depth // chips
     whole = rows // 8 * 8
     rest = layers * (rows - whole)
-    step = 384
+    step = 256
+    end = width % step
     own = tokens // cores
+    kept = pl.BlockSpec((own, width), lambda i: (0, 0))
     return pl.pallas_call(
         functools.partial(gate_up_kernel, layer),
         grid=(width // step,),
@@ -135,27 +155,25 @@
             pl.BlockSpec((tokens, depth), lambda i: (0, 0)),
             pl.BlockSpec((chips, whole, step), lambda i: (0, 0, i)),
             pl.BlockSpec((chips, rest, step), lambda i: (0, whole // rest, i)),
+            pl.BlockSpec((chips, whole, end), lambda i: (0, 0, width // end - 1)),
+            pl.BlockSpec((chips, rest, end), lambda i: (0, whole // rest, width // end - 1)),
         ],
-        out_specs=[pl.BlockSpec((own, step), lambda i: (0, i))] * 2,
+        out_specs=[kept, kept],
         out_shape=[jax.ShapeDtypeStruct((own, width), jnp.bfloat16)] * 2,
-        scratch_shapes=[
-            pltpu.VMEM((tokens, chips * rest), jnp.bfloat16),
-            pltpu.VMEM((tokens, tokens), jnp.bfloat16),
-        ],
+        scratch_shapes=[pltpu.VMEM((tokens, chips * rest), jnp.bfloat16)],
         compiler_params=pltpu.CompilerParams(vmem_limit_bytes=56 * 2**20),
         name="gate_up",
-    )(core.reshape(1), normed, weights, rests)
+    )(core.reshape(1), normed, weights, rests, weights, rests)
 
 
 def down_kernel(place_ref, mine_ref, got_ref, *refs):
     own_low_ref, own_high_ref, other_low_ref, other_high_ref, out_ref = refs[:5]
-    hidden_ref, own_ref, other_ref, order_ref = refs[5:]
-    rows, width = mine_ref.shape
+    hidden_ref, turned_ref, weight_ref = refs[5:]
+    _, width = mine_ref.shape
     half = width // 2
     aligned = half // 128 * 128
-    stored = own_ref.shape[1]
+    stored = half // 2
     chips, put_rows, step = out_ref.shape
-    count = put_rows // 2
 
     @pl.when(pl.program_id(0) == 0)
     def _():
@@ -167,45 +185,38 @@
 
         @pl.when(place_ref[1] == 0)
         def _():
-            hidden_ref[:, :aligned] = main
-            hidden_ref[:, aligned:] = tail
+            turned_ref[:, :aligned] = main
+            turned_ref[:, aligned:] = tail
 
         @pl.when(place_ref[1] != 0)
         def _():
-            hidden_ref[:, : half - aligned] = tail
-            hidden_ref[:, half - aligned :] = main
+            turned_ref[:, : half - aligned] = tail
+            turned_ref[:, half - aligned :] = main
 
         @pl.when(place_ref[0] == 0)
         def _():
-            own_ref[...] = hidden_ref[:, :stored]
-            other_ref[...] = hidden_ref[:, stored:]
+            hidden_ref[...] = turned_ref[...]
 
         @pl.when(place_ref[0] != 0)
         def _():
-            own_ref[...] = hidden_ref[:, stored:]
-            other_ref[...] = hidden_ref[:, :stored]
-
-        put = lax.broadcasted_iota(jnp.int32, (2 * rows, 2 * rows), 0)
-        taken = lax.broadcasted_iota(jnp.int32, (2 * rows, 2 * rows), 1)
-        side = (put >> bits(count)) & 1
-        place = side * rows + ((put >> bits(put_rows)) << bits(count)) + (put & (count - 1))
-        order_ref[...] = one_hot(place, taken)
+            hidden_ref[:, :stored] = turned_ref[:, stored:]
+            hidden_ref[:, stored:] = turned_ref[:, :stored]
 
     sides = []
     for mine, theirs in ((own_low_ref, other_low_ref), (own_high_ref, other_high_ref)):
-        part = jnp.dot(own_ref[...], mine[0], preferred_element_type=jnp.float32)
-        part += jnp.dot(other_ref[...], theirs[0], preferred_element_type=jnp.float32)
-        sides.append(part.astype(jnp.bfloat16))
-    ordered = jnp.dot(
-        order_ref[...], jnp.concatenate(sides, axis=0), preferred_element_type=jnp.float32
-    )
-    out_ref[...] = ordered.reshape(chips, put_rows, step).astype(out_ref.dtype)
+        weight_ref[:stored] = mine[0]
+        weight_ref[stored:] = theirs[0]
+        part = jnp.dot(hidden_ref[...], weight_ref[...], preferred_element_type=jnp.float32)
+        sides.append(part.reshape(chips // 2, put_rows, step))
+    even, odd = turned(*sides)
+    both = jnp.stack((even, odd), axis=1).reshape(chips, put_rows, step)
+    out_ref[...] = both.astype(out_ref.dtype)
 
 
 def down(mine, got, own_down, other_down, layer, place, chips):
     rows, width = mine.shape
     _, stored, model_width = own_down.shape
-    step = 384
+    step = 768
     steps = model_width // 2 // step
     whole = pl.BlockSpec((rows, width), lambda i: (0, 0))
     low = pl.BlockSpec((1, stored, step), lambda i: (layer, 0, i))
@@ -219,9 +230,8 @@
         out_shape=jax.ShapeDtypeStruct((chips, put_rows, model_width // 2), jnp.bfloat16),
         scratch_shapes=[
             pltpu.VMEM((rows, width // 2), jnp.bfloat16),
-            pltpu.VMEM((rows, stored), jnp.bfloat16),
-            pltpu.VMEM((rows, stored), jnp.bfloat16),
-            pltpu.VMEM((2 * rows, 2 * rows), jnp.bfloat16),
+            pltpu.VMEM((rows, width // 2), jnp.bfloat16),
+            pltpu.VMEM((width // 2, step), jnp.bfloat16),
         ],
         compiler_params=pltpu.CompilerParams(vmem_limit_bytes=48 * 2**20),
         name="down",
@@ -234,6 +244,13 @@
 
 def exchanged(blocks, axes):
     return lax.all_to_all(blocks, axes, split_axis=0, concat_axis=0, tiled=True)
+
+
+def swapped(blocks, axis):
+    index = lax.axis_index(axis)
+    own = jnp.where(index == 0, blocks[0], blocks[1])
+    got = lax.ppermute(jnp.where(index == 0, blocks[1], blocks[0]), axis, SWAP)
+    return jnp.where(index == 0, jnp.stack((own, got)), jnp.stack((got, own)))
 
 
 def slabs(normed, chips, cores):
@@ -260,24 +277,26 @@
 
     halves = lax.axis_size("row")
     count = tokens.shape[0] // halves
-    gains = copies_of(jnp.concatenate((pre_gain, post_gain), axis=0), "row")
-    mixed = tokens.reshape(halves, count, tokens.shape[1]).astype(jnp.float32)
-    mixed = exchanged(jnp.concatenate((mixed, gains), axis=1), "row")
-    current = mixed[:, :count].astype(jnp.bfloat16)
-    gains = 1.0 + mixed[:, count:]
+    current = swapped(tokens.reshape(halves, count, tokens.shape[1]), "row")
+    gains = jnp.concatenate((pre_gain, post_gain), axis=0)
+    gains = 1.0 + swapped(jnp.stack((gains, gains)), "row")
 
     other_down = lax.ppermute(down_weight, "core", SWAP)
     first, later = packed(gate_weight, up_weight, chips)
-    first, other_down = lax.optimization_barrier((first, other_down))
+    values = current.astype(jnp.float32)
+    normed = (values * scale_of(values) * gains[:, 0][:, None]).astype(jnp.bfloat16)
+    cut = swapped(slabs(normed, chips, cores), "core").reshape(cores * count, -1)
+    first, other_down, cut = lax.optimization_barrier((first, other_down, cut))
+    everything = lax.all_gather(cut, ORDER, axis=0, tiled=True)
     first = exchanged(first, CHIP)
     later = exchanged(later, CHIP)
 
     for layer in range(layers):
         values = current.astype(jnp.float32)
-        normed = (values * scale_of(values) * gains[:, layer][:, None]).astype(jnp.bfloat16)
-        cut = exchanged(slabs(normed, chips, cores), "core")
-        cut = cut.reshape(cores * count, -1)
-        everything = exchanged(copies_of(cut, CHIP), CHIP).reshape(-1, cut.shape[1])
+        if layer > 0:
+            normed = (values * scale_of(values) * gains[:, layer][:, None]).astype(jnp.bfloat16)
+            cut = swapped(slabs(normed, chips, cores), "core").reshape(cores * count, -1)
+            everything = exchanged(copies_of(cut, ORDER), ORDER).reshape(-1, cut.shape[1])
         weights = first if layer == 0 else later
         mine, theirs = gate_up(everything, weights, first, layer, core, cores)
         got = lax.ppermute(theirs, "core", SWAP)
@@ -288,7 +307,7 @@
         branch = jnp.sum(arrived.astype(jnp.float32), axis=0).reshape(values.shape)
         post = branch * scale_of(branch) * gains[:, layers + layer][:, None]
         current = (values + post).astype(jnp.bfloat16)
-    return exchanged(current, "row").reshape(tokens.shape)
+    return swapped(current, "row").reshape(tokens.shape)
 
 
 def solution(mesh):

time: 351 us -> 366 us (1.043)
  blocking collectives: 137 us -> 40 us
  waiting for transfers between devices: 121 us -> 217 us
  between operations: 0.23 us -> 13.7 us
  starting transfers between devices: 32.6 us -> 42.3 us
  Pallas kernels: 48.9 us -> 41.4 us
    all_to_all x6 -> x1, blocking collectives: 137 us -> 40 us  [exchanged(): return lax.all_to_all(blocks, axes, split_axis=0, concat_axis=0, tiled=True)]
    all_gather x0 -> x1, waiting for transfers between devices: none -> 60.4 us  [on_device(): everything = lax.all_gather(cut, ORDER, axis=0, tiled=True)]
    all_to_all x4, waiting for transfers between devices: 117 us -> 144 us  [exchanged(): return lax.all_to_all(blocks, axes, split_axis=0, concat_axis=0, tiled=True)]
    ppermute x0 -> x5, waiting for transfers between devices: none -> 7.64 us  [swapped(): got = lax.ppermute(jnp.where(index == 0, blocks[1], blocks[0]), axis, SWAP)]
    all_to_all x4, starting transfers between devices: 32.6 us -> 39 us  [exchanged(): return lax.all_to_all(blocks, axes, split_axis=0, concat_axis=0, tiled=True)]
    pallas_call x2, Pallas kernels: 19 us -> 12.7 us  [down(): pl.pallas_call(down_kernel, grid=(steps,), in_specs=[pl.BlockSpec(memory_...]
  transfers between devices with their start and end apart: 7 -> 13, of which waited for: 6 -> 10; matrix products, arithmetic and copies ran while one was open for 1% -> 1% of each run, Pallas kernels for 9% -> 7%
where the time goes in v4:
time: 366 us; the launch traced here: 365 us
  waiting for transfers between devices  217 us (59%)
  starting transfers between devices  42.3 us (12%)
  Pallas kernels  41.4 us (11%)
  blocking collectives  40 us (11%)
  between operations  13.7 us (4%)
  local copies, waits for them, and re-layouts  6.5 us (2%)
  other arithmetic  4.04 us (1%)
    all_to_all x4, waiting for transfers between devices, exchanged(): return lax.all_to_all(blocks, axes, split_axis=0, concat_axis=0, tiled=True)  144 us
    all_gather x1, waiting for transfers between devices, on_device(): everything = lax.all_gather(cut, ORDER, axis=0, tiled=True)  60.4 us
    all_to_all x1, blocking collectives, exchanged(): return lax.all_to_all(blocks, axes, split_axis=0, concat_axis=0, tiled=True)  40 us
    all_to_all x4, starting transfers between devices, exchanged(): return lax.all_to_all(blocks, axes, split_axis=0, concat_axis=0, tiled=True)  39 us
    pallas_call x2, Pallas kernels, gate_up(): pl.pallas_call(functools.partial(gate_up_kernel, layer), grid=(width // s...  17.1 us
    pallas_call x2, Pallas kernels, down(): pl.pallas_call(down_kernel, grid=(steps,), in_specs=[pl.BlockSpec(memory_...  12.7 us
    pallas_call x1, Pallas kernels, packed(): pl.pallas_call(pack_kernel, grid=(chips // 2 // pairs,), in_specs=[taken,...  11.7 us
    ppermute x5, waiting for transfers between devices, swapped(): got = lax.ppermute(jnp.where(index == 0, blocks[1], blocks[0]), axis, SWAP)  7.64 us
  transfers between devices with their start and end apart: 13, of which 10 were waited for; matrix products, arithmetic and copies ran while one was open for 1% of the time, Pallas kernels for 7%

profile of v4, /device:TPU:0, one launch (start us, length us, event | category | flops | bytes accessed | tf_op | source)
XLA Modules:
  0.0 364.8 jit_solution(4685697269100802516)
XLA Ops:
  6.5 0.0 collective-permute-start.1
  6.5 0.9 broadcast_select_fusion.3
  7.4 2.1 collective-permute-start
  9.5 0.8 fusion.10
  10.3 0.1 collective-permute-start.2
  10.4 0.2 stack.88
  10.6 0.7 collective-permute-done
  11.3 0.2 fusion.5
  11.4 0.2 stack.89
  11.6 2.7 collective-permute-done.2
  14.3 0.2 slice_reduce_fusion.2
  14.5 0.1 mul.117
  14.7 0.3 fusion.4
  15.0 0.2 slice.76
  15.2 0.2 reshape.137
  15.4 0.2 reshape.136
  15.6 0.1 collective-permute-start.3
  15.7 11.7 %pack.1 = (bf16[64,40,1152]{2,1,0:T(8,128)(2,1)}, bf16[64,32,1152]{2,1,0:T(8,128)(2,1)}) custom-call(bf16[36,2,36864]{2,1,0:T(2,128)(2,1)} %bitcast.40, bf16[36,2,36864]{2,1,0:T(2,128)(2,1)} %bitcast.41), custom_call_target="tpu_custom_call" | custom-call | tf_op jit(solution)/shard_map/pack/pallas_call | solution.py:57
  27.4 0.0 collective-permute-done.3
  27.5 0.6 select_n.123
  28.1 0.0 collective-permute-done.1.refs_2_.refs_3_
  28.1 11.2 %all-to-all-start = ((bf16[64,40,1152]{2,1,0:T(8,128)(2,1)}), bf16[64,40,1152]{2,1,0:T(8,128)(2,1)}, u32[]{:S(2)}, u32[]{:S(2)}) async-start(bf16[64,40,1152]{2,1,0:T(8,128)(2,1)} %get-tuple-element.18), calls=%async_computation | async-start | bytes 11796480 | tf_op jit(solution)/shard_map/all_to_all | solution.py:246
  39.3 0.0 all-gather.2.cloned.1.call-start
  39.3 0.7 all-gather.2.cloned.1.call-update
  40.0 80.4 %all-to-all-done.refs_0_.refs_1_.refs_2_.refs_3_ = bf16[64,40,1152]{2,1,0:T(8,128)(2,1)} async-done(((bf16[64,40,1152]{2,1,0:T(8,128)(2,1)}), bf16[64,40,1152]{2,1,0:T(8,128)(2,1)}, u32[]{:S(2)}, u32[]{:S(2)}) %all-to-all-start) | async-done | bytes 5898272 | tf_op jit(solution)/shard_map/all_to_all | solution.py:246
  120.4 11.9 %all-to-all-start.1 = ((bf16[64,32,1152]{2,1,0:T(8,128)(2,1)}), bf16[64,32,1152]{2,1,0:T(8,128)(2,1)}, u32[]{:S(2)}, u32[]{:S(2)}) async-start(bf16[64,32,1152]{2,1,0:T(8,128)(2,1)} %get-tuple-element.22), calls=%async_computation.1 | async-start | bytes 9437184 | tf_op jit(solution)/shard_map/all_to_all | solution.py:246
  132.3 60.4 %all-gather.2.cloned.1.call-done.normed_ref = bf16[512,2304]{1,0:T(8,128)(2,1)} async-done(((bf16[8,2304]{1,0:T(8,128)(2,1)}), bf16[512,2304]{1,0:T(8,128)(2,1)}) %all-gather.2.cloned.1.call-update) | async-done | bytes 2359312 | tf_op jit(solution)/shard_map/all_gather | solution.py:290
  192.7 8.5 %gate_up.2 = (bf16[256,1152]{1,0:T(8,128)(2,1)}, bf16[256,1152]{1,0:T(8,128)(2,1)}) custom-call(s32[1]{0:T(128)} %bitcast.2.core_ref, bf16[512,2304]{1,0:T(8,128)(2,1)} %all-gather.2.cloned.1.call-done.normed_ref, bf16[64,40,1152]{2,1,0:T(8,128)(2,1)} %all-to-all-done.refs_0_.refs_1_.refs_2_.refs_3_, ...), custom_call_target="tpu_custom_call" | custom-call | tf_op jit(solution)/shard_map/gate_up/pallas_call | solution.py:150
  201.2 0.1 pad_add_fusion.place_ref
  201.3 2.1 collective-permute-done.4.got_ref
  203.5 1.1 copy-done
  204.5 6.3 %down.2 = bf16[64,8,2304]{2,1,0:T(8,128)(2,1)} custom-call(s32[2]{0:T(128)S(1)} %pad_add_fusion.place_ref, bf16[256,1152]{1,0:T(8,128)(2,1)S(1)} %copy-done, bf16[256,1152]{1,0:T(8,128)(2,1)S(1)} %collective-permute-done.4.got_ref, bf16[2,288,4608]{2,1,0:T(8,128)(2,1)} %refs_1_.3, bf16[2,288,4608]{2,1,0:T(8,128)(2,1)} %refs_1_.3, ...), custom_call_target="tpu_custom_call" | custom-call | tf_op jit(solution)/shard_map/down/pallas_call | solution.py:225
  210.8 0.0 all-to-all-done.1.refs_0_.refs_2_
  210.8 10.4 %all-to-all-start.2 = ((bf16[64,8,2304]{2,1,0:T(8,128)(2,1)}), bf16[64,8,2304]{2,1,0:T(8,128)(2,1)S(1)}, u32[]{:S(2)}, u32[]{:S(2)}) async-start(bf16[64,8,2304]{2,1,0:T(8,128)(2,1)} %down.2), calls=%async_computation.2 | async-start | bytes 4718592 | tf_op jit(solution)/shard_map/all_to_all | solution.py:246
  221.3 0.1 mul.128
  221.4 0.1 mul.134
  221.6 31.5 %all-to-all-done.2 = bf16[64,8,2304]{2,1,0:T(8,128)(2,1)S(1)} async-done(((bf16[64,8,2304]{2,1,0:T(8,128)(2,1)}), bf16[64,8,2304]{2,1,0:T(8,128)(2,1)S(1)}, u32[]{:S(2)}, u32[]{:S(2)}) %all-to-all-start.2) | async-done | bytes 2359328 | tf_op jit(solution)/shard_map/all_to_all | solution.py:246
  253.1 0.3 convert_reduce_fusion.1
  253.4 0.4 reshape.139
  253.9 0.1 multiply_reduce_fusion.1
  254.0 0.1 reduce_sum.71
  254.2 0.2 fusion.7
  254.4 0.4 fusion.3
  254.8 0.2 slice.82
  255.0 0.2 reshape.141
  255.2 0.2 reshape.140
  255.5 0.3 collective-permute-start.5
  255.8 1.2 collective-permute-done.5
  257.0 0.2 broadcast_in_dim.2
  257.1 40.0 %all_to_all.25 = bf16[64,8,2304]{2,1,0:T(8,128)(2,1)} all-to-all(bf16[64,8,2304]{2,1,0:T(8,128)(2,1)S(1)} %broadcast_in_dim.2), channel_id=1, replica_groups=mesh['row'=2,'col_0'=4,'col_1'=4,'col_2'=2,'core'=2] {'col_2','row','col..., dimensions={0} | all-to-all | bytes 4718592 | tf_op jit(solution)/shard_map/all_to_all | solution.py:246
  297.1 8.6 %gate_up.3 = (bf16[256,1152]{1,0:T(8,128)(2,1)}, bf16[256,1152]{1,0:T(8,128)(2,1)}) custom-call(s32[1]{0:T(128)} %bitcast.2.core_ref, bf16[512,2304]{1,0:T(8,128)(2,1)} %bitcast.39, bf16[64,32,1152]{2,1,0:T(8,128)(2,1)} %all-to-all-done.1.refs_0_.refs_2_, bf16[64,40,1152]{2,1,0:T(8,128)(2,1)} %all-to-all-done.refs_0_.refs_1_.refs_2_.refs_3_, ...), custom_call_target="tpu_custom_call" | custom-call | tf_op jit(solution)/shard_map/gate_up/pallas_call | solution.py:150
  305.7 0.0 collective-permute-start.6
  305.7 2.2 collective-permute-done.6.got_ref
  307.9 1.1 copy-done.1
  309.0 6.3 %down.3 = bf16[64,8,2304]{2,1,0:T(8,128)(2,1)} custom-call(s32[2]{0:T(128)S(1)} %pad_add_fusion.place_ref, bf16[256,1152]{1,0:T(8,128)(2,1)S(1)} %copy-done.1, bf16[256,1152]{1,0:T(8,128)(2,1)S(1)} %collective-permute-done.6.got_ref, bf16[2,288,4608]{2,1,0:T(8,128)(2,1)} %refs_1_.3, bf16[2,288,4608]{2,1,0:T(8,128)(2,1)} %refs_1_.3, ...), custom_call_target="tpu_custom_call" | custom-call | tf_op jit(solution)/shard_map/down/pallas_call | solution.py:225
  315.3 5.5 %all-to-all-start.4 = ((bf16[64,8,2304]{2,1,0:T(8,128)(2,1)}), bf16[64,8,2304]{2,1,0:T(8,128)(2,1)S(1)}, u32[]{:S(2)}, u32[]{:S(2)}) async-start(bf16[64,8,2304]{2,1,0:T(8,128)(2,1)} %down.3), calls=%async_computation.4 | async-start | bytes 4718592 | tf_op jit(solution)/shard_map/all_to_all | solution.py:246
  320.8 31.8 %all-to-all-done.4 = bf16[64,8,2304]{2,1,0:T(8,128)(2,1)S(1)} async-done(((bf16[64,8,2304]{2,1,0:T(8,128)(2,1)}), bf16[64,8,2304]{2,1,0:T(8,128)(2,1)S(1)}, u32[]{:S(2)}, u32[]{:S(2)}) %all-to-all-start.4) | async-done | bytes 2359328 | tf_op jit(solution)/shard_map/all_to_all | solution.py:246
  352.7 0.3 convert_reduce_fusion
  353.0 0.1 multiply_reduce_fusion
  353.2 0.1 reduce_sum.76
  353.3 0.1 fusion.8
  353.4 0.8 collective-permute-start.7
  354.2 3.1 collective-permute-done.7
  357.3 0.6 select_n.133
  (29 shorter events, 0.5 us)
Async XLA Ops:
  6.5 21.6 %collective-permute-start.1 = (bf16[2,288,4608]{2,1,0:T(8,128)(2,1)}, bf16[2,288,4608]{2,1,0:T(8,128)(2,1)}, u32[]{:S(2)}, u32[]{:S(2)}) collective-permute-start(bf16[2,288,4608]{2,1,0:T(8,128)(2,1)} %refs_1_.3), channel_id=1, source_target_pairs={{0,1},{1,0},{2,3},{3,2},{4,5},{5,4},{6,7},{7,6},{8,9},{9,8},{10,11... | collective-permute-start | bytes 15925256 | tf_op jit(solution)/shard_map/ppermute | solution.py:284
  7.4 3.9 %collective-permute-start = (bf16[4,2304]{1,0:T(4,128)(2,1)S(1)}, bf16[4,2304]{1,0:T(4,128)(2,1)S(1)}, u32[]{:S(2)}, u32[]{:S(2)}) collective-permute-start(bf16[4,2304]{1,0:T(4,128)(2,1)S(1)} %get-tuple-element.40), channel_id=1, source_target_pairs={{0,64},{64,0},{1,65},{65,1},{2,66},{66,2},{3,67},{67,3},{4,68},{68... | collective-permute-start | bytes 55304 | tf_op jit(solution)/shard_map/ppermute | solution.py:252
  10.3 4.0 %collective-permute-start.2 = (f32[4,2304]{1,0:T(4,128)S(1)}, f32[4,2304]{1,0:T(4,128)S(1)}, u32[]{:S(2)}, u32[]{:S(2)}) collective-permute-start(f32[4,2304]{1,0:T(4,128)S(1)} %get-tuple-element.43), channel_id=1, source_target_pairs={{0,64},{64,0},{1,65},{65,1},{2,66},{66,2},{3,67},{67,3},{4,68},{68... | collective-permute-start | bytes 110600 | tf_op jit(solution)/shard_map/ppermute | solution.py:252
  15.6 11.8 %collective-permute-start.3 = (bf16[4,2304]{1,0:T(4,128)(2,1)S(1)}, bf16[4,2304]{1,0:T(4,128)(2,1)S(1)}, u32[]{:S(2)}, u32[]{:S(2)}) collective-permute-start(bf16[4,2304]{1,0:T(4,128)(2,1)S(1)} %get-tuple-element.39), channel_id=1, source_target_pairs={{0,1},{1,0},{2,3},{3,2},{4,5},{5,4},{6,7},{7,6},{8,9},{9,8},{10,11... | collective-permute-start | bytes 55304 | tf_op jit(solution)/shard_map/ppermute | solution.py:252
  28.1 92.3 %all-to-all-start = ((bf16[64,40,1152]{2,1,0:T(8,128)(2,1)}), bf16[64,40,1152]{2,1,0:T(8,128)(2,1)}, u32[]{:S(2)}, u32[]{:S(2)}) async-start(bf16[64,40,1152]{2,1,0:T(8,128)(2,1)} %get-tuple-element.18), calls=%async_computation | async-start | bytes 11796480 | tf_op jit(solution)/shard_map/all_to_all | solution.py:246
  39.3 153.4 %all-gather.2.cloned.1.call-start = ((), (), s32[]{:S(2)}) async-start(), calls=%async_computation.5 | async-start | bytes 2396160 | tf_op jit(solution)/shard_map/all_gather | solution.py:290
  120.4 90.4 %all-to-all-start.1 = ((bf16[64,32,1152]{2,1,0:T(8,128)(2,1)}), bf16[64,32,1152]{2,1,0:T(8,128)(2,1)}, u32[]{:S(2)}, u32[]{:S(2)}) async-start(bf16[64,32,1152]{2,1,0:T(8,128)(2,1)} %get-tuple-element.22), calls=%async_computation.1 | async-start | bytes 9437184 | tf_op jit(solution)/shard_map/all_to_all | solution.py:246
  201.2 2.2 collective-permute-start.4
  203.4 1.1 copy-start
  210.8 42.2 %all-to-all-start.2 = ((bf16[64,8,2304]{2,1,0:T(8,128)(2,1)}), bf16[64,8,2304]{2,1,0:T(8,128)(2,1)S(1)}, u32[]{:S(2)}, u32[]{:S(2)}) async-start(bf16[64,8,2304]{2,1,0:T(8,128)(2,1)} %down.2), calls=%async_computation.2 | async-start | bytes 4718592 | tf_op jit(solution)/shard_map/all_to_all | solution.py:246
  255.5 1.4 collective-permute-start.5
  305.7 2.2 collective-permute-start.6
  307.9 1.1 copy-start.1
  315.3 37.3 %all-to-all-start.4 = ((bf16[64,8,2304]{2,1,0:T(8,128)(2,1)}), bf16[64,8,2304]{2,1,0:T(8,128)(2,1)S(1)}, u32[]{:S(2)}, u32[]{:S(2)}) async-start(bf16[64,8,2304]{2,1,0:T(8,128)(2,1)} %down.3), calls=%async_computation.4 | async-start | bytes 4718592 | tf_op jit(solution)/shard_map/all_to_all | solution.py:246
  353.4 3.8 %collective-permute-start.7 = (bf16[4,2304]{1,0:T(4,128)(2,1)S(1)}, bf16[4,2304]{1,0:T(4,128)(2,1)S(1)}, u32[]{:S(2)}, u32[]{:S(2)}) collective-permute-start(bf16[4,2304]{1,0:T(4,128)(2,1)S(1)} %get-tuple-element.35), channel_id=1, source_target_pairs={{0,64},{64,0},{1,65},{65,1},{2,66},{66,2},{3,67},{67,3},{4,68},{68... | collective-permute-start | bytes 55304 | tf_op jit(solution)/shard_map/ppermute | solution.py:252
Sparse Core Ops, SparseCore 0:
  42.9 149.8 all-gather.1

commit v5 on v4

--- a/solution.py
+++ b/solution.py
@@ -281,13 +281,14 @@
     gains = jnp.concatenate((pre_gain, post_gain), axis=0)
     gains = 1.0 + swapped(jnp.stack((gains, gains)), "row")
 
-    other_down = lax.ppermute(down_weight, "core", SWAP)
     first, later = packed(gate_weight, up_weight, chips)
     values = current.astype(jnp.float32)
     normed = (values * scale_of(values) * gains[:, 0][:, None]).astype(jnp.bfloat16)
     cut = swapped(slabs(normed, chips, cores), "core").reshape(cores * count, -1)
-    first, other_down, cut = lax.optimization_barrier((first, other_down, cut))
-    everything = lax.all_gather(cut, ORDER, axis=0, tiled=True)
+    cut, leaving = lax.optimization_barrier((cut, down_weight))
+    other_down = lax.ppermute(leaving, "core", SWAP)
+    everything = exchanged(copies_of(cut, ORDER), ORDER).reshape(-1, cut.shape[1])
+    first, other_down, everything = lax.optimization_barrier((first, other_down, everything))
     first = exchanged(first, CHIP)
     later = exchanged(later, CHIP)
 

time: 366 us -> 342 us (0.934)
  waiting for transfers between devices: 217 us -> 136 us
  blocking collectives: 40 us -> 115 us
  between operations: 13.7 us -> 0.3 us
  starting transfers between devices: 42.3 us -> 35.8 us
    all_to_all x1 -> x2, blocking collectives: 40 us -> 115 us  [exchanged(): return lax.all_to_all(blocks, axes, split_axis=0, concat_axis=0, tiled=True)]
    all_gather x1 -> x0, waiting for transfers between devices: 60.4 us -> none  [on_device(): everything = lax.all_gather(cut, ORDER, axis=0, tiled=True)]
    all_to_all x4, waiting for transfers between devices: 144 us -> 123 us  [exchanged(): return lax.all_to_all(blocks, axes, split_axis=0, concat_axis=0, tiled=True)]
    all_to_all x4, starting transfers between devices: 39 us -> 32.4 us  [exchanged(): return lax.all_to_all(blocks, axes, split_axis=0, concat_axis=0, tiled=True)]
  transfers between devices with their start and end apart: 13 -> 12, of which waited for: 10 -> 11; matrix products, arithmetic and copies ran while one was open for 1% -> 1% of each run, Pallas kernels for 7% -> 8%
where the time goes in v5:
time: 342 us; the launch traced here: 340 us
  waiting for transfers between devices  136 us (40%)
  blocking collectives  115 us (34%)
  Pallas kernels  41.4 us (12%)
  starting transfers between devices  35.8 us (10%)
  local copies, waits for them, and re-layouts  7.45 us (2%)
  other arithmetic  4.04 us (1%)
    all_to_all x4, waiting for transfers between devices, exchanged(): return lax.all_to_all(blocks, axes, split_axis=0, concat_axis=0, tiled=True)  123 us
    all_to_all x2, blocking collectives, exchanged(): return lax.all_to_all(blocks, axes, split_axis=0, concat_axis=0, tiled=True)  115 us
    all_to_all x4, starting transfers between devices, exchanged(): return lax.all_to_all(blocks, axes, split_axis=0, concat_axis=0, tiled=True)  32.4 us
    pallas_call x2, Pallas kernels, gate_up(): pl.pallas_call(functools.partial(gate_up_kernel, layer), grid=(width // s...  17.1 us
    pallas_call x2, Pallas kernels, down(): pl.pallas_call(down_kernel, grid=(steps,), in_specs=[pl.BlockSpec(memory_...  12.7 us
    pallas_call x1, Pallas kernels, packed(): pl.pallas_call(pack_kernel, grid=(chips // 2 // pairs,), in_specs=[taken,...  11.7 us
    ppermute x5, waiting for transfers between devices, swapped(): got = lax.ppermute(jnp.where(index == 0, blocks[1], blocks[0]), axis, SWAP)  8.81 us
  transfers between devices with their start and end apart: 12, of which 11 were waited for; matrix products, arithmetic and copies ran while one was open for 1% of the time, Pallas kernels for 8%

profile of v5, /device:TPU:0, one launch (start us, length us, event | category | flops | bytes accessed | tf_op | source)
XLA Modules:
  0.0 340.4 jit_solution(14017807053438633115)
XLA Ops:
  0.0 0.9 broadcast_select_fusion.3
  0.9 2.1 collective-permute-start
  3.0 0.8 fusion.10
  3.7 0.1 collective-permute-start.1
  3.8 0.2 stack.88
  4.0 0.7 collective-permute-done
  4.7 0.2 fusion.5
  4.9 0.2 stack.89
  5.1 2.7 collective-permute-done.1
  7.8 0.2 slice_reduce_fusion.2
  8.0 0.1 mul.117
  8.1 0.3 fusion.4
  8.4 0.2 slice.76
  8.7 0.2 reshape.140
  8.9 0.2 reshape.139
  9.1 0.1 collective-permute-start.2
  9.2 1.2 collective-permute-done.2
  10.4 0.2 collective-permute-start.3
  10.7 1.6 broadcast_in_dim.4
  12.2 11.0 %all-to-all-start = ((bf16[64,8,2304]{2,1,0:T(8,128)(2,1)}), bf16[64,8,2304]{2,1,0:T(8,128)(2,1)S(1)}, u32[]{:S(2)}, u32[]{:S(2)}) async-start(bf16[64,8,2304]{2,1,0:T(8,128)(2,1)} %broadcast_in_dim.4), calls=%async_computation | async-start | bytes 4718592 | tf_op jit(solution)/shard_map/all_to_all | solution.py:246
  23.2 11.7 %pack.1 = (bf16[64,40,1152]{2,1,0:T(8,128)(2,1)}, bf16[64,32,1152]{2,1,0:T(8,128)(2,1)}) custom-call(bf16[36,2,36864]{2,1,0:T(2,128)(2,1)} %bitcast.42, bf16[36,2,36864]{2,1,0:T(2,128)(2,1)} %bitcast.43), custom_call_target="tpu_custom_call" | custom-call | tf_op jit(solution)/shard_map/pack/pallas_call | solution.py:57
  34.9 22.0 %all-to-all-done = bf16[64,8,2304]{2,1,0:T(8,128)(2,1)S(1)} async-done(((bf16[64,8,2304]{2,1,0:T(8,128)(2,1)}), bf16[64,8,2304]{2,1,0:T(8,128)(2,1)S(1)}, u32[]{:S(2)}, u32[]{:S(2)}) %all-to-all-start) | async-done | bytes 2359328 | tf_op jit(solution)/shard_map/all_to_all | solution.py:246
  56.9 0.0 collective-permute-done.3.refs_2_.refs_3_
  56.9 75.5 %all_to_all.30.refs_0_.refs_1_.refs_2_.refs_3_ = bf16[64,40,1152]{2,1,0:T(8,128)(2,1)} all-to-all(bf16[64,40,1152]{2,1,0:T(8,128)(2,1)} %get-tuple-element.22), channel_id=1, replica_groups=mesh['row'=2,'col_0'=4,'col_1'=4,'col_2'=2,'core'=2] {'row','col_0','col..., dimensions={0} | all-to-all | bytes 11796480 | tf_op jit(solution)/shard_map/all_to_all | solution.py:246
  132.4 0.0 copy-done.2
  132.4 5.8 %all-to-all-start.2 = ((bf16[64,32,1152]{2,1,0:T(8,128)(2,1)}), bf16[64,32,1152]{2,1,0:T(8,128)(2,1)}, u32[]{:S(2)}, u32[]{:S(2)}) async-start(bf16[64,32,1152]{2,1,0:T(8,128)(2,1)} %get-tuple-element.26), calls=%async_computation.2 | async-start | bytes 9437184 | tf_op jit(solution)/shard_map/all_to_all | solution.py:246
  138.2 8.6 %gate_up.2 = (bf16[256,1152]{1,0:T(8,128)(2,1)}, bf16[256,1152]{1,0:T(8,128)(2,1)}) custom-call(s32[1]{0:T(128)} %bitcast.2.core_ref, bf16[512,2304]{1,0:T(8,128)(2,1)} %bitcast.41, bf16[64,40,1152]{2,1,0:T(8,128)(2,1)} %all_to_all.30.refs_0_.refs_1_.refs_2_.refs_3_, bf16[64,40,1152]{2,1,0:T(8,128)(2,1)} %all_to_all.30.refs_0_.refs_1_.refs_2_.refs_3_, ...), custom_call_target="tpu_custom_call" | custom-call | tf_op jit(solution)/shard_map/gate_up/pallas_call | solution.py:150
  146.8 0.0 collective-permute-start.4
  146.8 0.1 pad_add_fusion.place_ref
  146.8 2.1 collective-permute-done.4.got_ref
  149.0 1.1 copy-done
  150.0 6.3 %down.2 = bf16[64,8,2304]{2,1,0:T(8,128)(2,1)} custom-call(s32[2]{0:T(128)S(1)} %pad_add_fusion.place_ref, bf16[256,1152]{1,0:T(8,128)(2,1)S(1)} %copy-done, bf16[256,1152]{1,0:T(8,128)(2,1)S(1)} %collective-permute-done.4.got_ref, bf16[2,288,4608]{2,1,0:T(8,128)(2,1)} %refs_1_.3, bf16[2,288,4608]{2,1,0:T(8,128)(2,1)} %refs_1_.3, ...), custom_call_target="tpu_custom_call" | custom-call | tf_op jit(solution)/shard_map/down/pallas_call | solution.py:225
  156.4 38.4 %all-to-all-done.2.refs_0_.refs_2_ = bf16[64,32,1152]{2,1,0:T(8,128)(2,1)} async-done(((bf16[64,32,1152]{2,1,0:T(8,128)(2,1)}), bf16[64,32,1152]{2,1,0:T(8,128)(2,1)}, u32[]{:S(2)}, u32[]{:S(2)}) %all-to-all-start.2) | async-done | bytes 4718624 | tf_op jit(solution)/shard_map/all_to_all | solution.py:246
  194.8 10.1 %all-to-all-start.3 = ((bf16[64,8,2304]{2,1,0:T(8,128)(2,1)}), bf16[64,8,2304]{2,1,0:T(8,128)(2,1)S(1)}, u32[]{:S(2)}, u32[]{:S(2)}) async-start(bf16[64,8,2304]{2,1,0:T(8,128)(2,1)} %down.2), calls=%async_computation.3 | async-start | bytes 4718592 | tf_op jit(solution)/shard_map/all_to_all | solution.py:246
  204.9 0.1 mul.128
  205.1 0.1 mul.134
  205.3 30.8 %all-to-all-done.3 = bf16[64,8,2304]{2,1,0:T(8,128)(2,1)S(1)} async-done(((bf16[64,8,2304]{2,1,0:T(8,128)(2,1)}), bf16[64,8,2304]{2,1,0:T(8,128)(2,1)S(1)}, u32[]{:S(2)}, u32[]{:S(2)}) %all-to-all-start.3) | async-done | bytes 2359328 | tf_op jit(solution)/shard_map/all_to_all | solution.py:246
  236.1 0.3 convert_reduce_fusion.1
  236.4 0.4 reshape.143
  236.9 0.1 multiply_reduce_fusion.1
  237.0 0.1 reduce_sum.71
  237.1 0.2 fusion.7
  237.3 0.4 fusion.3
  237.7 0.2 slice.82
  238.0 0.2 reshape.145
  238.2 0.2 reshape.144
  238.4 0.1 collective-permute-start.5
  238.5 1.2 collective-permute-done.5
  239.8 0.2 broadcast_in_dim.5
  239.9 39.6 %all_to_all.31 = bf16[64,8,2304]{2,1,0:T(8,128)(2,1)} all-to-all(bf16[64,8,2304]{2,1,0:T(8,128)(2,1)S(1)} %broadcast_in_dim.5), channel_id=1, replica_groups=mesh['row'=2,'col_0'=4,'col_1'=4,'col_2'=2,'core'=2] {'col_2','row','col..., dimensions={0} | all-to-all | bytes 4718592 | tf_op jit(solution)/shard_map/all_to_all | solution.py:246
  279.6 8.6 %gate_up.3 = (bf16[256,1152]{1,0:T(8,128)(2,1)}, bf16[256,1152]{1,0:T(8,128)(2,1)}) custom-call(s32[1]{0:T(128)} %bitcast.2.core_ref, bf16[512,2304]{1,0:T(8,128)(2,1)} %bitcast.40, bf16[64,32,1152]{2,1,0:T(8,128)(2,1)} %all-to-all-done.2.refs_0_.refs_2_, bf16[64,40,1152]{2,1,0:T(8,128)(2,1)} %all_to_all.30.refs_0_.refs_1_.refs_2_.refs_3_, ...), custom_call_target="tpu_custom_call" | custom-call | tf_op jit(solution)/shard_map/gate_up/pallas_call | solution.py:150
  288.1 0.0 collective-permute-start.6
  288.1 2.2 collective-permute-done.6.got_ref
  290.4 1.1 copy-done.1
  291.4 6.3 %down.3 = bf16[64,8,2304]{2,1,0:T(8,128)(2,1)} custom-call(s32[2]{0:T(128)S(1)} %pad_add_fusion.place_ref, bf16[256,1152]{1,0:T(8,128)(2,1)S(1)} %copy-done.1, bf16[256,1152]{1,0:T(8,128)(2,1)S(1)} %collective-permute-done.6.got_ref, bf16[2,288,4608]{2,1,0:T(8,128)(2,1)} %refs_1_.3, bf16[2,288,4608]{2,1,0:T(8,128)(2,1)} %refs_1_.3, ...), custom_call_target="tpu_custom_call" | custom-call | tf_op jit(solution)/shard_map/down/pallas_call | solution.py:225
  297.8 5.5 %all-to-all-start.5 = ((bf16[64,8,2304]{2,1,0:T(8,128)(2,1)}), bf16[64,8,2304]{2,1,0:T(8,128)(2,1)S(1)}, u32[]{:S(2)}, u32[]{:S(2)}) async-start(bf16[64,8,2304]{2,1,0:T(8,128)(2,1)} %down.3), calls=%async_computation.5 | async-start | bytes 4718592 | tf_op jit(solution)/shard_map/all_to_all | solution.py:246
  303.3 31.8 %all-to-all-done.5 = bf16[64,8,2304]{2,1,0:T(8,128)(2,1)S(1)} async-done(((bf16[64,8,2304]{2,1,0:T(8,128)(2,1)}), bf16[64,8,2304]{2,1,0:T(8,128)(2,1)S(1)}, u32[]{:S(2)}, u32[]{:S(2)}) %all-to-all-start.5) | async-done | bytes 2359328 | tf_op jit(solution)/shard_map/all_to_all | solution.py:246
  335.1 0.3 convert_reduce_fusion
  335.5 0.1 multiply_reduce_fusion
  335.6 0.1 reduce_sum.76
  335.7 0.1 fusion.8
  335.9 0.8 collective-permute-start.7
  336.6 3.1 collective-permute-done.7
  339.7 0.6 select_n.133
  (30 shorter events, 0.5 us)
Async XLA Ops:
  0.9 3.8 %collective-permute-start = (bf16[4,2304]{1,0:T(4,128)(2,1)S(1)}, bf16[4,2304]{1,0:T(4,128)(2,1)S(1)}, u32[]{:S(2)}, u32[]{:S(2)}) collective-permute-start(bf16[4,2304]{1,0:T(4,128)(2,1)S(1)} %get-tuple-element.44), channel_id=1, source_target_pairs={{0,64},{64,0},{1,65},{65,1},{2,66},{66,2},{3,67},{67,3},{4,68},{68... | collective-permute-start | bytes 55304 | tf_op jit(solution)/shard_map/ppermute | solution.py:252
  3.7 4.0 %collective-permute-start.1 = (f32[4,2304]{1,0:T(4,128)S(1)}, f32[4,2304]{1,0:T(4,128)S(1)}, u32[]{:S(2)}, u32[]{:S(2)}) collective-permute-start(f32[4,2304]{1,0:T(4,128)S(1)} %get-tuple-element.47), channel_id=1, source_target_pairs={{0,64},{64,0},{1,65},{65,1},{2,66},{66,2},{3,67},{67,3},{4,68},{68... | collective-permute-start | bytes 110600 | tf_op jit(solution)/shard_map/ppermute | solution.py:252
  9.1 1.3 collective-permute-start.2
  10.4 46.4 %collective-permute-start.3 = (bf16[2,288,4608]{2,1,0:T(8,128)(2,1)}, bf16[2,288,4608]{2,1,0:T(8,128)(2,1)}, u32[]{:S(2)}, u32[]{:S(2)}) collective-permute-start(bf16[2,288,4608]{2,1,0:T(8,128)(2,1)} %refs_1_.3), channel_id=1, source_target_pairs={{0,1},{1,0},{2,3},{3,2},{4,5},{5,4},{6,7},{7,6},{8,9},{9,8},{10,11... | collective-permute-start | bytes 15925256 | tf_op jit(solution)/shard_map/ppermute | solution.py:289
  12.2 44.6 %all-to-all-start = ((bf16[64,8,2304]{2,1,0:T(8,128)(2,1)}), bf16[64,8,2304]{2,1,0:T(8,128)(2,1)S(1)}, u32[]{:S(2)}, u32[]{:S(2)}) async-start(bf16[64,8,2304]{2,1,0:T(8,128)(2,1)} %broadcast_in_dim.4), calls=%async_computation | async-start | bytes 4718592 | tf_op jit(solution)/shard_map/all_to_all | solution.py:246
  56.9 75.5 %copy-start.2 = (bf16[64,8,2304]{2,1,0:T(8,128)(2,1)}, bf16[64,8,2304]{2,1,0:T(8,128)(2,1)S(1)}, u32[]{:S(2)}) copy-start(bf16[64,8,2304]{2,1,0:T(8,128)(2,1)S(1)} %all-to-all-done) | copy-start | bytes 7077892
  132.4 62.4 %all-to-all-start.2 = ((bf16[64,32,1152]{2,1,0:T(8,128)(2,1)}), bf16[64,32,1152]{2,1,0:T(8,128)(2,1)}, u32[]{:S(2)}, u32[]{:S(2)}) async-start(bf16[64,32,1152]{2,1,0:T(8,128)(2,1)} %get-tuple-element.26), calls=%async_computation.2 | async-start | bytes 9437184 | tf_op jit(solution)/shard_map/all_to_all | solution.py:246
  146.8 2.2 collective-permute-start.4
  149.0 1.1 copy-start
  194.8 41.3 %all-to-all-start.3 = ((bf16[64,8,2304]{2,1,0:T(8,128)(2,1)}), bf16[64,8,2304]{2,1,0:T(8,128)(2,1)S(1)}, u32[]{:S(2)}, u32[]{:S(2)}) async-start(bf16[64,8,2304]{2,1,0:T(8,128)(2,1)} %down.2), calls=%async_computation.3 | async-start | bytes 4718592 | tf_op jit(solution)/shard_map/all_to_all | solution.py:246
  238.4 1.3 collective-permute-start.5
  288.1 2.2 collective-permute-start.6
  290.4 1.1 copy-start.1
  297.8 37.3 %all-to-all-start.5 = ((bf16[64,8,2304]{2,1,0:T(8,128)(2,1)}), bf16[64,8,2304]{2,1,0:T(8,128)(2,1)S(1)}, u32[]{:S(2)}, u32[]{:S(2)}) async-start(bf16[64,8,2304]{2,1,0:T(8,128)(2,1)} %down.3), calls=%async_computation.5 | async-start | bytes 4718592 | tf_op jit(solution)/shard_map/all_to_all | solution.py:246
  335.9 3.8 %collective-permute-start.7 = (bf16[4,2304]{1,0:T(4,128)(2,1)S(1)}, bf16[4,2304]{1,0:T(4,128)(2,1)S(1)}, u32[]{:S(2)}, u32[]{:S(2)}) collective-permute-start(bf16[4,2304]{1,0:T(4,128)(2,1)S(1)} %get-tuple-element.39), channel_id=1, source_target_pairs={{0,64},{64,0},{1,65},{65,1},{2,66},{66,2},{3,67},{67,3},{4,68},{68... | collective-permute-start | bytes 55304 | tf_op jit(solution)/shard_map/ppermute | solution.py:252

commit v6 on v5

--- a/solution.py
+++ b/solution.py
@@ -166,6 +166,38 @@
     )(core.reshape(1), normed, weights, rests, weights, rests)
 
 
+def part_kernel(core_ref, whole_ref, own_ref, other_ref):
+    chips = whole_ref.shape[0] // 8
+    width = whole_ref.shape[1]
+    part = whole_ref[...].astype(jnp.float32).reshape(chips, 8, width)
+    first, second = turned(part[: chips // 2], part[chips // 2 :])
+    first = first.reshape(-1, width).astype(own_ref.dtype)
+    second = second.reshape(-1, width).astype(own_ref.dtype)
+
+    @pl.when(core_ref[0] == 0)
+    def _():
+        own_ref[...] = first
+        other_ref[...] = second
+
+    @pl.when(core_ref[0] != 0)
+    def _():
+        own_ref[...] = second
+        other_ref[...] = first
+
+
+def parted(whole, core, cores):
+    tokens, width = whole.shape
+    own = tokens // cores
+    return pl.pallas_call(
+        part_kernel,
+        in_specs=[pl.BlockSpec(memory_space=pltpu.SMEM), pl.BlockSpec(memory_space=pltpu.VMEM)],
+        out_specs=[pl.BlockSpec(memory_space=pltpu.VMEM)] * 2,
+        out_shape=[jax.ShapeDtypeStruct((own, width), jnp.bfloat16)] * 2,
+        compiler_params=pltpu.CompilerParams(vmem_limit_bytes=20 * 2**20),
+        name="parted",
+    )(core.reshape(1), whole)
+
+
 def down_kernel(place_ref, mine_ref, got_ref, *refs):
     own_low_ref, own_high_ref, other_low_ref, other_high_ref, out_ref = refs[:5]
     hidden_ref, turned_ref, weight_ref = refs[5:]
@@ -298,12 +330,18 @@
             normed = (values * scale_of(values) * gains[:, layer][:, None]).astype(jnp.bfloat16)
             cut = swapped(slabs(normed, chips, cores), "core").reshape(cores * count, -1)
             everything = exchanged(copies_of(cut, ORDER), ORDER).reshape(-1, cut.shape[1])
-        weights = first if layer == 0 else later
-        mine, theirs = gate_up(everything, weights, first, layer, core, cores)
+        if layer == 0:
+            mine, theirs = gate_up(everything, first, first, layer, core, cores)
+        else:
+            whole = jnp.dot(everything, joined, preferred_element_type=jnp.float32)
+            mine, theirs = parted(whole.astype(jnp.bfloat16), core, cores)
         got = lax.ppermute(theirs, "core", SWAP)
         sent = down(mine, got, down_weight, other_down, layer, place, chips)
         if layer == 0:
             sent, later = lax.optimization_barrier((sent, later))
+            rest = (first.shape[1] - later.shape[1]) // layers
+            tails = first[:, first.shape[1] - rest :].reshape(-1, first.shape[2])
+            joined = jnp.concatenate((later.reshape(-1, later.shape[2]), tails), axis=0)
         arrived = exchanged(sent, CHIP)
         branch = jnp.sum(arrived.astype(jnp.float32), axis=0).reshape(values.shape)
         post = branch * scale_of(branch) * gains[:, layers + layer][:, None]

time: 342 us -> 341 us (level)
  blocking collectives: 115 us -> 75.5 us
  waiting for transfers between devices: 136 us -> 168 us
  Pallas kernels: 41.4 us -> 33.5 us
  starting transfers between devices: 35.8 us -> 42.7 us
  matrix products: 0 us -> 5.57 us
    all_to_all x2 -> x1, blocking collectives: 115 us -> 75.5 us  [exchanged(): return lax.all_to_all(blocks, axes, split_axis=0, concat_axis=0, tiled=True)]
    all_to_all x4 -> x5, waiting for transfers between devices: 123 us -> 155 us  [exchanged(): return lax.all_to_all(blocks, axes, split_axis=0, concat_axis=0, tiled=True)]
    pallas_call x2 -> x1, Pallas kernels: 17.1 us -> 8.55 us  [gate_up(): pl.pallas_call(functools.partial(gate_up_kernel, layer), grid=(width // s...]
    all_to_all x4 -> x5, starting transfers between devices: 32.4 us -> 39.3 us  [exchanged(): return lax.all_to_all(blocks, axes, split_axis=0, concat_axis=0, tiled=True)]
    dot_general x0 -> x1, matrix products: none -> 5.57 us  [on_device(): whole = jnp.dot(everything, joined, preferred_element_type=jnp.float32)]
  transfers between devices with their start and end apart: 12 -> 13, of which waited for: 11 -> 12; matrix products, arithmetic and copies ran while one was open for 1% -> 1% of each run, Pallas kernels for 8% -> 8%
where the time goes in v6:
time: 341 us; the launch traced here: 340 us
  waiting for transfers between devices  168 us (49%)
  blocking collectives  75.5 us (22%)
  starting transfers between devices  42.7 us (13%)
  Pallas kernels  33.5 us (10%)
  local copies, waits for them, and re-layouts  10 us (3%)
  matrix products  5.57 us (2%)
  other arithmetic  4.64 us (1%)
    all_to_all x5, waiting for transfers between devices, exchanged(): return lax.all_to_all(blocks, axes, split_axis=0, concat_axis=0, tiled=True)  155 us
    all_to_all x1, blocking collectives, exchanged(): return lax.all_to_all(blocks, axes, split_axis=0, concat_axis=0, tiled=True)  75.5 us
    all_to_all x5, starting transfers between devices, exchanged(): return lax.all_to_all(blocks, axes, split_axis=0, concat_axis=0, tiled=True)  39.3 us
    pallas_call x2, Pallas kernels, down(): pl.pallas_call(down_kernel, grid=(steps,), in_specs=[pl.BlockSpec(memory_...  12.7 us
    pallas_call x1, Pallas kernels, packed(): pl.pallas_call(pack_kernel, grid=(chips // 2 // pairs,), in_specs=[taken,...  11.7 us
    ppermute x5, waiting for transfers between devices, swapped(): got = lax.ppermute(jnp.where(index == 0, blocks[1], blocks[0]), axis, SWAP)  8.81 us
    pallas_call x1, Pallas kernels, gate_up(): pl.pallas_call(functools.partial(gate_up_kernel, layer), grid=(width // s...  8.55 us
  transfers between devices with their start and end apart: 13, of which 12 were waited for; matrix products, arithmetic and copies ran while one was open for 1% of the time, Pallas kernels for 8%

profile of v6, /device:TPU:0, one launch (start us, length us, event | category | flops | bytes accessed | tf_op | source)
XLA Modules:
  0.0 339.9 jit_solution(4476260949212842742)
XLA Ops:
  0.0 0.9 broadcast_select_fusion.3
  0.9 2.1 collective-permute-start
  3.0 0.8 fusion.19
  3.7 0.1 collective-permute-start.1
  3.8 0.2 stack.88
  4.0 0.7 collective-permute-done
  4.7 0.2 fusion.13
  4.9 0.2 stack.89
  5.1 2.7 collective-permute-done.1
  7.8 0.7 slice_reduce_fusion.2
  8.5 0.1 mul.117
  8.7 0.3 fusion.12
  8.9 0.2 slice.80
  9.2 0.2 reshape.146
  9.4 0.2 reshape.145
  9.6 0.1 collective-permute-start.2
  9.7 1.2 collective-permute-done.2
  10.9 0.2 collective-permute-start.3
  11.2 1.6 broadcast_in_dim.4
  12.8 11.0 %all-to-all-start = ((bf16[64,8,2304]{2,1,0:T(8,128)(2,1)}), bf16[64,8,2304]{2,1,0:T(8,128)(2,1)S(1)}, u32[]{:S(2)}, u32[]{:S(2)}) async-start(bf16[64,8,2304]{2,1,0:T(8,128)(2,1)} %broadcast_in_dim.4), calls=%async_computation | async-start | bytes 4718592 | tf_op jit(solution)/shard_map/all_to_all | solution.py:278
  23.7 11.7 %pack.1 = (bf16[64,40,1152]{2,1,0:T(8,128)(2,1)}, bf16[64,32,1152]{2,1,0:T(8,128)(2,1)}) custom-call(bf16[36,2,36864]{2,1,0:T(2,128)(2,1)} %bitcast.44, bf16[36,2,36864]{2,1,0:T(2,128)(2,1)} %bitcast.45), custom_call_target="tpu_custom_call" | custom-call | tf_op jit(solution)/shard_map/pack/pallas_call | solution.py:57
  35.4 22.0 %all-to-all-done = bf16[64,8,2304]{2,1,0:T(8,128)(2,1)S(1)} async-done(((bf16[64,8,2304]{2,1,0:T(8,128)(2,1)}), bf16[64,8,2304]{2,1,0:T(8,128)(2,1)S(1)}, u32[]{:S(2)}, u32[]{:S(2)}) %all-to-all-start) | async-done | bytes 2359328 | tf_op jit(solution)/shard_map/all_to_all | solution.py:278
  57.4 75.5 %all_to_all.30.refs_0_.refs_1_.refs_2_.refs_3_ = bf16[64,40,1152]{2,1,0:T(8,128)(2,1)} all-to-all(bf16[64,40,1152]{2,1,0:T(8,128)(2,1)} %get-tuple-element.22), channel_id=1, replica_groups=mesh['row'=2,'col_0'=4,'col_1'=4,'col_2'=2,'core'=2] {'row','col_0','col..., dimensions={0} | all-to-all | bytes 11796480 | tf_op jit(solution)/shard_map/all_to_all | solution.py:278
  132.9 5.8 %all-to-all-start.2 = ((bf16[64,32,1152]{2,1,0:T(8,128)(2,1)}), bf16[64,32,1152]{2,1,0:T(8,128)(2,1)}, u32[]{:S(2)}, u32[]{:S(2)}) async-start(bf16[64,32,1152]{2,1,0:T(8,128)(2,1)} %get-tuple-element.26), calls=%async_computation.2 | async-start | bytes 9437184 | tf_op jit(solution)/shard_map/all_to_all | solution.py:278
  138.7 8.6 %gate_up.1 = (bf16[256,1152]{1,0:T(8,128)(2,1)}, bf16[256,1152]{1,0:T(8,128)(2,1)}) custom-call(s32[1]{0:T(128)} %bitcast.2.core_ref, bf16[512,2304]{1,0:T(8,128)(2,1)} %bitcast.43, bf16[64,40,1152]{2,1,0:T(8,128)(2,1)} %all_to_all.30.refs_0_.refs_1_.refs_2_.refs_3_, bf16[64,40,1152]{2,1,0:T(8,128)(2,1)} %all_to_all.30.refs_0_.refs_1_.refs_2_.refs_3_, ...), custom_call_target="tpu_custom_call" | custom-call | tf_op jit(solution)/shard_map/gate_up/pallas_call | solution.py:150
  147.3 0.1 pad_add_fusion.place_ref
  147.3 2.1 collective-permute-done.4.got_ref
  149.5 1.1 copy-done
  150.5 6.3 %down.2 = bf16[64,8,2304]{2,1,0:T(8,128)(2,1)} custom-call(s32[2]{0:T(128)S(1)} %pad_add_fusion.place_ref, bf16[256,1152]{1,0:T(8,128)(2,1)S(1)} %copy-done, bf16[256,1152]{1,0:T(8,128)(2,1)S(1)} %collective-permute-done.4.got_ref, bf16[2,288,4608]{2,1,0:T(8,128)(2,1)} %refs_1_.3, bf16[2,288,4608]{2,1,0:T(8,128)(2,1)} %refs_1_.3, ...), custom_call_target="tpu_custom_call" | custom-call | tf_op jit(solution)/shard_map/down/pallas_call | solution.py:257
  156.9 38.4 %all-to-all-done.2 = bf16[64,32,1152]{2,1,0:T(8,128)(2,1)} async-done(((bf16[64,32,1152]{2,1,0:T(8,128)(2,1)}), bf16[64,32,1152]{2,1,0:T(8,128)(2,1)}, u32[]{:S(2)}, u32[]{:S(2)}) %all-to-all-start.2) | async-done | bytes 4718624 | tf_op jit(solution)/shard_map/all_to_all | solution.py:278
  195.3 10.1 %all-to-all-start.3 = ((bf16[64,8,2304]{2,1,0:T(8,128)(2,1)}), bf16[64,8,2304]{2,1,0:T(8,128)(2,1)S(1)}, u32[]{:S(2)}, u32[]{:S(2)}) async-start(bf16[64,8,2304]{2,1,0:T(8,128)(2,1)} %down.2), calls=%async_computation.3 | async-start | bytes 4718592 | tf_op jit(solution)/shard_map/all_to_all | solution.py:278
  205.5 0.1 mul.128
  205.6 0.1 mul.134
  205.8 30.8 %all-to-all-done.3 = bf16[64,8,2304]{2,1,0:T(8,128)(2,1)S(1)} async-done(((bf16[64,8,2304]{2,1,0:T(8,128)(2,1)}), bf16[64,8,2304]{2,1,0:T(8,128)(2,1)S(1)}, u32[]{:S(2)}, u32[]{:S(2)}) %all-to-all-start.3) | async-done | bytes 2359328 | tf_op jit(solution)/shard_map/all_to_all | solution.py:278
  236.6 0.3 convert_reduce_fusion.1
  236.9 0.4 reshape.149
  237.4 0.1 multiply_reduce_fusion.1
  237.5 0.1 reduce_sum.71
  237.6 0.8 fusion.15
  238.5 0.4 fusion.11
  238.9 0.2 slice.86
  239.1 0.2 reshape.151
  239.3 0.2 reshape.150
  239.6 0.1 collective-permute-start.5
  239.7 1.2 collective-permute-done.5
  240.9 1.6 broadcast_in_dim.5
  242.5 6.3 %all-to-all-start.4 = ((bf16[64,8,2304]{2,1,0:T(8,128)(2,1)}), bf16[64,8,2304]{2,1,0:T(8,128)(2,1)S(1)}, u32[]{:S(2)}, u32[]{:S(2)}) async-start(bf16[64,8,2304]{2,1,0:T(8,128)(2,1)} %broadcast_in_dim.5), calls=%async_computation.4 | async-start | bytes 4718592 | tf_op jit(solution)/shard_map/all_to_all | solution.py:278
  248.8 1.6 slice.89
  250.4 0.1 reshape.154
  250.5 31.6 %all-to-all-done.4 = bf16[64,8,2304]{2,1,0:T(8,128)(2,1)S(1)} async-done(((bf16[64,8,2304]{2,1,0:T(8,128)(2,1)}), bf16[64,8,2304]{2,1,0:T(8,128)(2,1)S(1)}, u32[]{:S(2)}, u32[]{:S(2)}) %all-to-all-start.4) | async-done | bytes 2359328 | tf_op jit(solution)/shard_map/all_to_all | solution.py:278
  282.2 5.6 %fusion.4.whole_ref = bf16[512,1152]{1,0:T(8,128)(2,1)S(1)} fusion(bf16[256,1152]{1,0:T(8,128)(2,1)S(1)} %reshape.154, bf16[2048,1152]{1,0:T(8,128)(2,1)} %bitcast.16, bf16[64,8,2304]{2,1,0:T(8,128)(2,1)S(1)} %all-to-all-done.4), kind=kOutput, calls=%fused_computation.6 | convolution fusion | flops 2729115648 | bytes 8847360 | tf_op jit(solution)/shard_map/dot_general | solution.py:336
  287.7 0.6 parted.1
  288.4 0.1 collective-permute-start.6
  288.5 2.0 collective-permute-done.6.got_ref
  290.5 6.3 %down.3 = bf16[64,8,2304]{2,1,0:T(8,128)(2,1)} custom-call(s32[2]{0:T(128)S(1)} %pad_add_fusion.place_ref, bf16[256,1152]{1,0:T(8,128)(2,1)S(1)} %get-tuple-element.29.mine_ref, bf16[256,1152]{1,0:T(8,128)(2,1)S(1)} %collective-permute-done.6.got_ref, bf16[2,288,4608]{2,1,0:T(8,128)(2,1)} %refs_1_.3, bf16[2,288,4608]{2,1,0:T(8,128)(2,1)} %refs_1_.3, ...), custom_call_target="tpu_custom_call" | custom-call | tf_op jit(solution)/shard_map/down/pallas_call | solution.py:257
  296.8 6.0 %all-to-all-start.5 = ((bf16[64,8,2304]{2,1,0:T(8,128)(2,1)}), bf16[64,8,2304]{2,1,0:T(8,128)(2,1)S(1)}, u32[]{:S(2)}, u32[]{:S(2)}) async-start(bf16[64,8,2304]{2,1,0:T(8,128)(2,1)} %down.3), calls=%async_computation.5 | async-start | bytes 4718592 | tf_op jit(solution)/shard_map/all_to_all | solution.py:278
  302.9 31.8 %all-to-all-done.5 = bf16[64,8,2304]{2,1,0:T(8,128)(2,1)S(1)} async-done(((bf16[64,8,2304]{2,1,0:T(8,128)(2,1)}), bf16[64,8,2304]{2,1,0:T(8,128)(2,1)S(1)}, u32[]{:S(2)}, u32[]{:S(2)}) %all-to-all-start.5) | async-done | bytes 2359328 | tf_op jit(solution)/shard_map/all_to_all | solution.py:278
  334.7 0.3 convert_reduce_fusion
  335.0 0.1 multiply_reduce_fusion
  335.2 0.1 reduce_sum.76
  335.3 0.1 fusion.16
  335.4 0.8 collective-permute-start.7
  336.2 3.1 collective-permute-done.7
  339.3 0.6 select_n.133
  (36 shorter events, 0.5 us)
Async XLA Ops:
  0.9 3.8 %collective-permute-start = (bf16[4,2304]{1,0:T(4,128)(2,1)S(1)}, bf16[4,2304]{1,0:T(4,128)(2,1)S(1)}, u32[]{:S(2)}, u32[]{:S(2)}) collective-permute-start(bf16[4,2304]{1,0:T(4,128)(2,1)S(1)} %get-tuple-element.44), channel_id=1, source_target_pairs={{0,64},{64,0},{1,65},{65,1},{2,66},{66,2},{3,67},{67,3},{4,68},{68... | collective-permute-start | bytes 55304 | tf_op jit(solution)/shard_map/ppermute | solution.py:284
  3.7 4.0 %collective-permute-start.1 = (f32[4,2304]{1,0:T(4,128)S(1)}, f32[4,2304]{1,0:T(4,128)S(1)}, u32[]{:S(2)}, u32[]{:S(2)}) collective-permute-start(f32[4,2304]{1,0:T(4,128)S(1)} %get-tuple-element.47), channel_id=1, source_target_pairs={{0,64},{64,0},{1,65},{65,1},{2,66},{66,2},{3,67},{67,3},{4,68},{68... | collective-permute-start | bytes 110600 | tf_op jit(solution)/shard_map/ppermute | solution.py:284
  9.6 1.3 collective-permute-start.2
  10.9 46.4 %collective-permute-start.3 = (bf16[2,288,4608]{2,1,0:T(8,128)(2,1)}, bf16[2,288,4608]{2,1,0:T(8,128)(2,1)}, u32[]{:S(2)}, u32[]{:S(2)}) collective-permute-start(bf16[2,288,4608]{2,1,0:T(8,128)(2,1)} %refs_1_.3), channel_id=1, source_target_pairs={{0,1},{1,0},{2,3},{3,2},{4,5},{5,4},{6,7},{7,6},{8,9},{9,8},{10,11... | collective-permute-start | bytes 15925256 | tf_op jit(solution)/shard_map/ppermute | solution.py:321
  12.8 44.6 %all-to-all-start = ((bf16[64,8,2304]{2,1,0:T(8,128)(2,1)}), bf16[64,8,2304]{2,1,0:T(8,128)(2,1)S(1)}, u32[]{:S(2)}, u32[]{:S(2)}) async-start(bf16[64,8,2304]{2,1,0:T(8,128)(2,1)} %broadcast_in_dim.4), calls=%async_computation | async-start | bytes 4718592 | tf_op jit(solution)/shard_map/all_to_all | solution.py:278
  57.4 75.5 %copy-start.1 = (bf16[64,8,2304]{2,1,0:T(8,128)(2,1)}, bf16[64,8,2304]{2,1,0:T(8,128)(2,1)S(1)}, u32[]{:S(2)}) copy-start(bf16[64,8,2304]{2,1,0:T(8,128)(2,1)S(1)} %all-to-all-done) | copy-start | bytes 7077892
  132.9 62.4 %all-to-all-start.2 = ((bf16[64,32,1152]{2,1,0:T(8,128)(2,1)}), bf16[64,32,1152]{2,1,0:T(8,128)(2,1)}, u32[]{:S(2)}, u32[]{:S(2)}) async-start(bf16[64,32,1152]{2,1,0:T(8,128)(2,1)} %get-tuple-element.26), calls=%async_computation.2 | async-start | bytes 9437184 | tf_op jit(solution)/shard_map/all_to_all | solution.py:278
  147.3 2.2 collective-permute-start.4
  149.5 1.1 copy-start
  195.3 41.3 %all-to-all-start.3 = ((bf16[64,8,2304]{2,1,0:T(8,128)(2,1)}), bf16[64,8,2304]{2,1,0:T(8,128)(2,1)S(1)}, u32[]{:S(2)}, u32[]{:S(2)}) async-start(bf16[64,8,2304]{2,1,0:T(8,128)(2,1)} %down.2), calls=%async_computation.3 | async-start | bytes 4718592 | tf_op jit(solution)/shard_map/all_to_all | solution.py:278
  239.6 1.3 collective-permute-start.5
  242.5 39.7 %all-to-all-start.4 = ((bf16[64,8,2304]{2,1,0:T(8,128)(2,1)}), bf16[64,8,2304]{2,1,0:T(8,128)(2,1)S(1)}, u32[]{:S(2)}, u32[]{:S(2)}) async-start(bf16[64,8,2304]{2,1,0:T(8,128)(2,1)} %broadcast_in_dim.5), calls=%async_computation.4 | async-start | bytes 4718592 | tf_op jit(solution)/shard_map/all_to_all | solution.py:278
  288.4 2.1 collective-permute-start.6
  296.8 6.0 %copy-start.3 = (f32[2,1,2304]{2,1,0:T(1,128)S(1)}, f32[2,1,2304]{2,1,0:T(1,128)}, u32[]{:S(2)}) copy-start(f32[2,1,2304]{2,1,0:T(1,128)} %get-tuple-element.36) | copy-start | bytes 55300
  296.8 38.5 %copy-start.2 = (bf16[2,4,2304]{2,1,0:T(4,128)(2,1)S(1)}, bf16[2,4,2304]{2,1,0:T(4,128)(2,1)}, u32[]{:S(2)}) copy-start(bf16[2,4,2304]{2,1,0:T(4,128)(2,1)} %get-tuple-element.35) | copy-start | bytes 110596
  296.8 37.8 %all-to-all-start.5 = ((bf16[64,8,2304]{2,1,0:T(8,128)(2,1)}), bf16[64,8,2304]{2,1,0:T(8,128)(2,1)S(1)}, u32[]{:S(2)}, u32[]{:S(2)}) async-start(bf16[64,8,2304]{2,1,0:T(8,128)(2,1)} %down.3), calls=%async_computation.5 | async-start | bytes 4718592 | tf_op jit(solution)/shard_map/all_to_all | solution.py:278
  335.4 3.8 %collective-permute-start.7 = (bf16[4,2304]{1,0:T(4,128)(2,1)S(1)}, bf16[4,2304]{1,0:T(4,128)(2,1)S(1)}, u32[]{:S(2)}, u32[]{:S(2)}) collective-permute-start(bf16[4,2304]{1,0:T(4,128)(2,1)S(1)} %get-tuple-element.39), channel_id=1, source_target_pairs={{0,64},{64,0},{1,65},{65,1},{2,66},{66,2},{3,67},{67,3},{4,68},{68... | collective-permute-start | bytes 55304 | tf_op jit(solution)/shard_map/ppermute | solution.py:284

commit v7 on v5

--- a/solution.py
+++ b/solution.py
@@ -47,19 +47,20 @@
                     first_ref[place, put, tail] = block[layer, whole:, extra : extra + odd]
 
 
-def packed(gate_weight, up_weight, chips):
+def packed(gate_weight, up_weight, chips, spare):
     layers, rows, hidden = gate_weight.shape
     width = hidden // chips * 2
     whole = rows // 8 * 8
     pairs = 4
     taken = pl.BlockSpec((rows, layers, pairs * width), lambda i: (0, 0, i))
     lengths = (whole + layers * (rows - whole), (layers - 1) * whole)
+    room = (lengths[0] + spare, lengths[1])
     return pl.pallas_call(
         pack_kernel,
         grid=(chips // 2 // pairs,),
         in_specs=[taken, taken],
         out_specs=[pl.BlockSpec((2 * pairs, n, width), lambda i: (i, 0, 0)) for n in lengths],
-        out_shape=[jax.ShapeDtypeStruct((chips, n, width), gate_weight.dtype) for n in lengths],
+        out_shape=[jax.ShapeDtypeStruct((chips, n, width), gate_weight.dtype) for n in room],
         compiler_params=pltpu.CompilerParams(vmem_limit_bytes=59 * 2**20),
         name="pack",
     )(jnp.swapaxes(gate_weight, 0, 1), jnp.swapaxes(up_weight, 0, 1))
@@ -71,6 +72,30 @@
 
 def one_hot(place, taken):
     return (place == taken).astype(jnp.float32).astype(jnp.bfloat16)
+
+
+def board_kernel(cut_ref, held_ref, out_ref):
+    del held_ref
+    out_ref[...] = jnp.broadcast_to(cut_ref[...][None], out_ref.shape)
+
+
+def boarded(held, cut):
+    chips, rows, width = held.shape
+    count, depth = cut.shape
+    parts = depth // width
+    return pl.pallas_call(
+        board_kernel,
+        grid=(parts,),
+        in_specs=[
+            pl.BlockSpec((count, width), lambda i: (0, i)),
+            pl.BlockSpec(memory_space=pl.ANY),
+        ],
+        out_specs=pl.BlockSpec((chips, count, width), lambda i: (0, rows // count - parts + i, 0)),
+        out_shape=jax.ShapeDtypeStruct(held.shape, held.dtype),
+        input_output_aliases={1: 0},
+        compiler_params=pltpu.CompilerParams(vmem_limit_bytes=59 * 2**20),
+        name="board",
+    )(cut, held)
 
 
 def turned(low, high):
@@ -80,12 +105,15 @@
     return jnp.where(low_first, low, high_turned), jnp.where(low_first, low_turned, high)
 
 
-def gate_up_kernel(layer, core_ref, normed_ref, *refs):
+def gate_up_kernel(layer, pieces, core_ref, *refs):
+    normed_refs, refs = refs[:pieces], refs[pieces:]
     weight_ref, rest_ref, weight_end_ref, rest_end_ref = refs[:4]
     own_ref, other_ref, spread_ref = refs[4:]
     chips, whole, _ = weight_ref.shape
     rest = rest_ref.shape[1]
-    narrow = normed_ref.shape[1] - chips * whole
+    lanes_each = normed_refs[0].shape[-1]
+    narrow = pieces * lanes_each - chips * whole
+    held = [ref[...].reshape(-1, lanes_each) for ref in normed_refs]
     step = pl.program_id(0)
 
     @pl.when(step == 0)
@@ -95,7 +123,7 @@
         put = lax.broadcasted_iota(jnp.int32, (narrow, chips * rest), 1)
         place = ((taken >> bits(part)) << bits(rest)) + layer * part + (taken & (part - 1))
         spread_ref[...] = jnp.dot(
-            normed_ref[:, chips * whole :],
+            held[-1][:, lanes_each - narrow :],
             one_hot(place, put),
             preferred_element_type=jnp.float32,
         ).astype(jnp.bfloat16)
@@ -103,17 +131,25 @@
     def product(main_ref, tail_ref, lanes):
         width = main_ref.shape[2]
         part = jnp.dot(
-            normed_ref[:, : chips * whole],
-            main_ref[...].reshape(chips * whole, width),
-            preferred_element_type=jnp.float32,
-        )
-        part += jnp.dot(
             spread_ref[...],
             tail_ref[...].reshape(chips * rest, width),
             preferred_element_type=jnp.float32,
         )
-        part = part.reshape(chips, -1, width)
-        first, second = turned(part[: chips // 2], part[chips // 2 :])
+        main = main_ref[...].reshape(chips * whole, width)
+        for piece in range(pieces):
+            start = piece * lanes_each
+            stop = min(start + lanes_each, chips * whole)
+            part += jnp.dot(
+                held[piece][:, : stop - start],
+                main[start:stop],
+                preferred_element_type=jnp.float32,
+            )
+        if pieces == 1:
+            part = part.reshape(chips, -1, width)
+            first, second = turned(part[: chips // 2], part[chips // 2 :])
+        else:
+            part = part.reshape(chips // 2, 2, -1, width)
+            first, second = turned(part[:, 0], part[:, 1])
         first = first.reshape(-1, width).astype(own_ref.dtype)
         second = second.reshape(-1, width).astype(own_ref.dtype)
 
@@ -137,9 +173,22 @@
 
 
 def gate_up(normed, weights, rests, layer, core, cores):
-    tokens, depth = normed.shape
     chips, _, width = weights.shape
     layers = 2
+    if normed is None:
+        count = 4 * cores
+        tokens, pieces = chips * count, 2
+        depth = pieces * width
+        base = rests.shape[1] // count - pieces
+        lhs = [rests] * pieces
+        lhs_specs = [
+            pl.BlockSpec((chips, count, width), lambda i, piece=piece: (0, base + piece, 0))
+            for piece in range(pieces)
+        ]
+    else:
+        tokens, depth = normed.shape
+        pieces, lhs = 1, [normed]
+        lhs_specs = [pl.BlockSpec((tokens, depth), lambda i: (0, 0))]
     rows = depth // chips
     whole = rows // 8 * 8
     rest = layers * (rows - whole)
@@ -148,11 +197,11 @@
     own = tokens // cores
     kept = pl.BlockSpec((own, width), lambda i: (0, 0))
     return pl.pallas_call(
-        functools.partial(gate_up_kernel, layer),
+        functools.partial(gate_up_kernel, layer, pieces),
         grid=(width // step,),
         in_specs=[
             pl.BlockSpec(memory_space=pltpu.SMEM),
-            pl.BlockSpec((tokens, depth), lambda i: (0, 0)),
+            *lhs_specs,
             pl.BlockSpec((chips, whole, step), lambda i: (0, 0, i)),
             pl.BlockSpec((chips, rest, step), lambda i: (0, whole // rest, i)),
             pl.BlockSpec((chips, whole, end), lambda i: (0, 0, width // end - 1)),
@@ -163,7 +212,7 @@
         scratch_shapes=[pltpu.VMEM((tokens, chips * rest), jnp.bfloat16)],
         compiler_params=pltpu.CompilerParams(vmem_limit_bytes=56 * 2**20),
         name="gate_up",
-    )(core.reshape(1), normed, weights, rests, weights, rests)
+    )(core.reshape(1), *lhs, weights, rests, weights, rests)
 
 
 def down_kernel(place_ref, mine_ref, got_ref, *refs):
@@ -281,14 +330,15 @@
     gains = jnp.concatenate((pre_gain, post_gain), axis=0)
     gains = 1.0 + swapped(jnp.stack((gains, gains)), "row")
 
-    first, later = packed(gate_weight, up_weight, chips)
+    spare = 4 * cores * 2
+    first, later = packed(gate_weight, up_weight, chips, spare)
     values = current.astype(jnp.float32)
     normed = (values * scale_of(values) * gains[:, 0][:, None]).astype(jnp.bfloat16)
     cut = swapped(slabs(normed, chips, cores), "core").reshape(cores * count, -1)
     cut, leaving = lax.optimization_barrier((cut, down_weight))
     other_down = lax.ppermute(leaving, "core", SWAP)
-    everything = exchanged(copies_of(cut, ORDER), ORDER).reshape(-1, cut.shape[1])
-    first, other_down, everything = lax.optimization_barrier((first, other_down, everything))
+    everything = None
+    first, other_down = lax.optimization_barrier((boarded(first, cut), other_down))
     first = exchanged(first, CHIP)
     later = exchanged(later, CHIP)
 

time: 342 us -> 342 us (level)
  blocking collectives: 115 us -> 146 us
  waiting for transfers between devices: 136 us -> 114 us
  starting transfers between devices: 35.8 us -> 25.4 us
    all_to_all x2, blocking collectives: 115 us -> 146 us  [exchanged(): return lax.all_to_all(blocks, axes, split_axis=0, concat_axis=0, tiled=True)]
    all_to_all x4 -> x3, waiting for transfers between devices: 123 us -> 101 us  [exchanged(): return lax.all_to_all(blocks, axes, split_axis=0, concat_axis=0, tiled=True)]
    all_to_all x4 -> x3, starting transfers between devices: 32.4 us -> 22.1 us  [exchanged(): return lax.all_to_all(blocks, axes, split_axis=0, concat_axis=0, tiled=True)]
    pallas_call x2 -> x3, Pallas kernels: 17.1 us -> 20.4 us  [the longest x2 18.2 us: gate_up(): pl.pallas_call(functools.partial(gate_up_kernel, layer, pieces), grid=(wi...]
  transfers between devices with their start and end apart: 12 -> 11, of which waited for: 11 -> 10; matrix products, arithmetic and copies ran while one was open for 1% -> 0% of each run, Pallas kernels for 8% -> 9%
where the time goes in v7:
time: 342 us; the launch traced here: 341 us
  blocking collectives  146 us (43%)
  waiting for transfers between devices  114 us (33%)
  Pallas kernels  44.8 us (13%)
  starting transfers between devices  25.4 us (7%)
  local copies, waits for them, and re-layouts  6.5 us (2%)
  other arithmetic  4.06 us (1%)
    all_to_all x2, blocking collectives, exchanged(): return lax.all_to_all(blocks, axes, split_axis=0, concat_axis=0, tiled=True)  146 us
    all_to_all x3, waiting for transfers between devices, exchanged(): return lax.all_to_all(blocks, axes, split_axis=0, concat_axis=0, tiled=True)  101 us
    all_to_all x3, starting transfers between devices, exchanged(): return lax.all_to_all(blocks, axes, split_axis=0, concat_axis=0, tiled=True)  22.1 us
    pallas_call x2, Pallas kernels, gate_up(): pl.pallas_call(functools.partial(gate_up_kernel, layer, pieces), grid=(wi...  18.2 us
    pallas_call x2, Pallas kernels, down(): pl.pallas_call(down_kernel, grid=(steps,), in_specs=[pl.BlockSpec(memory_...  12.7 us
    pallas_call x1, Pallas kernels, packed(): pl.pallas_call(pack_kernel, grid=(chips // 2 // pairs,), in_specs=[taken,...  11.7 us
    ppermute x5, waiting for transfers between devices, swapped(): got = lax.ppermute(jnp.where(index == 0, blocks[1], blocks[0]), axis, SWAP)  8.81 us
  transfers between devices with their start and end apart: 11, of which 10 were waited for; matrix products, arithmetic and copies ran while one was open for 0% of the time, Pallas kernels for 9%

profile of v7, /device:TPU:0, one launch (start us, length us, event | category | flops | bytes accessed | tf_op | source)
XLA Modules:
  0.0 340.7 jit_solution(6781915277419819255)
XLA Ops:
  0.0 0.9 broadcast_select_fusion.3
  0.9 2.1 collective-permute-start
  3.0 0.8 fusion.10
  3.7 0.1 collective-permute-start.1
  3.8 0.2 stack.88
  4.0 0.7 collective-permute-done
  4.7 0.2 fusion.5
  4.9 0.2 stack.89
  5.1 2.7 collective-permute-done.1
  7.8 0.2 slice_reduce_fusion.2
  8.0 0.1 mul.117
  8.1 0.3 fusion.4
  8.4 0.2 slice.76
  8.7 0.2 reshape.137
  8.9 0.2 reshape.136
  9.1 0.1 collective-permute-start.2
  9.2 1.2 collective-permute-done.2
  10.4 0.6 select_n.123.cut_ref
  11.0 0.2 collective-permute-start.3
  11.2 11.7 %pack.1 = (bf16[64,56,1152]{2,1,0:T(8,128)(2,1)}, bf16[64,32,1152]{2,1,0:T(8,128)(2,1)}) custom-call(bf16[36,2,36864]{2,1,0:T(2,128)(2,1)} %bitcast.40, bf16[36,2,36864]{2,1,0:T(2,128)(2,1)} %bitcast.41), custom_call_target="tpu_custom_call" | custom-call | tf_op jit(solution)/shard_map/pack/pallas_call | solution.py:58
  23.0 2.3 board.1
  25.2 0.0 collective-permute-done.3.refs_2_.refs_3_
  25.2 106.3 %all_to_all.25.refs_0_.refs_1_.refs_2_.refs_3_.refs_4_.refs_5_ = bf16[64,56,1152]{2,1,0:T(8,128)(2,1)} all-to-all(bf16[64,56,1152]{2,1,0:T(8,128)(2,1)} %board.1), channel_id=1, replica_groups=mesh['row'=2,'col_0'=4,'col_1'=4,'col_2'=2,'core'=2] {'row','col_0','col..., dimensions={0} | all-to-all | bytes 16515072 | tf_op jit(solution)/shard_map/all_to_all | solution.py:295
  131.5 6.5 %all-to-all-start.1 = ((bf16[64,32,1152]{2,1,0:T(8,128)(2,1)}), bf16[64,32,1152]{2,1,0:T(8,128)(2,1)}, u32[]{:S(2)}, u32[]{:S(2)}) async-start(bf16[64,32,1152]{2,1,0:T(8,128)(2,1)} %get-tuple-element.24), calls=%async_computation.1 | async-start | bytes 9437184 | tf_op jit(solution)/shard_map/all_to_all | solution.py:295
  138.0 9.2 %gate_up.2 = (bf16[256,1152]{1,0:T(8,128)(2,1)}, bf16[256,1152]{1,0:T(8,128)(2,1)}) custom-call(s32[1]{0:T(128)} %bitcast.2.core_ref, bf16[64,56,1152]{2,1,0:T(8,128)(2,1)} %all_to_all.25.refs_0_.refs_1_.refs_2_.refs_3_.refs_4_.refs_5_, bf16[64,56,1152]{2,1,0:T(8,128)(2,1)} %all_to_all.25.refs_0_.refs_1_.refs_2_.refs_3_.refs_4_.refs_5_, ...), custom_call_target="tpu_custom_call" | custom-call | tf_op jit(solution)/shard_map/gate_up/pallas_call | solution.py:199
  147.2 0.0 collective-permute-start.4
  147.2 0.1 pad_add_fusion.place_ref
  147.3 2.1 collective-permute-done.4.got_ref
  149.4 0.0 copy-start
  149.4 1.1 copy-done
  150.5 6.3 %down.2 = bf16[64,8,2304]{2,1,0:T(8,128)(2,1)} custom-call(s32[2]{0:T(128)S(1)} %pad_add_fusion.place_ref, bf16[256,1152]{1,0:T(8,128)(2,1)S(1)} %copy-done, bf16[256,1152]{1,0:T(8,128)(2,1)S(1)} %collective-permute-done.4.got_ref, bf16[2,288,4608]{2,1,0:T(8,128)(2,1)} %refs_1_.3, bf16[2,288,4608]{2,1,0:T(8,128)(2,1)} %refs_1_.3, ...), custom_call_target="tpu_custom_call" | custom-call | tf_op jit(solution)/shard_map/down/pallas_call | solution.py:274
  156.8 38.9 %all-to-all-done.1.refs_1_.refs_3_ = bf16[64,32,1152]{2,1,0:T(8,128)(2,1)} async-done(((bf16[64,32,1152]{2,1,0:T(8,128)(2,1)}), bf16[64,32,1152]{2,1,0:T(8,128)(2,1)}, u32[]{:S(2)}, u32[]{:S(2)}) %all-to-all-start.1) | async-done | bytes 4718624 | tf_op jit(solution)/shard_map/all_to_all | solution.py:295
  195.7 10.1 %all-to-all-start.2 = ((bf16[64,8,2304]{2,1,0:T(8,128)(2,1)}), bf16[64,8,2304]{2,1,0:T(8,128)(2,1)S(1)}, u32[]{:S(2)}, u32[]{:S(2)}) async-start(bf16[64,8,2304]{2,1,0:T(8,128)(2,1)} %down.2), calls=%async_computation.2 | async-start | bytes 4718592 | tf_op jit(solution)/shard_map/all_to_all | solution.py:295
  205.8 0.1 mul.128
  206.0 0.1 mul.134
  206.2 30.1 %all-to-all-done.2 = bf16[64,8,2304]{2,1,0:T(8,128)(2,1)S(1)} async-done(((bf16[64,8,2304]{2,1,0:T(8,128)(2,1)}), bf16[64,8,2304]{2,1,0:T(8,128)(2,1)S(1)}, u32[]{:S(2)}, u32[]{:S(2)}) %all-to-all-start.2) | async-done | bytes 2359328 | tf_op jit(solution)/shard_map/all_to_all | solution.py:295
  236.2 0.4 convert_reduce_fusion.1
  236.6 0.4 reshape.139
  237.1 0.1 multiply_reduce_fusion.1
  237.2 0.1 reduce_sum.71
  237.3 0.2 fusion.7
  237.5 0.4 fusion.3
  237.9 0.2 slice.82
  238.2 0.2 reshape.141
  238.4 0.2 reshape.140
  238.6 0.1 collective-permute-start.5
  238.7 1.2 collective-permute-done.5
  240.0 0.2 broadcast_in_dim.2
  240.1 39.4 %all_to_all.26 = bf16[64,8,2304]{2,1,0:T(8,128)(2,1)} all-to-all(bf16[64,8,2304]{2,1,0:T(8,128)(2,1)S(1)} %broadcast_in_dim.2), channel_id=1, replica_groups=mesh['row'=2,'col_0'=4,'col_1'=4,'col_2'=2,'core'=2] {'col_2','row','col..., dimensions={0} | all-to-all | bytes 4718592 | tf_op jit(solution)/shard_map/all_to_all | solution.py:295
  279.5 9.0 %gate_up.3 = (bf16[256,1152]{1,0:T(8,128)(2,1)}, bf16[256,1152]{1,0:T(8,128)(2,1)}) custom-call(s32[1]{0:T(128)} %bitcast.2.core_ref, bf16[512,2304]{1,0:T(8,128)(2,1)} %bitcast.39, bf16[64,32,1152]{2,1,0:T(8,128)(2,1)} %all-to-all-done.1.refs_1_.refs_3_, bf16[64,56,1152]{2,1,0:T(8,128)(2,1)} %all_to_all.25.refs_0_.refs_1_.refs_2_.refs_3_.refs_4_.refs_5_, ...), custom_call_target="tpu_custom_call" | custom-call | tf_op jit(solution)/shard_map/gate_up/pallas_call | solution.py:199
  288.5 0.0 collective-permute-start.6
  288.5 2.2 collective-permute-done.6.got_ref
  290.7 0.0 copy-start.1
  290.7 1.1 copy-done.1
  291.7 6.3 %down.3 = bf16[64,8,2304]{2,1,0:T(8,128)(2,1)} custom-call(s32[2]{0:T(128)S(1)} %pad_add_fusion.place_ref, bf16[256,1152]{1,0:T(8,128)(2,1)S(1)} %copy-done.1, bf16[256,1152]{1,0:T(8,128)(2,1)S(1)} %collective-permute-done.6.got_ref, bf16[2,288,4608]{2,1,0:T(8,128)(2,1)} %refs_1_.3, bf16[2,288,4608]{2,1,0:T(8,128)(2,1)} %refs_1_.3, ...), custom_call_target="tpu_custom_call" | custom-call | tf_op jit(solution)/shard_map/down/pallas_call | solution.py:274
  298.1 5.5 %all-to-all-start.4 = ((bf16[64,8,2304]{2,1,0:T(8,128)(2,1)}), bf16[64,8,2304]{2,1,0:T(8,128)(2,1)S(1)}, u32[]{:S(2)}, u32[]{:S(2)}) async-start(bf16[64,8,2304]{2,1,0:T(8,128)(2,1)} %down.3), calls=%async_computation.4 | async-start | bytes 4718592 | tf_op jit(solution)/shard_map/all_to_all | solution.py:295
  303.6 31.8 %all-to-all-done.4 = bf16[64,8,2304]{2,1,0:T(8,128)(2,1)S(1)} async-done(((bf16[64,8,2304]{2,1,0:T(8,128)(2,1)}), bf16[64,8,2304]{2,1,0:T(8,128)(2,1)S(1)}, u32[]{:S(2)}, u32[]{:S(2)}) %all-to-all-start.4) | async-done | bytes 2359328 | tf_op jit(solution)/shard_map/all_to_all | solution.py:295
  335.4 0.4 convert_reduce_fusion
  335.8 0.1 multiply_reduce_fusion
  335.9 0.1 reduce_sum.76
  336.0 0.1 fusion.8
  336.2 0.8 collective-permute-start.7
  336.9 3.1 collective-permute-done.7
  340.1 0.6 select_n.133
  (26 shorter events, 0.5 us)
Async XLA Ops:
  0.9 3.8 %collective-permute-start = (bf16[4,2304]{1,0:T(4,128)(2,1)S(1)}, bf16[4,2304]{1,0:T(4,128)(2,1)S(1)}, u32[]{:S(2)}, u32[]{:S(2)}) collective-permute-start(bf16[4,2304]{1,0:T(4,128)(2,1)S(1)} %get-tuple-element.42), channel_id=1, source_target_pairs={{0,64},{64,0},{1,65},{65,1},{2,66},{66,2},{3,67},{67,3},{4,68},{68... | collective-permute-start | bytes 55304 | tf_op jit(solution)/shard_map/ppermute | solution.py:301
  3.7 4.0 %collective-permute-start.1 = (f32[4,2304]{1,0:T(4,128)S(1)}, f32[4,2304]{1,0:T(4,128)S(1)}, u32[]{:S(2)}, u32[]{:S(2)}) collective-permute-start(f32[4,2304]{1,0:T(4,128)S(1)} %get-tuple-element.45), channel_id=1, source_target_pairs={{0,64},{64,0},{1,65},{65,1},{2,66},{66,2},{3,67},{67,3},{4,68},{68... | collective-permute-start | bytes 110600 | tf_op jit(solution)/shard_map/ppermute | solution.py:301
  9.1 1.3 collective-permute-start.2
  11.0 14.2 %collective-permute-start.3 = (bf16[2,288,4608]{2,1,0:T(8,128)(2,1)}, bf16[2,288,4608]{2,1,0:T(8,128)(2,1)}, u32[]{:S(2)}, u32[]{:S(2)}) collective-permute-start(bf16[2,288,4608]{2,1,0:T(8,128)(2,1)} %refs_1_.3), channel_id=1, source_target_pairs={{0,1},{1,0},{2,3},{3,2},{4,5},{5,4},{6,7},{7,6},{8,9},{9,8},{10,11... | collective-permute-start | bytes 15925256 | tf_op jit(solution)/shard_map/ppermute | solution.py:339
  131.5 64.2 %all-to-all-start.1 = ((bf16[64,32,1152]{2,1,0:T(8,128)(2,1)}), bf16[64,32,1152]{2,1,0:T(8,128)(2,1)}, u32[]{:S(2)}, u32[]{:S(2)}) async-start(bf16[64,32,1152]{2,1,0:T(8,128)(2,1)} %get-tuple-element.24), calls=%async_computation.1 | async-start | bytes 9437184 | tf_op jit(solution)/shard_map/all_to_all | solution.py:295
  147.2 2.2 collective-permute-start.4
  149.4 1.1 copy-start
  195.7 40.5 %all-to-all-start.2 = ((bf16[64,8,2304]{2,1,0:T(8,128)(2,1)}), bf16[64,8,2304]{2,1,0:T(8,128)(2,1)S(1)}, u32[]{:S(2)}, u32[]{:S(2)}) async-start(bf16[64,8,2304]{2,1,0:T(8,128)(2,1)} %down.2), calls=%async_computation.2 | async-start | bytes 4718592 | tf_op jit(solution)/shard_map/all_to_all | solution.py:295
  238.6 1.3 collective-permute-start.5
  288.5 2.2 collective-permute-start.6
  290.7 1.1 copy-start.1
  298.1 37.3 %all-to-all-start.4 = ((bf16[64,8,2304]{2,1,0:T(8,128)(2,1)}), bf16[64,8,2304]{2,1,0:T(8,128)(2,1)S(1)}, u32[]{:S(2)}, u32[]{:S(2)}) async-start(bf16[64,8,2304]{2,1,0:T(8,128)(2,1)} %down.3), calls=%async_computation.4 | async-start | bytes 4718592 | tf_op jit(solution)/shard_map/all_to_all | solution.py:295
  336.2 3.8 %collective-permute-start.7 = (bf16[4,2304]{1,0:T(4,128)(2,1)S(1)}, bf16[4,2304]{1,0:T(4,128)(2,1)S(1)}, u32[]{:S(2)}, u32[]{:S(2)}) collective-permute-start(bf16[4,2304]{1,0:T(4,128)(2,1)S(1)} %get-tuple-element.37), channel_id=1, source_target_pairs={{0,64},{64,0},{1,65},{65,1},{2,66},{66,2},{3,67},{67,3},{4,68},{68... | collective-permute-start | bytes 55304 | tf_op jit(solution)/shard_map/ppermute | solution.py:301

commit v8 on v7

--- a/solution.py
+++ b/solution.py
@@ -18,9 +18,9 @@
 norm_eps = 1e-06
 
 
-def pack_kernel(gate_ref, up_ref, first_ref, later_ref):
+def pack_kernel(early, gate_ref, up_ref, out_ref):
     rows, layers, lanes = gate_ref.shape
-    pairs = first_ref.shape[0] // 2
+    pairs = out_ref.shape[0] // 2
     width = lanes // pairs
     whole = rows // 8 * 8
     rest = rows - whole
@@ -37,32 +37,32 @@
                 tail = slice(2 * aligned + index * odd, 2 * aligned + (index + 1) * odd)
                 place = 2 * pair + side
                 for layer in range(layers):
-                    out_ref = first_ref if layer == 0 else later_ref
-                    start = 0 if layer == 0 else (layer - 1) * whole
-                    put = slice(start, start + whole)
-                    out_ref[place, put, main] = block[layer, :whole, first : first + aligned]
-                    out_ref[place, put, tail] = block[layer, :whole, extra : extra + odd]
-                    put = slice(whole + layer * rest, whole + (layer + 1) * rest)
-                    first_ref[place, put, main] = block[layer, whole:, first : first + aligned]
-                    first_ref[place, put, tail] = block[layer, whole:, extra : extra + odd]
-
-
-def packed(gate_weight, up_weight, chips, spare):
+                    if early == (layer == 0):
+                        start = max(layer - 1, 0) * whole
+                        put = slice(start, start + whole)
+                        out_ref[place, put, main] = block[layer, :whole, first : first + aligned]
+                        out_ref[place, put, tail] = block[layer, :whole, extra : extra + odd]
+                    if early:
+                        put = slice(whole + layer * rest, whole + (layer + 1) * rest)
+                        out_ref[place, put, main] = block[layer, whole:, first : first + aligned]
+                        out_ref[place, put, tail] = block[layer, whole:, extra : extra + odd]
+
+
+def packed(gate_weight, up_weight, chips, early, spare):
     layers, rows, hidden = gate_weight.shape
     width = hidden // chips * 2
     whole = rows // 8 * 8
     pairs = 4
     taken = pl.BlockSpec((rows, layers, pairs * width), lambda i: (0, 0, i))
-    lengths = (whole + layers * (rows - whole), (layers - 1) * whole)
-    room = (lengths[0] + spare, lengths[1])
+    length = whole + layers * (rows - whole) if early else (layers - 1) * whole
     return pl.pallas_call(
-        pack_kernel,
+        functools.partial(pack_kernel, early),
         grid=(chips // 2 // pairs,),
         in_specs=[taken, taken],
-        out_specs=[pl.BlockSpec((2 * pairs, n, width), lambda i: (i, 0, 0)) for n in lengths],
-        out_shape=[jax.ShapeDtypeStruct((chips, n, width), gate_weight.dtype) for n in room],
+        out_specs=pl.BlockSpec((2 * pairs, length, width), lambda i: (i, 0, 0)),
+        out_shape=jax.ShapeDtypeStruct((chips, length + spare, width), gate_weight.dtype),
         compiler_params=pltpu.CompilerParams(vmem_limit_bytes=59 * 2**20),
-        name="pack",
+        name="pack_early" if early else "pack_late",
     )(jnp.swapaxes(gate_weight, 0, 1), jnp.swapaxes(up_weight, 0, 1))
 
 
@@ -215,6 +215,38 @@
     )(core.reshape(1), *lhs, weights, rests, weights, rests)
 
 
+def part_kernel(core_ref, whole_ref, own_ref, other_ref):
+    chips = whole_ref.shape[0] // 8
+    width = whole_ref.shape[1]
+    part = whole_ref[...].astype(jnp.float32).reshape(chips, 8, width)
+    first, second = turned(part[: chips // 2], part[chips // 2 :])
+    first = first.reshape(-1, width).astype(own_ref.dtype)
+    second = second.reshape(-1, width).astype(own_ref.dtype)
+
+    @pl.when(core_ref[0] == 0)
+    def _():
+        own_ref[...] = first
+        other_ref[...] = second
+
+    @pl.when(core_ref[0] != 0)
+    def _():
+        own_ref[...] = second
+        other_ref[...] = first
+
+
+def parted(whole, core, cores):
+    tokens, width = whole.shape
+    own = tokens // cores
+    return pl.pallas_call(
+        part_kernel,
+        in_specs=[pl.BlockSpec(memory_space=pltpu.SMEM), pl.BlockSpec(memory_space=pltpu.VMEM)],
+        out_specs=[pl.BlockSpec(memory_space=pltpu.VMEM)] * 2,
+        out_shape=[jax.ShapeDtypeStruct((own, width), jnp.bfloat16)] * 2,
+        compiler_params=pltpu.CompilerParams(vmem_limit_bytes=20 * 2**20),
+        name="parted",
+    )(core.reshape(1), whole)
+
+
 def down_kernel(place_ref, mine_ref, got_ref, *refs):
     own_low_ref, own_high_ref, other_low_ref, other_high_ref, out_ref = refs[:5]
     hidden_ref, turned_ref, weight_ref = refs[5:]
@@ -331,7 +363,8 @@
     gains = 1.0 + swapped(jnp.stack((gains, gains)), "row")
 
     spare = 4 * cores * 2
-    first, later = packed(gate_weight, up_weight, chips, spare)
+    first = packed(gate_weight, up_weight, chips, True, spare)
+    later = packed(gate_weight, up_weight, chips, False, 0)
     values = current.astype(jnp.float32)
     normed = (values * scale_of(values) * gains[:, 0][:, None]).astype(jnp.bfloat16)
     cut = swapped(slabs(normed, chips, cores), "core").reshape(cores * count, -1)
@@ -348,12 +381,18 @@
             normed = (values * scale_of(values) * gains[:, layer][:, None]).astype(jnp.bfloat16)
             cut = swapped(slabs(normed, chips, cores), "core").reshape(cores * count, -1)
             everything = exchanged(copies_of(cut, ORDER), ORDER).reshape(-1, cut.shape[1])
-        weights = first if layer == 0 else later
-        mine, theirs = gate_up(everything, weights, first, layer, core, cores)
+        if layer == 0:
+            mine, theirs = gate_up(everything, first, first, layer, core, cores)
+        else:
+            whole = jnp.dot(everything, joined, preferred_element_type=jnp.float32)
+            mine, theirs = parted(whole.astype(jnp.bfloat16), core, cores)
         got = lax.ppermute(theirs, "core", SWAP)
         sent = down(mine, got, down_weight, other_down, layer, place, chips)
         if layer == 0:
-            sent, later = lax.optimization_barrier((sent, later))
+            rows = gate_weight.shape[1]
+            tails = first[:, rows : rows + rows - later.shape[1]].reshape(-1, first.shape[2])
+            sent, later, tails = lax.optimization_barrier((sent, later, tails))
+            joined = jnp.concatenate((later.reshape(-1, later.shape[2]), tails), axis=0)
         arrived = exchanged(sent, CHIP)
         branch = jnp.sum(arrived.astype(jnp.float32), axis=0).reshape(values.shape)
         post = branch * scale_of(branch) * gains[:, layers + layer][:, None]

time: 342 us -> 375 us (1.096)
  waiting for transfers between devices: 114 us -> 226 us
  blocking collectives: 146 us -> 39.3 us
  starting transfers between devices: 25.4 us -> 47.8 us
  matrix products: 0 us -> 5.54 us
    all_to_all x3 -> x4, waiting for transfers between devices: 101 us -> 215 us  [exchanged(): return lax.all_to_all(blocks, axes, split_axis=0, concat_axis=0, tiled=True)]
    all_to_all x2 -> x1, blocking collectives: 146 us -> 39.3 us  [exchanged(): return lax.all_to_all(blocks, axes, split_axis=0, concat_axis=0, tiled=True)]
    all_to_all x3 -> x4, starting transfers between devices: 22.1 us -> 44.4 us  [exchanged(): return lax.all_to_all(blocks, axes, split_axis=0, concat_axis=0, tiled=True)]
    pallas_call x2 -> x1, Pallas kernels: 18.2 us -> 9.19 us  [gate_up(): pl.pallas_call(functools.partial(gate_up_kernel, layer, pieces), grid=(wi...]
    pallas_call x1 -> x3, Pallas kernels: 11.7 us -> 19.1 us  [the longest x2 18.4 us: packed(): pl.pallas_call(functools.partial(pack_kernel, early), grid=(chips // 2 //...]
    dot_general x0 -> x1, matrix products: none -> 5.54 us  [on_device(): whole = jnp.dot(everything, joined, preferred_element_type=jnp.float32)]
  transfers between devices with their start and end apart: 11 -> 12, of which waited for: 10 -> 11; matrix products, arithmetic and copies ran while one was open for 0% -> 1% of each run, Pallas kernels for 9% -> 10%
where the time goes in v8:
time: 375 us; the launch traced here: 374 us
  waiting for transfers between devices  226 us (60%)
  starting transfers between devices  47.8 us (13%)
  Pallas kernels  43.2 us (12%)
  blocking collectives  39.3 us (10%)
  local copies, waits for them, and re-layouts  7.15 us (2%)
  matrix products  5.54 us (1%)
  other arithmetic  4.04 us (1%)
    all_to_all x4, waiting for transfers between devices, exchanged(): return lax.all_to_all(blocks, axes, split_axis=0, concat_axis=0, tiled=True)  215 us
    all_to_all x4, starting transfers between devices, exchanged(): return lax.all_to_all(blocks, axes, split_axis=0, concat_axis=0, tiled=True)  44.4 us
    all_to_all x1, blocking collectives, exchanged(): return lax.all_to_all(blocks, axes, split_axis=0, concat_axis=0, tiled=True)  39.3 us
    pallas_call x2, Pallas kernels, packed(): pl.pallas_call(functools.partial(pack_kernel, early), grid=(chips // 2 //...  18.4 us
    pallas_call x2, Pallas kernels, down(): pl.pallas_call(down_kernel, grid=(steps,), in_specs=[pl.BlockSpec(memory_...  12.7 us
    pallas_call x1, Pallas kernels, gate_up(): pl.pallas_call(functools.partial(gate_up_kernel, layer, pieces), grid=(wi...  9.19 us
    ppermute x5, waiting for transfers between devices, swapped(): got = lax.ppermute(jnp.where(index == 0, blocks[1], blocks[0]), axis, SWAP)  8.81 us
  transfers between devices with their start and end apart: 12, of which 11 were waited for; matrix products, arithmetic and copies ran while one was open for 1% of the time, Pallas kernels for 10%

profile of v8, /device:TPU:0, one launch (start us, length us, event | category | flops | bytes accessed | tf_op | source)
XLA Modules:
  0.0 373.5 jit_solution(10206522643630448100)
XLA Ops:
  0.0 0.9 broadcast_select_fusion.3
  0.9 2.1 collective-permute-start
  3.0 0.8 fusion.19
  3.7 0.1 collective-permute-start.1
  3.8 0.2 stack.88
  4.0 0.7 collective-permute-done
  4.7 0.2 fusion.13
  4.9 0.2 stack.89
  5.1 2.7 collective-permute-done.1
  7.8 0.2 slice_reduce_fusion.2
  8.0 0.2 mul.117
  8.1 0.3 fusion.12
  8.4 0.2 slice.80
  8.7 0.2 reshape.143
  8.9 0.2 reshape.142
  9.1 0.1 collective-permute-start.2
  9.2 1.2 collective-permute-done.2
  10.4 0.6 select_n.123.cut_ref
  11.0 0.2 collective-permute-start.3
  11.2 9.4 %pack_early.1.held_ref = bf16[64,56,1152]{2,1,0:T(8,128)(2,1)} custom-call(bf16[36,2,36864]{2,1,0:T(2,128)(2,1)} %bitcast.42, bf16[36,2,36864]{2,1,0:T(2,128)(2,1)} %bitcast.44), custom_call_target="tpu_custom_call" | custom-call | tf_op jit(solution)/shard_map/pack_early/pallas_call | solution.py:58
  20.6 2.3 board.1
  22.9 11.2 %all-to-all-start = ((bf16[64,56,1152]{2,1,0:T(8,128)(2,1)}), bf16[64,56,1152]{2,1,0:T(8,128)(2,1)}, u32[]{:S(2)}, u32[]{:S(2)}) async-start(bf16[64,56,1152]{2,1,0:T(8,128)(2,1)} %board.1), calls=%async_computation | async-start | bytes 16515072 | tf_op jit(solution)/shard_map/all_to_all | solution.py:327
  34.1 9.0 %pack_late.1 = bf16[64,32,1152]{2,1,0:T(8,128)(2,1)} custom-call(bf16[36,2,36864]{2,1,0:T(2,128)(2,1)} %bitcast.43, bf16[36,2,36864]{2,1,0:T(2,128)(2,1)} %bitcast.45), custom_call_target="tpu_custom_call" | custom-call | tf_op jit(solution)/shard_map/pack_late/pallas_call | solution.py:58
  43.1 114.2 %all-to-all-done.refs_0_.refs_1_.refs_2_.refs_3_.refs_4_.refs_5_ = bf16[64,56,1152]{2,1,0:T(8,128)(2,1)} async-done(((bf16[64,56,1152]{2,1,0:T(8,128)(2,1)}), bf16[64,56,1152]{2,1,0:T(8,128)(2,1)}, u32[]{:S(2)}, u32[]{:S(2)}) %all-to-all-start) | async-done | bytes 8257568 | tf_op jit(solution)/shard_map/all_to_all | solution.py:327
  157.3 17.7 %all-to-all-start.1 = ((bf16[64,32,1152]{2,1,0:T(8,128)(2,1)}), bf16[64,32,1152]{2,1,0:T(8,128)(2,1)}, u32[]{:S(2)}, u32[]{:S(2)}) async-start(bf16[64,32,1152]{2,1,0:T(8,128)(2,1)} %pack_late.1), calls=%async_computation.1 | async-start | bytes 9437184 | tf_op jit(solution)/shard_map/all_to_all | solution.py:327
  175.0 9.2 %gate_up.1 = (bf16[256,1152]{1,0:T(8,128)(2,1)}, bf16[256,1152]{1,0:T(8,128)(2,1)}) custom-call(s32[1]{0:T(128)} %bitcast.2.core_ref, bf16[64,56,1152]{2,1,0:T(8,128)(2,1)} %all-to-all-done.refs_0_.refs_1_.refs_2_.refs_3_.refs_4_.refs_5_, bf16[64,56,1152]{2,1,0:T(8,128)(2,1)} %all-to-all-done.refs_0_.refs_1_.refs_2_.refs_3_.refs_4_.refs_5_, ...), custom_call_target="tpu_custom_call" | custom-call | tf_op jit(solution)/shard_map/gate_up/pallas_call | solution.py:199
  184.2 0.1 pad_add_fusion.place_ref
  184.3 1.6 slice.83
  185.9 0.1 reshape.144
  186.0 0.4 collective-permute-done.4.got_ref
  186.4 1.1 copy-done
  187.5 6.3 %down.2 = bf16[64,8,2304]{2,1,0:T(8,128)(2,1)} custom-call(s32[2]{0:T(128)S(1)} %pad_add_fusion.place_ref, bf16[256,1152]{1,0:T(8,128)(2,1)S(1)} %copy-done, bf16[256,1152]{1,0:T(8,128)(2,1)S(1)} %collective-permute-done.4.got_ref, bf16[2,288,4608]{2,1,0:T(8,128)(2,1)} %refs_1_.3, bf16[2,288,4608]{2,1,0:T(8,128)(2,1)} %refs_1_.3, ...), custom_call_target="tpu_custom_call" | custom-call | tf_op jit(solution)/shard_map/down/pallas_call | solution.py:306
  193.8 39.0 %all-to-all-done.1 = bf16[64,32,1152]{2,1,0:T(8,128)(2,1)} async-done(((bf16[64,32,1152]{2,1,0:T(8,128)(2,1)}), bf16[64,32,1152]{2,1,0:T(8,128)(2,1)}, u32[]{:S(2)}, u32[]{:S(2)}) %all-to-all-start.1) | async-done | bytes 4718624 | tf_op jit(solution)/shard_map/all_to_all | solution.py:327
  232.8 10.0 %all-to-all-start.2 = ((bf16[64,8,2304]{2,1,0:T(8,128)(2,1)}), bf16[64,8,2304]{2,1,0:T(8,128)(2,1)S(1)}, u32[]{:S(2)}, u32[]{:S(2)}) async-start(bf16[64,8,2304]{2,1,0:T(8,128)(2,1)} %down.2), calls=%async_computation.2 | async-start | bytes 4718592 | tf_op jit(solution)/shard_map/all_to_all | solution.py:327
  242.8 0.1 mul.128
  243.0 0.1 mul.134
  243.1 30.0 %all-to-all-done.2 = bf16[64,8,2304]{2,1,0:T(8,128)(2,1)S(1)} async-done(((bf16[64,8,2304]{2,1,0:T(8,128)(2,1)}), bf16[64,8,2304]{2,1,0:T(8,128)(2,1)S(1)}, u32[]{:S(2)}, u32[]{:S(2)}) %all-to-all-start.2) | async-done | bytes 2359328 | tf_op jit(solution)/shard_map/all_to_all | solution.py:327
  273.1 0.3 convert_reduce_fusion.1
  273.5 0.4 reshape.146
  273.9 0.1 multiply_reduce_fusion.1
  274.1 0.1 reduce_sum.71
  274.2 0.2 fusion.15
  274.4 0.4 fusion.11
  274.8 0.2 slice.87
  275.0 0.2 reshape.148
  275.3 0.2 reshape.147
  275.5 0.1 collective-permute-start.5
  275.6 1.2 collective-permute-done.5
  276.8 0.2 broadcast_in_dim.2
  277.0 39.3 %all_to_all.25 = bf16[64,8,2304]{2,1,0:T(8,128)(2,1)S(1)} all-to-all(bf16[64,8,2304]{2,1,0:T(8,128)(2,1)S(1)} %broadcast_in_dim.2), channel_id=1, replica_groups=mesh['row'=2,'col_0'=4,'col_1'=4,'col_2'=2,'core'=2] {'col_2','row','col..., dimensions={0} | all-to-all | bytes 4718592 | tf_op jit(solution)/shard_map/all_to_all | solution.py:327
  316.3 5.5 %fusion.4.whole_ref = bf16[512,1152]{1,0:T(8,128)(2,1)S(1)} fusion(bf16[256,1152]{1,0:T(8,128)(2,1)S(1)} %reshape.144, bf16[2048,1152]{1,0:T(8,128)(2,1)} %bitcast.15, bf16[64,8,2304]{2,1,0:T(8,128)(2,1)S(1)} %all_to_all.25), kind=kOutput, calls=%fused_computation.6 | convolution fusion | flops 2729115648 | bytes 8847360 | tf_op jit(solution)/shard_map/dot_general | solution.py:387
  321.9 0.6 parted.1
  322.5 0.1 collective-permute-start.6
  322.6 2.0 collective-permute-done.6.got_ref
  324.6 6.3 %down.3 = bf16[64,8,2304]{2,1,0:T(8,128)(2,1)} custom-call(s32[2]{0:T(128)S(1)} %pad_add_fusion.place_ref, bf16[256,1152]{1,0:T(8,128)(2,1)S(1)} %get-tuple-element.25.mine_ref, bf16[256,1152]{1,0:T(8,128)(2,1)S(1)} %collective-permute-done.6.got_ref, bf16[2,288,4608]{2,1,0:T(8,128)(2,1)} %refs_1_.3, bf16[2,288,4608]{2,1,0:T(8,128)(2,1)} %refs_1_.3, ...), custom_call_target="tpu_custom_call" | custom-call | tf_op jit(solution)/shard_map/down/pallas_call | solution.py:306
  330.9 5.5 %all-to-all-start.4 = ((bf16[64,8,2304]{2,1,0:T(8,128)(2,1)}), bf16[64,8,2304]{2,1,0:T(8,128)(2,1)S(1)}, u32[]{:S(2)}, u32[]{:S(2)}) async-start(bf16[64,8,2304]{2,1,0:T(8,128)(2,1)} %down.3), calls=%async_computation.4 | async-start | bytes 4718592 | tf_op jit(solution)/shard_map/all_to_all | solution.py:327
  336.5 31.8 %all-to-all-done.4 = bf16[64,8,2304]{2,1,0:T(8,128)(2,1)S(1)} async-done(((bf16[64,8,2304]{2,1,0:T(8,128)(2,1)}), bf16[64,8,2304]{2,1,0:T(8,128)(2,1)S(1)}, u32[]{:S(2)}, u32[]{:S(2)}) %all-to-all-start.4) | async-done | bytes 2359328 | tf_op jit(solution)/shard_map/all_to_all | solution.py:327
  368.3 0.3 convert_reduce_fusion
  368.6 0.1 multiply_reduce_fusion
  368.8 0.1 reduce_sum.76
  368.9 0.1 fusion.16
  369.0 0.8 collective-permute-start.7
  369.8 3.1 collective-permute-done.7
  372.9 0.6 select_n.133
  (29 shorter events, 0.5 us)
Async XLA Ops:
  0.9 3.8 %collective-permute-start = (bf16[4,2304]{1,0:T(4,128)(2,1)S(1)}, bf16[4,2304]{1,0:T(4,128)(2,1)S(1)}, u32[]{:S(2)}, u32[]{:S(2)}) collective-permute-start(bf16[4,2304]{1,0:T(4,128)(2,1)S(1)} %get-tuple-element.40), channel_id=1, source_target_pairs={{0,64},{64,0},{1,65},{65,1},{2,66},{66,2},{3,67},{67,3},{4,68},{68... | collective-permute-start | bytes 55304 | tf_op jit(solution)/shard_map/ppermute | solution.py:333
  3.7 4.0 %collective-permute-start.1 = (f32[4,2304]{1,0:T(4,128)S(1)}, f32[4,2304]{1,0:T(4,128)S(1)}, u32[]{:S(2)}, u32[]{:S(2)}) collective-permute-start(f32[4,2304]{1,0:T(4,128)S(1)} %get-tuple-element.43), channel_id=1, source_target_pairs={{0,64},{64,0},{1,65},{65,1},{2,66},{66,2},{3,67},{67,3},{4,68},{68... | collective-permute-start | bytes 110600 | tf_op jit(solution)/shard_map/ppermute | solution.py:333
  9.1 1.3 collective-permute-start.2
  11.0 11.9 %collective-permute-start.3 = (bf16[2,288,4608]{2,1,0:T(8,128)(2,1)}, bf16[2,288,4608]{2,1,0:T(8,128)(2,1)}, u32[]{:S(2)}, u32[]{:S(2)}) collective-permute-start(bf16[2,288,4608]{2,1,0:T(8,128)(2,1)} %refs_1_.3), channel_id=1, source_target_pairs={{0,1},{1,0},{2,3},{3,2},{4,5},{5,4},{6,7},{7,6},{8,9},{9,8},{10,11... | collective-permute-start | bytes 15925256 | tf_op jit(solution)/shard_map/ppermute | solution.py:372
  22.9 134.4 %all-to-all-start = ((bf16[64,56,1152]{2,1,0:T(8,128)(2,1)}), bf16[64,56,1152]{2,1,0:T(8,128)(2,1)}, u32[]{:S(2)}, u32[]{:S(2)}) async-start(bf16[64,56,1152]{2,1,0:T(8,128)(2,1)} %board.1), calls=%async_computation | async-start | bytes 16515072 | tf_op jit(solution)/shard_map/all_to_all | solution.py:327
  157.3 75.5 %all-to-all-start.1 = ((bf16[64,32,1152]{2,1,0:T(8,128)(2,1)}), bf16[64,32,1152]{2,1,0:T(8,128)(2,1)}, u32[]{:S(2)}, u32[]{:S(2)}) async-start(bf16[64,32,1152]{2,1,0:T(8,128)(2,1)} %pack_late.1), calls=%async_computation.1 | async-start | bytes 9437184 | tf_op jit(solution)/shard_map/all_to_all | solution.py:327
  184.2 2.2 collective-permute-start.4
  186.4 1.1 copy-start
  232.8 40.3 %all-to-all-start.2 = ((bf16[64,8,2304]{2,1,0:T(8,128)(2,1)}), bf16[64,8,2304]{2,1,0:T(8,128)(2,1)S(1)}, u32[]{:S(2)}, u32[]{:S(2)}) async-start(bf16[64,8,2304]{2,1,0:T(8,128)(2,1)} %down.2), calls=%async_computation.2 | async-start | bytes 4718592 | tf_op jit(solution)/shard_map/all_to_all | solution.py:327
  275.5 1.3 collective-permute-start.5
  322.5 2.1 collective-permute-start.6
  330.9 37.3 %all-to-all-start.4 = ((bf16[64,8,2304]{2,1,0:T(8,128)(2,1)}), bf16[64,8,2304]{2,1,0:T(8,128)(2,1)S(1)}, u32[]{:S(2)}, u32[]{:S(2)}) async-start(bf16[64,8,2304]{2,1,0:T(8,128)(2,1)} %down.3), calls=%async_computation.4 | async-start | bytes 4718592 | tf_op jit(solution)/shard_map/all_to_all | solution.py:327
  369.0 3.8 %collective-permute-start.7 = (bf16[4,2304]{1,0:T(4,128)(2,1)S(1)}, bf16[4,2304]{1,0:T(4,128)(2,1)S(1)}, u32[]{:S(2)}, u32[]{:S(2)}) collective-permute-start(bf16[4,2304]{1,0:T(4,128)(2,1)S(1)} %get-tuple-element.35), channel_id=1, source_target_pairs={{0,64},{64,0},{1,65},{65,1},{2,66},{66,2},{3,67},{67,3},{4,68},{68... | collective-permute-start | bytes 55304 | tf_op jit(solution)/shard_map/ppermute | solution.py:333

commit v9 on v6

--- a/solution.py
+++ b/solution.py
@@ -248,7 +248,7 @@
 def down(mine, got, own_down, other_down, layer, place, chips):
     rows, width = mine.shape
     _, stored, model_width = own_down.shape
-    step = 768
+    step = 1152
     steps = model_width // 2 // step
     whole = pl.BlockSpec((rows, width), lambda i: (0, 0))
     low = pl.BlockSpec((1, stored, step), lambda i: (layer, 0, i))
@@ -338,9 +338,9 @@
         got = lax.ppermute(theirs, "core", SWAP)
         sent = down(mine, got, down_weight, other_down, layer, place, chips)
         if layer == 0:
-            sent, later = lax.optimization_barrier((sent, later))
-            rest = (first.shape[1] - later.shape[1]) // layers
-            tails = first[:, first.shape[1] - rest :].reshape(-1, first.shape[2])
+            rows = gate_weight.shape[1]
+            tails = first[:, rows : rows + rows - later.shape[1]].reshape(-1, first.shape[2])
+            sent, later, tails = lax.optimization_barrier((sent, later, tails))
             joined = jnp.concatenate((later.reshape(-1, later.shape[2]), tails), axis=0)
         arrived = exchanged(sent, CHIP)
         branch = jnp.sum(arrived.astype(jnp.float32), axis=0).reshape(values.shape)

time: 341 us -> 337 us (0.988)
  blocking collectives: 75.5 us -> 115 us
  waiting for transfers between devices: 168 us -> 135 us
  starting transfers between devices: 42.7 us -> 35.9 us
    all_to_all x1 -> x2, blocking collectives: 75.5 us -> 115 us  [exchanged(): return lax.all_to_all(blocks, axes, split_axis=0, concat_axis=0, tiled=True)]
    all_to_all x5 -> x4, waiting for transfers between devices: 155 us -> 123 us  [exchanged(): return lax.all_to_all(blocks, axes, split_axis=0, concat_axis=0, tiled=True)]
    all_to_all x5 -> x4, starting transfers between devices: 39.3 us -> 32.4 us  [exchanged(): return lax.all_to_all(blocks, axes, split_axis=0, concat_axis=0, tiled=True)]
  transfers between devices with their start and end apart: 13 -> 12, of which waited for: 12 -> 11; matrix products, arithmetic and copies ran while one was open for 1% -> 1% of each run, Pallas kernels for 8% -> 8%
where the time goes in v9:
time: 337 us; the launch traced here: 336 us
  waiting for transfers between devices  135 us (40%)
  blocking collectives  115 us (34%)
  starting transfers between devices  35.9 us (11%)
  Pallas kernels  32.6 us (10%)
  local copies, waits for them, and re-layouts  8.1 us (2%)
  matrix products  5.54 us (2%)
  other arithmetic  4.04 us (1%)
    all_to_all x4, waiting for transfers between devices, exchanged(): return lax.all_to_all(blocks, axes, split_axis=0, concat_axis=0, tiled=True)  123 us
    all_to_all x2, blocking collectives, exchanged(): return lax.all_to_all(blocks, axes, split_axis=0, concat_axis=0, tiled=True)  115 us
    all_to_all x4, starting transfers between devices, exchanged(): return lax.all_to_all(blocks, axes, split_axis=0, concat_axis=0, tiled=True)  32.4 us
    pallas_call x2, Pallas kernels, down(): pl.pallas_call(down_kernel, grid=(steps,), in_specs=[pl.BlockSpec(memory_...  11.8 us
    pallas_call x1, Pallas kernels, packed(): pl.pallas_call(pack_kernel, grid=(chips // 2 // pairs,), in_specs=[taken,...  11.7 us
    ppermute x5, waiting for transfers between devices, swapped(): got = lax.ppermute(jnp.where(index == 0, blocks[1], blocks[0]), axis, SWAP)  8.82 us
    pallas_call x1, Pallas kernels, gate_up(): pl.pallas_call(functools.partial(gate_up_kernel, layer), grid=(width // s...  8.55 us
  transfers between devices with their start and end apart: 12, of which 11 were waited for; matrix products, arithmetic and copies ran while one was open for 1% of the time, Pallas kernels for 8%

profile of v9, /device:TPU:0, one launch (start us, length us, event | category | flops | bytes accessed | tf_op | source)
XLA Modules:
  0.0 336.2 jit_solution(14396744134655527447)
XLA Ops:
  0.0 0.9 broadcast_select_fusion.3
  0.9 2.1 collective-permute-start
  3.0 0.8 fusion.19
  3.7 0.1 collective-permute-start.1
  3.8 0.2 stack.88
  4.0 0.7 collective-permute-done
  4.7 0.2 fusion.13
  4.9 0.2 stack.89
  5.1 2.7 collective-permute-done.1
  7.8 0.2 slice_reduce_fusion.2
  8.0 0.2 mul.117
  8.1 0.3 fusion.12
  8.4 0.2 slice.80
  8.7 0.2 reshape.146
  8.9 0.2 reshape.145
  9.1 0.1 collective-permute-start.2
  9.2 1.2 collective-permute-done.2
  10.4 0.2 collective-permute-start.3
  10.7 1.6 broadcast_in_dim.4
  12.2 11.0 %all-to-all-start = ((bf16[64,8,2304]{2,1,0:T(8,128)(2,1)}), bf16[64,8,2304]{2,1,0:T(8,128)(2,1)S(1)}, u32[]{:S(2)}, u32[]{:S(2)}) async-start(bf16[64,8,2304]{2,1,0:T(8,128)(2,1)} %broadcast_in_dim.4), calls=%async_computation | async-start | bytes 4718592 | tf_op jit(solution)/shard_map/all_to_all | solution.py:278
  23.2 11.7 %pack.1 = (bf16[64,40,1152]{2,1,0:T(8,128)(2,1)}, bf16[64,32,1152]{2,1,0:T(8,128)(2,1)}) custom-call(bf16[36,2,36864]{2,1,0:T(2,128)(2,1)} %bitcast.44, bf16[36,2,36864]{2,1,0:T(2,128)(2,1)} %bitcast.45), custom_call_target="tpu_custom_call" | custom-call | tf_op jit(solution)/shard_map/pack/pallas_call | solution.py:57
  34.9 22.0 %all-to-all-done = bf16[64,8,2304]{2,1,0:T(8,128)(2,1)S(1)} async-done(((bf16[64,8,2304]{2,1,0:T(8,128)(2,1)}), bf16[64,8,2304]{2,1,0:T(8,128)(2,1)S(1)}, u32[]{:S(2)}, u32[]{:S(2)}) %all-to-all-start) | async-done | bytes 2359328 | tf_op jit(solution)/shard_map/all_to_all | solution.py:278
  56.9 75.5 %all_to_all.30.refs_0_.refs_1_.refs_2_.refs_3_ = bf16[64,40,1152]{2,1,0:T(8,128)(2,1)} all-to-all(bf16[64,40,1152]{2,1,0:T(8,128)(2,1)} %get-tuple-element.23), channel_id=1, replica_groups=mesh['row'=2,'col_0'=4,'col_1'=4,'col_2'=2,'core'=2] {'row','col_0','col..., dimensions={0} | all-to-all | bytes 11796480 | tf_op jit(solution)/shard_map/all_to_all | solution.py:278
  132.4 5.8 %all-to-all-start.2 = ((bf16[64,32,1152]{2,1,0:T(8,128)(2,1)}), bf16[64,32,1152]{2,1,0:T(8,128)(2,1)}, u32[]{:S(2)}, u32[]{:S(2)}) async-start(bf16[64,32,1152]{2,1,0:T(8,128)(2,1)} %get-tuple-element.27), calls=%async_computation.2 | async-start | bytes 9437184 | tf_op jit(solution)/shard_map/all_to_all | solution.py:278
  138.2 8.6 %gate_up.1 = (bf16[256,1152]{1,0:T(8,128)(2,1)}, bf16[256,1152]{1,0:T(8,128)(2,1)}) custom-call(s32[1]{0:T(128)} %bitcast.2.core_ref, bf16[512,2304]{1,0:T(8,128)(2,1)} %bitcast.43, bf16[64,40,1152]{2,1,0:T(8,128)(2,1)} %all_to_all.30.refs_0_.refs_1_.refs_2_.refs_3_, bf16[64,40,1152]{2,1,0:T(8,128)(2,1)} %all_to_all.30.refs_0_.refs_1_.refs_2_.refs_3_, ...), custom_call_target="tpu_custom_call" | custom-call | tf_op jit(solution)/shard_map/gate_up/pallas_call | solution.py:150
  146.8 0.0 collective-permute-start.4
  146.8 0.1 pad_add_fusion.place_ref
  146.8 1.6 slice.83
  148.4 0.1 reshape.148
  148.6 0.4 collective-permute-done.4.got_ref
  149.0 1.1 copy-done
  150.0 5.9 %down.2 = bf16[64,8,2304]{2,1,0:T(8,128)(2,1)} custom-call(s32[2]{0:T(128)S(1)} %pad_add_fusion.place_ref, bf16[256,1152]{1,0:T(8,128)(2,1)S(1)} %copy-done, bf16[256,1152]{1,0:T(8,128)(2,1)S(1)} %collective-permute-done.4.got_ref, bf16[2,288,4608]{2,1,0:T(8,128)(2,1)} %refs_1_.3, bf16[2,288,4608]{2,1,0:T(8,128)(2,1)} %refs_1_.3, ...), custom_call_target="tpu_custom_call" | custom-call | tf_op jit(solution)/shard_map/down/pallas_call | solution.py:257
  155.9 38.9 %all-to-all-done.2 = bf16[64,32,1152]{2,1,0:T(8,128)(2,1)} async-done(((bf16[64,32,1152]{2,1,0:T(8,128)(2,1)}), bf16[64,32,1152]{2,1,0:T(8,128)(2,1)}, u32[]{:S(2)}, u32[]{:S(2)}) %all-to-all-start.2) | async-done | bytes 4718624 | tf_op jit(solution)/shard_map/all_to_all | solution.py:278
  194.8 10.1 %all-to-all-start.3 = ((bf16[64,8,2304]{2,1,0:T(8,128)(2,1)}), bf16[64,8,2304]{2,1,0:T(8,128)(2,1)S(1)}, u32[]{:S(2)}, u32[]{:S(2)}) async-start(bf16[64,8,2304]{2,1,0:T(8,128)(2,1)} %down.2), calls=%async_computation.3 | async-start | bytes 4718592 | tf_op jit(solution)/shard_map/all_to_all | solution.py:278
  204.9 0.1 mul.128
  205.1 0.1 mul.134
  205.3 30.8 %all-to-all-done.3 = bf16[64,8,2304]{2,1,0:T(8,128)(2,1)S(1)} async-done(((bf16[64,8,2304]{2,1,0:T(8,128)(2,1)}), bf16[64,8,2304]{2,1,0:T(8,128)(2,1)S(1)}, u32[]{:S(2)}, u32[]{:S(2)}) %all-to-all-start.3) | async-done | bytes 2359328 | tf_op jit(solution)/shard_map/all_to_all | solution.py:278
  236.1 0.3 convert_reduce_fusion.1
  236.4 0.4 reshape.150
  236.9 0.1 multiply_reduce_fusion.1
  237.0 0.1 reduce_sum.71
  237.1 0.2 fusion.15
  237.3 0.4 fusion.11
  237.7 0.2 slice.87
  238.0 0.2 reshape.152
  238.2 0.2 reshape.151
  238.4 0.1 collective-permute-start.5
  238.5 1.2 collective-permute-done.5
  239.8 0.2 broadcast_in_dim.5
  239.9 39.5 %all_to_all.31 = bf16[64,8,2304]{2,1,0:T(8,128)(2,1)S(1)} all-to-all(bf16[64,8,2304]{2,1,0:T(8,128)(2,1)S(1)} %broadcast_in_dim.5), channel_id=1, replica_groups=mesh['row'=2,'col_0'=4,'col_1'=4,'col_2'=2,'core'=2] {'col_2','row','col..., dimensions={0} | all-to-all | bytes 4718592 | tf_op jit(solution)/shard_map/all_to_all | solution.py:278
  279.5 5.5 %fusion.4.whole_ref = bf16[512,1152]{1,0:T(8,128)(2,1)S(1)} fusion(bf16[256,1152]{1,0:T(8,128)(2,1)S(1)} %reshape.148, bf16[2048,1152]{1,0:T(8,128)(2,1)} %bitcast.16, bf16[64,8,2304]{2,1,0:T(8,128)(2,1)S(1)} %all_to_all.31), kind=kOutput, calls=%fused_computation.6 | convolution fusion | flops 2729115648 | bytes 8847360 | tf_op jit(solution)/shard_map/dot_general | solution.py:336
  285.0 0.6 parted.1
  285.7 0.1 collective-permute-start.6
  285.8 2.0 collective-permute-done.6.got_ref
  287.8 5.9 %down.3 = bf16[64,8,2304]{2,1,0:T(8,128)(2,1)} custom-call(s32[2]{0:T(128)S(1)} %pad_add_fusion.place_ref, bf16[256,1152]{1,0:T(8,128)(2,1)S(1)} %get-tuple-element.31.mine_ref, bf16[256,1152]{1,0:T(8,128)(2,1)S(1)} %collective-permute-done.6.got_ref, bf16[2,288,4608]{2,1,0:T(8,128)(2,1)} %refs_1_.3, bf16[2,288,4608]{2,1,0:T(8,128)(2,1)} %refs_1_.3, ...), custom_call_target="tpu_custom_call" | custom-call | tf_op jit(solution)/shard_map/down/pallas_call | solution.py:257
  293.6 5.5 %all-to-all-start.5 = ((bf16[64,8,2304]{2,1,0:T(8,128)(2,1)}), bf16[64,8,2304]{2,1,0:T(8,128)(2,1)S(1)}, u32[]{:S(2)}, u32[]{:S(2)}) async-start(bf16[64,8,2304]{2,1,0:T(8,128)(2,1)} %down.3), calls=%async_computation.5 | async-start | bytes 4718592 | tf_op jit(solution)/shard_map/all_to_all | solution.py:278
  299.2 31.8 %all-to-all-done.5 = bf16[64,8,2304]{2,1,0:T(8,128)(2,1)S(1)} async-done(((bf16[64,8,2304]{2,1,0:T(8,128)(2,1)}), bf16[64,8,2304]{2,1,0:T(8,128)(2,1)S(1)}, u32[]{:S(2)}, u32[]{:S(2)}) %all-to-all-start.5) | async-done | bytes 2359328 | tf_op jit(solution)/shard_map/all_to_all | solution.py:278
  331.0 0.3 convert_reduce_fusion
  331.4 0.1 multiply_reduce_fusion
  331.5 0.1 reduce_sum.76
  331.6 0.1 fusion.16
  331.7 0.8 collective-permute-start.7
  332.5 3.1 collective-permute-done.7
  335.6 0.6 select_n.133
  (31 shorter events, 0.5 us)
Async XLA Ops:
  0.9 3.8 %collective-permute-start = (bf16[4,2304]{1,0:T(4,128)(2,1)S(1)}, bf16[4,2304]{1,0:T(4,128)(2,1)S(1)}, u32[]{:S(2)}, u32[]{:S(2)}) collective-permute-start(bf16[4,2304]{1,0:T(4,128)(2,1)S(1)} %get-tuple-element.46), channel_id=1, source_target_pairs={{0,64},{64,0},{1,65},{65,1},{2,66},{66,2},{3,67},{67,3},{4,68},{68... | collective-permute-start | bytes 55304 | tf_op jit(solution)/shard_map/ppermute | solution.py:284
  3.7 4.0 %collective-permute-start.1 = (f32[4,2304]{1,0:T(4,128)S(1)}, f32[4,2304]{1,0:T(4,128)S(1)}, u32[]{:S(2)}, u32[]{:S(2)}) collective-permute-start(f32[4,2304]{1,0:T(4,128)S(1)} %get-tuple-element.49), channel_id=1, source_target_pairs={{0,64},{64,0},{1,65},{65,1},{2,66},{66,2},{3,67},{67,3},{4,68},{68... | collective-permute-start | bytes 110600 | tf_op jit(solution)/shard_map/ppermute | solution.py:284
  9.1 1.3 collective-permute-start.2
  10.4 46.4 %collective-permute-start.3 = (bf16[2,288,4608]{2,1,0:T(8,128)(2,1)}, bf16[2,288,4608]{2,1,0:T(8,128)(2,1)}, u32[]{:S(2)}, u32[]{:S(2)}) collective-permute-start(bf16[2,288,4608]{2,1,0:T(8,128)(2,1)} %refs_1_.3), channel_id=1, source_target_pairs={{0,1},{1,0},{2,3},{3,2},{4,5},{5,4},{6,7},{7,6},{8,9},{9,8},{10,11... | collective-permute-start | bytes 15925256 | tf_op jit(solution)/shard_map/ppermute | solution.py:321
  12.2 44.6 %all-to-all-start = ((bf16[64,8,2304]{2,1,0:T(8,128)(2,1)}), bf16[64,8,2304]{2,1,0:T(8,128)(2,1)S(1)}, u32[]{:S(2)}, u32[]{:S(2)}) async-start(bf16[64,8,2304]{2,1,0:T(8,128)(2,1)} %broadcast_in_dim.4), calls=%async_computation | async-start | bytes 4718592 | tf_op jit(solution)/shard_map/all_to_all | solution.py:278
  56.9 75.5 %copy-start.1 = (bf16[64,8,2304]{2,1,0:T(8,128)(2,1)}, bf16[64,8,2304]{2,1,0:T(8,128)(2,1)S(1)}, u32[]{:S(2)}) copy-start(bf16[64,8,2304]{2,1,0:T(8,128)(2,1)S(1)} %all-to-all-done) | copy-start | bytes 7077892
  132.4 62.4 %all-to-all-start.2 = ((bf16[64,32,1152]{2,1,0:T(8,128)(2,1)}), bf16[64,32,1152]{2,1,0:T(8,128)(2,1)}, u32[]{:S(2)}, u32[]{:S(2)}) async-start(bf16[64,32,1152]{2,1,0:T(8,128)(2,1)} %get-tuple-element.27), calls=%async_computation.2 | async-start | bytes 9437184 | tf_op jit(solution)/shard_map/all_to_all | solution.py:278
  146.8 2.2 collective-permute-start.4
  149.0 1.1 copy-start
  194.8 41.3 %all-to-all-start.3 = ((bf16[64,8,2304]{2,1,0:T(8,128)(2,1)}), bf16[64,8,2304]{2,1,0:T(8,128)(2,1)S(1)}, u32[]{:S(2)}, u32[]{:S(2)}) async-start(bf16[64,8,2304]{2,1,0:T(8,128)(2,1)} %down.2), calls=%async_computation.3 | async-start | bytes 4718592 | tf_op jit(solution)/shard_map/all_to_all | solution.py:278
  238.4 1.3 collective-permute-start.5
  285.7 2.1 collective-permute-start.6
  293.6 37.3 %all-to-all-start.5 = ((bf16[64,8,2304]{2,1,0:T(8,128)(2,1)}), bf16[64,8,2304]{2,1,0:T(8,128)(2,1)S(1)}, u32[]{:S(2)}, u32[]{:S(2)}) async-start(bf16[64,8,2304]{2,1,0:T(8,128)(2,1)} %down.3), calls=%async_computation.5 | async-start | bytes 4718592 | tf_op jit(solution)/shard_map/all_to_all | solution.py:278
  331.7 3.8 %collective-permute-start.7 = (bf16[4,2304]{1,0:T(4,128)(2,1)S(1)}, bf16[4,2304]{1,0:T(4,128)(2,1)S(1)}, u32[]{:S(2)}, u32[]{:S(2)}) collective-permute-start(bf16[4,2304]{1,0:T(4,128)(2,1)S(1)} %get-tuple-element.41), channel_id=1, source_target_pairs={{0,64},{64,0},{1,65},{65,1},{2,66},{66,2},{3,67},{67,3},{4,68},{68... | collective-permute-start | bytes 55304 | tf_op jit(solution)/shard_map/ppermute | solution.py:284
